TPU v7x, 128 devices: a whole 4x4x4 slice. The times are simulated.
128 devices in a mesh: sx: 16 (over x, y_lo, core), sy: 8 (over z, y_hi).
Axes of the slice: x: 4, y: 4 (y_hi: 2, y_lo: 2; y = y_hi * 2 + y_lo), z: 4, core: 2. Of those that a mesh axis runs over, the one named last changes fastest.
Arguments:
- queries: bfloat16 [8192, 128, 128], P(('sx', 'sy')), may hold values from -8 to 8
- keys: bfloat16 [8192, 8, 128], P(('sx', 'sy')), may hold values from -8 to 8
- values: bfloat16 [8192, 8, 128], P(('sx', 'sy')), may hold values from -6 to 6
Outputs:
- attention: bfloat16 [8192, 128, 128], P(('sx', 'sy'))
All inputs are finite; a program needn't handle non-finite values.
Results may differ from a plain program's by a relative error of at most 0.005.
Values may be sent and summed in bfloat16 or wider, within the bound.
No kernel may reach another device: no remote copies, remote signals or barrier semaphores. Data moves between devices by JAX's collectives and lax.ppermute only.
A program may use at most 64 MiB of HBM per device.

v0:
```python
import math

import jax
import jax.numpy as jnp
from jax import lax
from jax.experimental import pallas as pl
from jax.experimental.pallas import tpu as pltpu
from jax.sharding import Mesh, PartitionSpec as P


LOG2E = 1.4426950408889634
LOW, HIGH = 2.0**-80, 2.0**100
CHUNKS = 2
TILE = 2048
AXES = ("x", "yl", "core", "sy")


def frequencies(head_width):
    half_index = jnp.arange(head_width // 2, dtype=jnp.float32)
    base_rate = jnp.power(jnp.float32(500000.0), -2.0 * half_index / head_width)
    wavelen = 2.0 * math.pi / base_rate
    smooth = (8192.0 / wavelen - 1.0) / 3.0
    blended = (1.0 - smooth) * base_rate / 8.0 + smooth * base_rate
    return jnp.where(
        wavelen < 2048.0, base_rate, jnp.where(wavelen > 8192.0, base_rate / 8.0, blended)
    )


def rotate(heads_in, positions):
    head_width = heads_in.shape[-1]
    half_width = head_width // 2
    angles = positions.astype(jnp.float32)[:, None] * frequencies(head_width)[None, :]
    cosine = jnp.cos(angles)[:, None, :]
    sine_wave = jnp.sin(angles)[:, None, :]
    widened = heads_in.astype(jnp.float32)
    front = widened[..., :half_width]
    second = widened[..., half_width:]
    turned = jnp.concatenate(
        [front * cosine - second * sine_wave, second * cosine + front * sine_wave], axis=-1
    )
    return turned.astype(jnp.bfloat16)


def attn(q, pieces, where, out, *, bq, period, which, sub=512, unroll=2):
    G, strip, D = q.shape
    BK = pieces[0].shape[1] // 2
    blocks = G * period // BK
    c = LOG2E / math.sqrt(D)
    devs = bq // strip
    nd = devs * period // BK
    w = bq // nd
    offset = which * strip

    def kernel(where_ref, q_ref, c_ref, cc_ref, u_ref, cu_ref, v_ref, cv_ref, h_ref, ch_ref, g_ref, cg_ref,
               *rest):
        o_ref, qT_ref, acc_ref, l_ref, kv_ref, sems = rest[-6:]
        qi = pl.program_id(0)
        first = qi * nd

        @pl.when(qi == 0)
        def _():
            x, core = where_ref[0], where_ref[1]
            for step, refs in ((0, (c_ref, cc_ref)), (3, (u_ref, cu_ref)), (1, (v_ref, cv_ref)), (2, ((h_ref, g_ref), (ch_ref, cg_ref)))):
                for other in (0, 1):
                    for yl in (0, 1):
                        src = refs[other][yl].at[0] if step == 2 else refs[other].at[yl]
                        b = lax.rem(x + step, 4) * 4 + yl * 2 + lax.rem(core + other, 2)
                        pltpu.make_async_copy(src, kv_ref.at[b], sems.at[b]).start()

        for t in range(nd):
            pltpu.make_async_copy(c_ref.at[0], kv_ref.at[first + t], sems.at[first + t]).wait()

        qT_ref[...] = q_ref[...].reshape(bq, D).astype(jnp.float32).T.astype(jnp.bfloat16)

        def values(blk, lo, n):
            return jnp.concatenate(
                [kv_ref[blk, BK + lo + t * 128: BK + lo + (t + 1) * 128, :] for t in range(n // 128)], axis=1)

        def block(blk, lo, masked):
            for s in range(0, BK, sub):
                k = kv_ref[blk, s:s + sub, :]
                st = jnp.dot(k, qT_ref[:, lo:], preferred_element_type=jnp.float32)
                p = jnp.exp2(st * c)
                if masked:
                    lane = lax.broadcasted_iota(jnp.int32, (1, w), 1)
                    at = lane // strip * period + offset + lane % strip
                    row = s + lax.broadcasted_iota(jnp.int32, (sub, 1), 0)
                    head = jnp.where(row <= at, p[:, :w], 0.0)
                    p = jnp.concatenate([head, p[:, w:]], axis=1) if bq - lo > w else head
                l_ref[:, lo:] += jnp.sum(p.reshape(sub // 8, 8, bq - lo), axis=0)
                acc_ref[:, lo:] += jnp.dot(
                    values(blk, s, sub), p.astype(jnp.bfloat16), preferred_element_type=jnp.float32)

        acc_ref[...] = jnp.zeros_like(acc_ref)
        l_ref[...] = jnp.zeros_like(l_ref)

        def body(j, _):
            for u in range(unroll):
                block(j * unroll + u, 0, False)
            return 0

        lax.fori_loop(0, first // unroll, body, 0)
        for t in range(nd):
            block(first + t, t * w, True)
        total = jnp.sum(l_ref[...], axis=0, keepdims=True)
        o_ref[...] = (acc_ref[...] * (1.0 / total)).T.astype(jnp.bfloat16).reshape(o_ref.shape)
        fine = jnp.logical_and(jnp.min(total) > LOW, jnp.max(total) < HIGH)

        @pl.when(jnp.logical_not(fine))
        def _():
            lane = lax.broadcasted_iota(jnp.int32, (1, bq), 1)
            at = qi * devs * period + lane // strip * period + offset + lane % strip

            def slow(blk, state):
                l, m = state
                st = jnp.dot(kv_ref[blk, :BK, :], qT_ref[...], preferred_element_type=jnp.float32) * c
                row = blk * BK + lax.broadcasted_iota(jnp.int32, (BK, 1), 0)
                st = jnp.where(row <= at, st, -jnp.inf)
                top = jnp.maximum(m, jnp.max(st, axis=0, keepdims=True))
                shrink = jnp.exp2(m - top)
                p = jnp.exp2(st - top)
                acc_ref[...] = acc_ref[...] * shrink + jnp.dot(
                    values(blk, 0, BK), p.astype(jnp.bfloat16), preferred_element_type=jnp.float32)
                return l * shrink + jnp.sum(p, axis=0, keepdims=True), top

            acc_ref[...] = jnp.zeros_like(acc_ref)
            start = (jnp.zeros((1, bq), jnp.float32), jnp.full((1, bq), -1e30, jnp.float32))
            l, _ = lax.fori_loop(0, first + nd, slow, start)
            o_ref[...] = (acc_ref[...] / l).T.astype(jnp.bfloat16).reshape(o_ref.shape)

    extra = () if out is None else (out,)
    anywhere = pl.BlockSpec(memory_space=pl.ANY)
    return pl.pallas_call(
        kernel, grid=(G // devs,),
        in_specs=[pl.BlockSpec(memory_space=pltpu.SMEM),
                  pl.BlockSpec((devs, strip, D), lambda i: (i, 0, 0))] + [anywhere] * (len(pieces) + len(extra)),
        out_specs=pl.BlockSpec((devs, strip, D), lambda i: (i, which, 0)),
        out_shape=jax.ShapeDtypeStruct((G, period, D), jnp.bfloat16),
        input_output_aliases={2 + len(pieces): 0} if extra else {},
        scratch_shapes=[pltpu.VMEM((D, bq), jnp.bfloat16), pltpu.VMEM((D, bq), jnp.float32),
                        pltpu.VMEM((8, bq), jnp.float32), pltpu.VMEM((blocks, 2 * BK, D), jnp.bfloat16),
                        pltpu.SemaphoreType.DMA((blocks,))],
        compiler_params=pltpu.CompilerParams(vmem_limit_bytes=40 * 2**20),
        name="attn",
    )(where, q, *(pltpu.with_memory_space_constraint(piece, pltpu.HBM) for piece in pieces), *extra)


def shards(queries, keys, values):
    rows, heads_all, width = queries.shape
    key_heads = keys.shape[1]
    group = heads_all // key_heads
    x, _, core, _ = (lax.axis_index(a) for a in AXES)
    start_row = lax.axis_index(AXES) * rows
    positions = start_row + jnp.arange(rows, dtype=jnp.int32)

    key_rot = rotate(keys, positions)
    pair = jnp.stack([key_rot, values], axis=1)
    pair = jnp.concatenate([pair, pair], axis=2)
    pair = lax.all_to_all(pair, ("yl", "sy"), split_axis=2, concat_axis=0, tiled=True)[:, :, 0]
    pair = pair.reshape(2, -1, 2, width)
    block = pair.shape[1]
    own_values = pair[:, :, 1].reshape(2, block // 128, 128, width).swapaxes(2, 3).reshape(2, block, width)
    c = jnp.concatenate([pair[:, :, 0], own_values], axis=1)
    ahead = [(i, (i + 1) % 4) for i in range(4)]
    behind = [(i, (i - 1) % 4) for i in range(4)]
    swap = [(0, 1), (1, 0)]
    u = lax.ppermute(c, "x", ahead)
    v = lax.ppermute(c, "x", behind)
    h = lax.ppermute(u[0:1], "x", ahead)
    g = lax.ppermute(v[1:2], "x", behind)
    pieces = []
    for piece in (c, u, v, h, g):
        pieces += [piece, lax.ppermute(piece, "core", swap)]
    where = jnp.stack([x, core]).astype(jnp.int32)

    query_rot = rotate(queries, positions)
    ordered = (
        query_rot.reshape(rows, key_heads, group, width)
        .transpose(0, 2, 1, 3)
        .reshape(rows, heads_all, width)
    )
    strip = rows // CHUNKS
    arrived = []
    for n in range(CHUNKS):
        piece = lax.all_to_all(
            ordered[n * strip:(n + 1) * strip], AXES, split_axis=1, concat_axis=0, tiled=True)
        arrived.append(piece[:, 0].reshape(heads_all, strip, width))
    out = None
    for n in range(CHUNKS):
        out = attn(arrived[n], pieces, where, out, bq=TILE, period=rows, which=n)
    merged = lax.all_to_all(out.swapaxes(0, 1), AXES, split_axis=1, concat_axis=1, tiled=True)
    return (
        merged.reshape(rows, group, key_heads, width)
        .transpose(0, 2, 1, 3)
        .reshape(rows, heads_all, width)
    )


def solution(mesh):
    finer = Mesh(mesh.devices.reshape(4, 2, 2, 8), AXES)
    placed = P(AXES, None, None)

    return jax.shard_map(shards, mesh=finer, in_specs=(placed,) * 3, out_specs=placed, check_vma=False)
```

profile of v0, /device:TPU:1, one launch (start us, length us, event | category | flops | bytes accessed | tf_op | source)
XLA Modules:
  0.0 179.4 jit_solution(10860280480955427289)
XLA Ops:
  0.0 1.1 copy.20
  1.1 0.9 copy_convert_fusion
  2.0 0.2 multiply_cosine_fusion
  2.2 0.2 fusion
  2.4 1.0 maximum_maximum_fusion
  3.4 8.6 %all-to-all-start.1 = ((bf16[64,2,16,128]{3,0,1,2:T(8,128)(2,1)}), bf16[64,2,16,128]{3,0,1,2:T(8,128)(2,1)S(1)}, u32[]{:S(2)}, u32[]{:S(2)}) async-start(bf16[64,2,16,128]{3,0,1,2:T(8,128)(2,1)} %maximum_maximum_fusion), calls=%async_computation.1 | async-start | bytes 1048576 | tf_op jit(solution)/shard_map/all_to_all | solution.py:159
  12.0 0.0 copy-done.4
  12.0 0.5 convert_element_type.24
  12.5 1.5 subtract_convert_fusion
  14.1 1.4 copy.11
  15.4 1.4 copy.10
  16.8 1.2 maximum_bitcast_fusion
  17.9 1.9 %fusion.2 = (bf16[32,16,8,128]{3,0,2,1:T(8,128)(2,1)}, bf16[32,16,8,128]{3,0,2,1:T(8,128)(2,1)}) fusion(bf16[64,16,8,128]{3,0,2,1:T(8,128)(2,1)S(1)} %maximum_bitcast_fusion), kind=kLoop, calls=%fused_computation.18 | loop fusion | bytes 4194304 | tf_op jit(solution)/shard_map/slice | solution.py:186
  19.9 1.3 all-to-all-done.1
  21.2 8.8 %all-to-all-start.2 = ((bf16[32,128,128]{2,0,1:T(8,128)(2,1)}), bf16[32,128,128]{2,0,1:T(8,128)(2,1)S(1)}, u32[]{:S(2)}, u32[]{:S(2)}) async-start(bf16[32,128,128]{2,0,1:T(8,128)(2,1)} %bitcast.20), calls=%async_computation.2 | async-start | bytes 2097152 | tf_op jit(solution)/shard_map/all_to_all | solution.py:185
  30.1 0.2 copy.16
  30.3 0.0 copy-start.2
  30.3 1.4 collective-permute-start.1
  31.8 1.3 collective-permute-start.3
  33.1 16.7 %all-to-all-done.2 = bf16[32,128,128]{2,0,1:T(8,128)(2,1)S(1)} async-done(((bf16[32,128,128]{2,0,1:T(8,128)(2,1)}), bf16[32,128,128]{2,0,1:T(8,128)(2,1)S(1)}, u32[]{:S(2)}, u32[]{:S(2)}) %all-to-all-start.2) | async-done | bytes 1048608 | tf_op jit(solution)/shard_map/all_to_all | solution.py:185
  49.8 3.9 %all-to-all-start = ((bf16[32,128,128]{2,0,1:T(8,128)(2,1)}), bf16[32,128,128]{2,0,1:T(8,128)(2,1)S(1)}, u32[]{:S(2)}, u32[]{:S(2)}) async-start(bf16[32,128,128]{2,0,1:T(8,128)(2,1)} %bitcast.48), calls=%async_computation | async-start | bytes 2097152 | tf_op jit(solution)/shard_map/all_to_all | solution.py:185
  53.7 1.1 collective-permute-start
  54.9 0.2 collective-permute-done.1.u_ref
  55.2 0.5 collective-permute-start.5
  55.7 0.5 collective-permute-start.2
  56.2 0.0 collective-permute-done.3.v_ref
  56.2 0.1 collective-permute-start.4
  56.3 1.0 slice.56
  57.3 2.8 %collective-permute-start.7 = (bf16[1,1024,128]{2,1,0:T(8,128)(2,1)S(1)}, bf16[1,1024,128]{2,1,0:T(8,128)(2,1)S(1)}, u32[]{:S(2)}, u32[]{:S(2)}) collective-permute-start(bf16[1,1024,128]{2,1,0:T(8,128)(2,1)S(1)} %slice.56), channel_id=1, source_target_pairs={{0,96},{32,0},{64,32},{96,64},{1,97},{33,1},{65,33},{97,65},{2,98}... | collective-permute-start | bytes 786440 | tf_op jit(solution)/shard_map/ppermute | solution.py:170
  60.1 13.1 %collective-permute-done.5.h_ref = bf16[1,1024,128]{2,1,0:T(8,128)(2,1)S(1)} collective-permute-done((bf16[1,1024,128]{2,1,0:T(8,128)(2,1)S(1)}, bf16[1,1024,128]{2,1,0:T(8,128)(2,1)S(1)}, u32[]{:S(2)}, u32[]{:S(2)}) %collective-permute-start.5) | collective-permute-done | bytes 262176 | tf_op jit(solution)/shard_map/ppermute | solution.py:169
  73.3 0.9 collective-permute-start.6
  74.1 0.0 collective-permute-done.7.g_ref
  74.2 0.3 collective-permute-start.8
  74.4 0.1 pad_add_fusion.where_ref
  74.5 0.0 collective-permute-done.cc_ref
  74.5 0.0 collective-permute-done.2.cu_ref
  74.5 0.0 collective-permute-done.4.cv_ref
  74.5 0.8 collective-permute-done.6.ch_ref
  75.3 0.4 collective-permute-done.8.cg_ref
  75.7 0.0 copy-done.2
  75.8 0.3 copy-done.10
  76.0 0.4 copy-done.11
  76.4 1.2 copy-done.1
  77.6 19.6 %attn.2.rest_0_ = bf16[128,64,128]{2,1,0:T(8,128)(2,1)S(1)} custom-call(s32[2]{0:T(128)S(1)} %pad_add_fusion.where_ref, bf16[128,32,128]{2,1,0:T(8,128)(2,1)S(1)} %bitcast.44, bf16[2,1024,128]{2,1,0:T(8,128)(2,1)} %copy-done.2, bf16[2,1024,128]{2,1,0:T(8,128)(2,1)} %copy-done.5, bf16[2,1024,128]{2,1,0:T(8,128)(2,1)} %copy-done.3, ...), custom_call_target="tpu_custom_call" | custom-call | tf_op jit(solution)/shard_map/attn/pallas_call | solution.py:133
  97.2 0.0 all-to-all-done
  97.2 19.8 %attn.3 = bf16[128,64,128]{2,1,0:T(8,128)(2,1)S(1)} custom-call(s32[2]{0:T(128)S(1)} %pad_add_fusion.where_ref, bf16[128,32,128]{2,1,0:T(8,128)(2,1)S(1)} %bitcast.43, bf16[2,1024,128]{2,1,0:T(8,128)(2,1)} %copy-done.2, bf16[2,1024,128]{2,1,0:T(8,128)(2,1)} %copy-done.5, bf16[2,1024,128]{2,1,0:T(8,128)(2,1)} %copy-done.3, ...), custom_call_target="tpu_custom_call", output_to_operand_aliasing={{}: (12, {})} | custom-call | tf_op jit(solution)/shard_map/attn/pallas_call | solution.py:133
  117.1 59.7 %all_to_all.50 = bf16[64,128,128]{2,0,1:T(8,128)(2,1)S(1)} all-to-all(bf16[64,128,128]{2,0,1:T(8,128)(2,1)S(1)} %bitcast.42), channel_id=1, replica_groups=mesh['x'=4,'yl'=2,'core'=2,'sy'=8] {'x','yl','core','sy'}, dimensions={1} | all-to-all | bytes 4194304 | tf_op jit(solution)/shard_map/all_to_all | solution.py:191
  176.8 2.7 %copy.17 = bf16[64,8,16,128]{3,2,1,0:T(8,128)(2,1)} copy(bf16[64,8,16,128]{3,0,1,2:T(8,128)(2,1)S(1)} %bitcast.45) | data formatting | bytes 4194304 | tf_op jit(solution)/shard_map/transpose | solution.py:194
  (24 shorter events, 0.2 us)
Async XLA Ops:
  0.0 12.0 %copy-start.4 = (bf16[64,128,128]{2,1,0:T(8,128)(2,1)S(1)}, bf16[64,128,128]{2,1,0:T(8,128)(2,1)}, u32[]{:S(2)}) copy-start(bf16[64,128,128]{2,1,0:T(8,128)(2,1)} %param.3) | copy-start | bytes 6291460
  3.4 17.8 %all-to-all-start.1 = ((bf16[64,2,16,128]{3,0,1,2:T(8,128)(2,1)}), bf16[64,2,16,128]{3,0,1,2:T(8,128)(2,1)S(1)}, u32[]{:S(2)}, u32[]{:S(2)}) async-start(bf16[64,2,16,128]{3,0,1,2:T(8,128)(2,1)} %maximum_maximum_fusion), calls=%async_computation.1 | async-start | bytes 1048576 | tf_op jit(solution)/shard_map/all_to_all | solution.py:159
  21.2 28.6 %all-to-all-start.2 = ((bf16[32,128,128]{2,0,1:T(8,128)(2,1)}), bf16[32,128,128]{2,0,1:T(8,128)(2,1)S(1)}, u32[]{:S(2)}, u32[]{:S(2)}) async-start(bf16[32,128,128]{2,0,1:T(8,128)(2,1)} %bitcast.20), calls=%async_computation.2 | async-start | bytes 2097152 | tf_op jit(solution)/shard_map/all_to_all | solution.py:185
  30.3 45.4 %copy-start.2 = (bf16[2,1024,128]{2,1,0:T(8,128)(2,1)}, bf16[2,1024,128]{2,1,0:T(8,128)(2,1)S(1)}, u32[]{:S(2)}) copy-start(bf16[2,1024,128]{2,1,0:T(8,128)(2,1)S(1)} %pad_maximum_fusion.c_ref) | copy-start | bytes 1572868
  30.3 24.8 %collective-permute-start.1 = (bf16[2,1024,128]{2,1,0:T(8,128)(2,1)S(1)}, bf16[2,1024,128]{2,1,0:T(8,128)(2,1)S(1)}, u32[]{:S(2)}, u32[]{:S(2)}) collective-permute-start(bf16[2,1024,128]{2,1,0:T(8,128)(2,1)S(1)} %pad_maximum_fusion.c_ref), channel_id=1, source_target_pairs={{0,32},{32,64},{64,96},{96,0},{1,33},{33,65},{65,97},{97,1},{2,34}... | collective-permute-start | bytes 1572872 | tf_op jit(solution)/shard_map/ppermute | solution.py:167
  31.8 24.5 %collective-permute-start.3 = (bf16[2,1024,128]{2,1,0:T(8,128)(2,1)S(1)}, bf16[2,1024,128]{2,1,0:T(8,128)(2,1)}, u32[]{:S(2)}, u32[]{:S(2)}) collective-permute-start(bf16[2,1024,128]{2,1,0:T(8,128)(2,1)S(1)} %pad_maximum_fusion.c_ref), channel_id=1, source_target_pairs={{0,96},{32,0},{64,32},{96,64},{1,97},{33,1},{65,33},{97,65},{2,98}... | collective-permute-start | bytes 1572872 | tf_op jit(solution)/shard_map/ppermute | solution.py:168
  49.8 25.9 %copy-start = (bf16[32,128,128]{2,0,1:T(8,128)(2,1)}, bf16[32,128,128]{2,0,1:T(8,128)(2,1)S(1)}, u32[]{:S(2)}) copy-start(bf16[32,128,128]{2,0,1:T(8,128)(2,1)S(1)} %all-to-all-done.2) | copy-start | bytes 3145732
  49.8 47.4 %all-to-all-start = ((bf16[32,128,128]{2,0,1:T(8,128)(2,1)}), bf16[32,128,128]{2,0,1:T(8,128)(2,1)S(1)}, u32[]{:S(2)}, u32[]{:S(2)}) async-start(bf16[32,128,128]{2,0,1:T(8,128)(2,1)} %bitcast.48), calls=%async_computation | async-start | bytes 2097152 | tf_op jit(solution)/shard_map/all_to_all | solution.py:185
  53.7 20.8 %collective-permute-start = (bf16[2,1024,128]{2,1,0:T(8,128)(2,1)S(1)}, bf16[2,1024,128]{2,1,0:T(8,128)(2,1)S(1)}, u32[]{:S(2)}, u32[]{:S(2)}) collective-permute-start(bf16[2,1024,128]{2,1,0:T(8,128)(2,1)S(1)} %pad_maximum_fusion.c_ref), channel_id=1, source_target_pairs={{0,8},{8,0},{1,9},{9,1},{2,10},{10,2},{3,11},{11,3},{4,12},{12,4},... | collective-permute-start | bytes 1572872 | tf_op jit(solution)/shard_map/ppermute | solution.py:173
  55.1 20.6 %copy-start.3 = (bf16[2,1024,128]{2,1,0:T(8,128)(2,1)}, bf16[2,1024,128]{2,1,0:T(8,128)(2,1)S(1)}, u32[]{:S(2)}) copy-start(bf16[2,1024,128]{2,1,0:T(8,128)(2,1)S(1)} %collective-permute-done.1.u_ref) | copy-start | bytes 1572868
  55.2 18.1 %collective-permute-start.5 = (bf16[1,1024,128]{2,1,0:T(8,128)(2,1)S(1)}, bf16[1,1024,128]{2,1,0:T(8,128)(2,1)S(1)}, u32[]{:S(2)}, u32[]{:S(2)}) collective-permute-start(bf16[1,1024,128]{2,1,0:T(8,128)(2,1)S(1)} %slice.55), channel_id=1, source_target_pairs={{0,32},{32,64},{64,96},{96,0},{1,33},{33,65},{65,97},{97,1},{2,34}... | collective-permute-start | bytes 786440 | tf_op jit(solution)/shard_map/ppermute | solution.py:169
  55.7 18.8 %collective-permute-start.2 = (bf16[2,1024,128]{2,1,0:T(8,128)(2,1)S(1)}, bf16[2,1024,128]{2,1,0:T(8,128)(2,1)S(1)}, u32[]{:S(2)}, u32[]{:S(2)}) collective-permute-start(bf16[2,1024,128]{2,1,0:T(8,128)(2,1)S(1)} %collective-permute-done.1.u_ref), channel_id=1, source_target_pairs={{0,8},{8,0},{1,9},{9,1},{2,10},{10,2},{3,11},{11,3},{4,12},{12,4},... | collective-permute-start | bytes 1572872 | tf_op jit(solution)/shard_map/ppermute | solution.py:173
  56.2 18.3 %collective-permute-start.4 = (bf16[2,1024,128]{2,1,0:T(8,128)(2,1)}, bf16[2,1024,128]{2,1,0:T(8,128)(2,1)S(1)}, u32[]{:S(2)}, u32[]{:S(2)}) collective-permute-start(bf16[2,1024,128]{2,1,0:T(8,128)(2,1)} %collective-permute-done.3.v_ref), channel_id=1, source_target_pairs={{0,8},{8,0},{1,9},{9,1},{2,10},{10,2},{3,11},{11,3},{4,12},{12,4},... | collective-permute-start | bytes 1572872 | tf_op jit(solution)/shard_map/ppermute | solution.py:173
  57.3 16.9 %collective-permute-start.7 = (bf16[1,1024,128]{2,1,0:T(8,128)(2,1)S(1)}, bf16[1,1024,128]{2,1,0:T(8,128)(2,1)S(1)}, u32[]{:S(2)}, u32[]{:S(2)}) collective-permute-start(bf16[1,1024,128]{2,1,0:T(8,128)(2,1)S(1)} %slice.56), channel_id=1, source_target_pairs={{0,96},{32,0},{64,32},{96,64},{1,97},{33,1},{65,33},{97,65},{2,98}... | collective-permute-start | bytes 786440 | tf_op jit(solution)/shard_map/ppermute | solution.py:170
  73.3 2.4 %copy-start.8 = (bf16[1,1024,128]{2,1,0:T(8,128)(2,1)}, bf16[1,1024,128]{2,1,0:T(8,128)(2,1)S(1)}, u32[]{:S(2)}) copy-start(bf16[1,1024,128]{2,1,0:T(8,128)(2,1)S(1)} %collective-permute-done.5.h_ref) | copy-start | bytes 786436
  73.3 2.0 %collective-permute-start.6 = (bf16[1,1024,128]{2,1,0:T(8,128)(2,1)S(1)}, bf16[1,1024,128]{2,1,0:T(8,128)(2,1)S(1)}, u32[]{:S(2)}, u32[]{:S(2)}) collective-permute-start(bf16[1,1024,128]{2,1,0:T(8,128)(2,1)S(1)} %collective-permute-done.5.h_ref), channel_id=1, source_target_pairs={{0,8},{8,0},{1,9},{9,1},{2,10},{10,2},{3,11},{11,3},{4,12},{12,4},... | collective-permute-start | bytes 786440 | tf_op jit(solution)/shard_map/ppermute | solution.py:173
  74.1 1.6 copy-start.9
  74.2 1.5 collective-permute-start.8
  74.5 1.2 copy-start.5
  74.5 1.2 copy-start.6
  74.5 1.2 copy-start.7
  75.3 0.7 copy-start.10
  75.7 0.7 copy-start.11
  76.4 1.2 copy-start.1
where the time goes:
time: 180 us; the launch traced here: 179 us
  blocking collectives  59.7 us (33%)
  Pallas kernels  39.4 us (22%)
  waiting for transfers between devices  32.6 us (18%)
  starting transfers between devices  30.3 us (17%)
  local copies, waits for them, and re-layouts  11.5 us (6%)
  other arithmetic  5.6 us (3%)
    all_to_all x1, blocking collectives, shards(): lax.all_to_all(out.swapaxes(0, 1), AXES, split_axis=1, concat_axis=1, til...  59.7 us
    pallas_call x2, Pallas kernels, attn(): pl.pallas_call(kernel, grid=(G // devs,), in_specs=[pl.BlockSpec(memory_s...  39.4 us
    all_to_all x2, waiting for transfers between devices, shards(): lax.all_to_all(ordered[n * strip:(n + 1) * strip], AXES, split_axis=1, co...  16.7 us
    ppermute x1, waiting for transfers between devices, shards(): h = lax.ppermute(u[0:1], 'x', ahead)  13.1 us
    all_to_all x2, starting transfers between devices, shards(): lax.all_to_all(ordered[n * strip:(n + 1) * strip], AXES, split_axis=1, co...  12.7 us
    all_to_all x1, starting transfers between devices, shards(): lax.all_to_all(pair, ('yl', 'sy'), split_axis=2, concat_axis=0, tiled=True)  8.59 us
  transfers between devices with their start and end apart: 12, of which 6 were waited for; matrix products, arithmetic and copies ran while one was open for 5% of the time, Pallas kernels for 11%

commit v1 on v0

--- a/solution.py
+++ b/solution.py
@@ -12,6 +12,7 @@
 LOW, HIGH = 2.0**-80, 2.0**100
 CHUNKS = 2
 TILE = 2048
+GROUPS = {8: {0: (0, 1), 1: tuple(range(2, 8))}}
 AXES = ("x", "yl", "core", "sy")
 
 
@@ -26,22 +27,54 @@
     )
 
 
-def rotate(heads_in, positions):
-    head_width = heads_in.shape[-1]
-    half_width = head_width // 2
-    angles = positions.astype(jnp.float32)[:, None] * frequencies(head_width)[None, :]
-    cosine = jnp.cos(angles)[:, None, :]
-    sine_wave = jnp.sin(angles)[:, None, :]
-    widened = heads_in.astype(jnp.float32)
-    front = widened[..., :half_width]
-    second = widened[..., half_width:]
-    turned = jnp.concatenate(
-        [front * cosine - second * sine_wave, second * cosine + front * sine_wave], axis=-1
-    )
-    return turned.astype(jnp.bfloat16)
-
-
-def attn(q, pieces, where, out, *, bq, period, which, sub=512, unroll=2):
+def turned(head, cosine, signed_sine):
+    return head * cosine + pltpu.roll(head, head.shape[-1] // 2, 1) * signed_sine
+
+
+def prepare_pair(keys, values, cosine, signed_sine):
+    rows, heads, width = keys.shape
+
+    def kernel(k_ref, v_ref, cos_ref, sin_ref, o_ref, kf_ref, vf_ref):
+        kf_ref[...] = k_ref[...].astype(jnp.float32)
+        vf_ref[...] = v_ref[...].astype(jnp.float32)
+        for h in range(heads):
+            key = turned(kf_ref[:, h, :], cos_ref[...], sin_ref[...]).astype(jnp.bfloat16)
+            value = vf_ref[:, h, :].astype(jnp.bfloat16)
+            for half in (0, heads):
+                o_ref[half + h, 0] = key
+                o_ref[half + h, 1] = value
+
+    wide = pltpu.VMEM((rows, heads, width), jnp.float32)
+    return pl.pallas_call(
+        kernel, out_shape=jax.ShapeDtypeStruct((2 * heads, 2, rows, width), jnp.bfloat16),
+        scratch_shapes=[wide, wide], name="pair",
+    )(keys, values, cosine, signed_sine)
+
+
+def prepare_queries(queries, cosine, signed_sine, group):
+    rows, heads, width = queries.shape
+    strip = rows // CHUNKS
+
+    def kernel(q_ref, cos_ref, sin_ref, *rest):
+        outs, wide_ref = rest[:-1], rest[-1]
+        wide_ref[...] = q_ref[...].astype(jnp.float32)
+        for h in range(group):
+            head = turned(wide_ref[:, h, :], cos_ref[...], sin_ref[...]).astype(jnp.bfloat16)
+            for n, o_ref in enumerate(outs):
+                o_ref[h, 0] = head[n * strip:(n + 1) * strip]
+
+    table = pl.BlockSpec((rows, width), lambda g: (0, 0))
+    parts = pl.pallas_call(
+        kernel, grid=(heads // group,),
+        in_specs=[pl.BlockSpec((rows, group, width), lambda g: (0, g, 0)), table, table],
+        out_specs=[pl.BlockSpec((group, 1, strip, width), lambda g: (0, g, 0, 0))] * CHUNKS,
+        out_shape=[jax.ShapeDtypeStruct((group, heads // group, strip, width), jnp.bfloat16)] * CHUNKS,
+        scratch_shapes=[pltpu.VMEM((rows, group, width), jnp.float32)], name="queries",
+    )(queries, cosine, signed_sine)
+    return [part.reshape(heads, strip, width) for part in parts]
+
+
+def attn(q, pieces, where, out, *, bq, period, which, sub=512, unroll=4):
     G, strip, D = q.shape
     BK = pieces[0].shape[1] // 2
     blocks = G * period // BK
@@ -50,15 +83,17 @@
     nd = devs * period // BK
     w = bq // nd
     offset = which * strip
+    groups = GROUPS[nd]
 
     def kernel(where_ref, q_ref, c_ref, cc_ref, u_ref, cu_ref, v_ref, cv_ref, h_ref, ch_ref, g_ref, cg_ref,
                *rest):
-        o_ref, qT_ref, acc_ref, l_ref, kv_ref, sems = rest[-6:]
+        o_ref, qT_ref, acc_ref, l_ref, kv_ref, qv_ref, sems = rest[-7:]
         qi = pl.program_id(0)
         first = qi * nd
 
         @pl.when(qi == 0)
         def _():
+            pltpu.make_async_copy(q_ref, qv_ref, sems.at[blocks]).start()
             x, core = where_ref[0], where_ref[1]
             for step, refs in ((0, (c_ref, cc_ref)), (3, (u_ref, cu_ref)), (1, (v_ref, cv_ref)), (2, ((h_ref, g_ref), (ch_ref, cg_ref)))):
                 for other in (0, 1):
@@ -67,10 +102,14 @@
                         b = lax.rem(x + step, 4) * 4 + yl * 2 + lax.rem(core + other, 2)
                         pltpu.make_async_copy(src, kv_ref.at[b], sems.at[b]).start()
 
-        for t in range(nd):
+        @pl.when(qi == 0)
+        def _():
+            pltpu.make_async_copy(q_ref, qv_ref, sems.at[blocks]).wait()
+
+        def landed(t):
             pltpu.make_async_copy(c_ref.at[0], kv_ref.at[first + t], sems.at[first + t]).wait()
 
-        qT_ref[...] = q_ref[...].reshape(bq, D).astype(jnp.float32).T.astype(jnp.bfloat16)
+        qT_ref[...] = qv_ref[pl.ds(qi * devs, devs)].reshape(bq, D).astype(jnp.float32).T.astype(jnp.bfloat16)
 
         def values(blk, lo, n):
             return jnp.concatenate(
@@ -101,6 +140,8 @@
 
         lax.fori_loop(0, first // unroll, body, 0)
         for t in range(nd):
+            for later in groups.get(t, ()):
+                landed(later)
             block(first + t, t * w, True)
         total = jnp.sum(l_ref[...], axis=0, keepdims=True)
         o_ref[...] = (acc_ref[...] * (1.0 / total)).T.astype(jnp.bfloat16).reshape(o_ref.shape)
@@ -133,16 +174,17 @@
     return pl.pallas_call(
         kernel, grid=(G // devs,),
         in_specs=[pl.BlockSpec(memory_space=pltpu.SMEM),
-                  pl.BlockSpec((devs, strip, D), lambda i: (i, 0, 0))] + [anywhere] * (len(pieces) + len(extra)),
+                  anywhere] + [anywhere] * (len(pieces) + len(extra)),
         out_specs=pl.BlockSpec((devs, strip, D), lambda i: (i, which, 0)),
         out_shape=jax.ShapeDtypeStruct((G, period, D), jnp.bfloat16),
         input_output_aliases={2 + len(pieces): 0} if extra else {},
         scratch_shapes=[pltpu.VMEM((D, bq), jnp.bfloat16), pltpu.VMEM((D, bq), jnp.float32),
                         pltpu.VMEM((8, bq), jnp.float32), pltpu.VMEM((blocks, 2 * BK, D), jnp.bfloat16),
-                        pltpu.SemaphoreType.DMA((blocks,))],
-        compiler_params=pltpu.CompilerParams(vmem_limit_bytes=40 * 2**20),
+                        pltpu.VMEM((G, strip, D), jnp.bfloat16),
+                        pltpu.SemaphoreType.DMA((blocks + 1,))],
+        compiler_params=pltpu.CompilerParams(vmem_limit_bytes=24 * 2**20),
         name="attn",
-    )(where, q, *(pltpu.with_memory_space_constraint(piece, pltpu.HBM) for piece in pieces), *extra)
+    )(where, *(pltpu.with_memory_space_constraint(piece, pltpu.HBM) for piece in (q, *pieces)), *extra)
 
 
 def shards(queries, keys, values):
@@ -153,14 +195,16 @@
     start_row = lax.axis_index(AXES) * rows
     positions = start_row + jnp.arange(rows, dtype=jnp.int32)
 
-    key_rot = rotate(keys, positions)
-    pair = jnp.stack([key_rot, values], axis=1)
-    pair = jnp.concatenate([pair, pair], axis=2)
-    pair = lax.all_to_all(pair, ("yl", "sy"), split_axis=2, concat_axis=0, tiled=True)[:, :, 0]
-    pair = pair.reshape(2, -1, 2, width)
-    block = pair.shape[1]
-    own_values = pair[:, :, 1].reshape(2, block // 128, 128, width).swapaxes(2, 3).reshape(2, block, width)
-    c = jnp.concatenate([pair[:, :, 0], own_values], axis=1)
+    angles = positions.astype(jnp.float32)[:, None] * jnp.tile(frequencies(width), 2)[None, :]
+    cosine = jnp.cos(angles)
+    signed_sine = jnp.sin(angles) * jnp.where(jnp.arange(width) < width // 2, -1.0, 1.0)
+
+    pair = prepare_pair(keys, values, cosine, signed_sine)
+    pair = lax.all_to_all(pair, ("yl", "sy"), split_axis=0, concat_axis=0, tiled=True)
+    pair = pair.swapaxes(0, 1).reshape(2, 2, -1, width)
+    block = pair.shape[2]
+    own_values = pair[1].reshape(2, block // 128, 128, width).swapaxes(2, 3).reshape(2, block, width)
+    c = jnp.concatenate([pair[0], own_values], axis=1)
     ahead = [(i, (i + 1) % 4) for i in range(4)]
     behind = [(i, (i - 1) % 4) for i in range(4)]
     swap = [(0, 1), (1, 0)]
@@ -173,18 +217,10 @@
         pieces += [piece, lax.ppermute(piece, "core", swap)]
     where = jnp.stack([x, core]).astype(jnp.int32)
 
-    query_rot = rotate(queries, positions)
-    ordered = (
-        query_rot.reshape(rows, key_heads, group, width)
-        .transpose(0, 2, 1, 3)
-        .reshape(rows, heads_all, width)
-    )
-    strip = rows // CHUNKS
+    ordered = prepare_queries(queries, cosine, signed_sine, group)
     arrived = []
     for n in range(CHUNKS):
-        piece = lax.all_to_all(
-            ordered[n * strip:(n + 1) * strip], AXES, split_axis=1, concat_axis=0, tiled=True)
-        arrived.append(piece[:, 0].reshape(heads_all, strip, width))
+        arrived.append(lax.all_to_all(ordered[n], AXES, split_axis=0, concat_axis=0, tiled=True))
     out = None
     for n in range(CHUNKS):
         out = attn(arrived[n], pieces, where, out, bq=TILE, period=rows, which=n)

time: 180 us -> 179 us (level)
  Pallas kernels: 39.4 us -> 46.8 us
  local copies, waits for them, and re-layouts: 11.5 us -> 4.47 us
  other arithmetic: 5.6 us -> 0.97 us
  blocking collectives: 59.7 us -> 62.2 us
  waiting for transfers between devices: 32.6 us -> 34.5 us
    ppermute x1, waiting for transfers between devices: 0.01 us -> 14 us  [shards(): g = lax.ppermute(v[1:2], 'x', behind)]
    ppermute x1, waiting for transfers between devices: 13.1 us -> 0.49 us  [shards(): h = lax.ppermute(u[0:1], 'x', ahead)]
    pallas_call x0 -> x2, Pallas kernels: none -> 9.45 us  [the longest x1 7.19 us: prepare_queries(): pl.pallas_call(kernel, grid=(heads // group,), in_specs=[pl.BlockSpec((ro...]
    concatenate x2 -> x0, local copies, waits for them, and re-layouts: 2.71 us -> none  [rotate(): jnp.concatenate([front * cosine - second * sine_wave, second * cosine + f...]
    all_to_all x1, blocking collectives: 59.7 us -> 62.2 us  [shards(): lax.all_to_all(out.swapaxes(0, 1), AXES, split_axis=1, concat_axis=1, til...]
    pallas_call x2, Pallas kernels: 39.4 us -> 37.3 us  [attn(): pl.pallas_call(kernel, grid=(G // devs,), in_specs=[pl.BlockSpec(memory_s...]
    slice x1, local copies, waits for them, and re-layouts: 1.94 us -> 0.04 us  [shards(): c = jnp.concatenate([pair[0], own_values], axis=1)]
  transfers between devices with their start and end apart: 12 -> 12, of which waited for: 6 -> 5; matrix products, arithmetic and copies ran while one was open for 5% -> 0% of each run, Pallas kernels for 11% -> 14%
where the time goes in v1:
time: 179 us
  blocking collectives  62.2 us (35%)
  Pallas kernels  46.8 us (26%)
  waiting for transfers between devices  34.5 us (19%)
  starting transfers between devices  29.5 us (16%)
  local copies, waits for them, and re-layouts  4.47 us (2%)
    all_to_all x1, blocking collectives, shards(): lax.all_to_all(out.swapaxes(0, 1), AXES, split_axis=1, concat_axis=1, til...  62.2 us
    pallas_call x2, Pallas kernels, attn(): pl.pallas_call(kernel, grid=(G // devs,), in_specs=[pl.BlockSpec(memory_s...  37.3 us
    all_to_all x2, waiting for transfers between devices, shards(): lax.all_to_all(ordered[n], AXES, split_axis=0, concat_axis=0, tiled=True)  16.9 us
    ppermute x1, waiting for transfers between devices, shards(): g = lax.ppermute(v[1:2], 'x', behind)  14 us
    all_to_all x2, starting transfers between devices, shards(): lax.all_to_all(ordered[n], AXES, split_axis=0, concat_axis=0, tiled=True)  12.9 us
    all_to_all x1, starting transfers between devices, shards(): lax.all_to_all(pair, ('yl', 'sy'), split_axis=0, concat_axis=0, tiled=True)  8.59 us
    pallas_call x1, Pallas kernels, prepare_queries(): pl.pallas_call(kernel, grid=(heads // group,), in_specs=[pl.BlockSpec((ro...  7.19 us
  transfers between devices with their start and end apart: 12, of which 5 were waited for; matrix products, arithmetic and copies ran while one was open for 0% of the time, Pallas kernels for 14%

profile of v1, /device:TPU:1, one launch (start us, length us, event | category | flops | bytes accessed | tf_op | source)
XLA Modules:
  0.0 178.5 jit_solution(17155206041548172002)
XLA Ops:
  0.1 0.1 mul.58
  0.1 0.8 fusion
  1.0 2.3 %pair.1 = bf16[16,2,64,128]{3,2,1,0:T(8,128)(2,1)} custom-call(bf16[64,8,128]{2,1,0:T(8,128)(2,1)} %k_ref.1, bf16[64,8,128]{2,1,0:T(8,128)(2,1)} %v_ref.1, f32[64,128]{1,0:T(8,128)} %get-tuple-element.12.cos_ref, f32[64,128]{1,0:T(8,128)} %get-tuple-element.11.sin_ref), custom_call_target="tpu_custom_call" | custom-call | tf_op jit(solution)/shard_map/pair/pallas_call | solution.py:48
  3.2 8.6 %all-to-all-start.1 = ((bf16[16,2,64,128]{3,2,1,0:T(8,128)(2,1)}), bf16[16,2,64,128]{3,2,1,0:T(8,128)(2,1)S(1)}, u32[]{:S(2)}, u32[]{:S(2)}) async-start(bf16[16,2,64,128]{3,2,1,0:T(8,128)(2,1)} %pair.1), calls=%async_computation.1 | async-start | bytes 1048576 | tf_op jit(solution)/shard_map/all_to_all | solution.py:203
  11.8 7.2 %queries.1 = (bf16[16,8,32,128]{3,2,1,0:T(8,128)(2,1)}, bf16[16,8,32,128]{3,2,1,0:T(8,128)(2,1)}) custom-call(bf16[64,128,128]{2,1,0:T(8,128)(2,1)} %q_ref.1, f32[64,128]{1,0:T(8,128)} %get-tuple-element.12.cos_ref, f32[64,128]{1,0:T(8,128)} %get-tuple-element.11.sin_ref), custom_call_target="tpu_custom_call" | custom-call | tf_op jit(solution)/shard_map/queries/pallas_call | solution.py:67
  19.0 2.0 %all-to-all-done.1 = bf16[16,2,64,128]{3,2,1,0:T(8,128)(2,1)S(1)} async-done(((bf16[16,2,64,128]{3,2,1,0:T(8,128)(2,1)}), bf16[16,2,64,128]{3,2,1,0:T(8,128)(2,1)S(1)}, u32[]{:S(2)}, u32[]{:S(2)}) %all-to-all-start.1) | async-done | bytes 524320 | tf_op jit(solution)/shard_map/all_to_all | solution.py:203
  21.1 8.3 %all-to-all-start.2 = ((bf16[128,32,128]{2,1,0:T(8,128)(2,1)}), bf16[128,32,128]{2,1,0:T(8,128)(2,1)S(1)}, u32[]{:S(2)}, u32[]{:S(2)}) async-start(bf16[128,32,128]{2,1,0:T(8,128)(2,1)} %bitcast.19), calls=%async_computation.2 | async-start | bytes 2097152 | tf_op jit(solution)/shard_map/all_to_all | solution.py:223
  29.4 0.2 copy.5
  29.6 0.0 copy-start
  29.6 2.6 %collective-permute-start.3 = (bf16[2,1024,128]{2,1,0:T(8,128)(2,1)S(1)}, bf16[2,1024,128]{2,1,0:T(8,128)(2,1)S(1)}, u32[]{:S(2)}, u32[]{:S(2)}) collective-permute-start(bf16[2,1024,128]{2,1,0:T(8,128)(2,1)S(1)} %pad_maximum_fusion.c_ref), channel_id=1, source_target_pairs={{0,96},{32,0},{64,32},{96,64},{1,97},{33,1},{65,33},{97,65},{2,98}... | collective-permute-start | bytes 1572872 | tf_op jit(solution)/shard_map/ppermute | solution.py:212
  32.2 0.0 collective-permute-start.1
  32.2 16.9 %all-to-all-done.2.q_ref = bf16[128,32,128]{2,1,0:T(8,128)(2,1)S(1)} async-done(((bf16[128,32,128]{2,1,0:T(8,128)(2,1)}), bf16[128,32,128]{2,1,0:T(8,128)(2,1)S(1)}, u32[]{:S(2)}, u32[]{:S(2)}) %all-to-all-start.2) | async-done | bytes 1048608 | tf_op jit(solution)/shard_map/all_to_all | solution.py:223
  49.1 4.7 %all-to-all-start = ((bf16[128,32,128]{2,1,0:T(8,128)(2,1)}), bf16[128,32,128]{2,1,0:T(8,128)(2,1)}, u32[]{:S(2)}, u32[]{:S(2)}) async-start(bf16[128,32,128]{2,1,0:T(8,128)(2,1)} %bitcast.18), calls=%async_computation | async-start | bytes 2097152 | tf_op jit(solution)/shard_map/all_to_all | solution.py:223
  53.8 1.2 collective-permute-start
  55.0 0.0 collective-permute-done.3.v_ref
  55.1 1.8 %collective-permute-start.7 = (bf16[1,1024,128]{2,1,0:T(8,128)(2,1)S(1)}, bf16[1,1024,128]{2,1,0:T(8,128)(2,1)S(1)}, u32[]{:S(2)}, u32[]{:S(2)}) collective-permute-start(bf16[1,1024,128]{2,1,0:T(8,128)(2,1)S(1)} %slice.21), channel_id=1, source_target_pairs={{0,96},{32,0},{64,32},{96,64},{1,97},{33,1},{65,33},{97,65},{2,98}... | collective-permute-start | bytes 786440 | tf_op jit(solution)/shard_map/ppermute | solution.py:214
  56.9 0.4 collective-permute-start.4
  57.3 0.0 collective-permute-done.1.u_ref
  57.3 0.1 collective-permute-start.5
  57.4 0.2 collective-permute-start.2
  57.6 14.0 %collective-permute-done.7.g_ref = bf16[1,1024,128]{2,1,0:T(8,128)(2,1)S(1)} collective-permute-done((bf16[1,1024,128]{2,1,0:T(8,128)(2,1)S(1)}, bf16[1,1024,128]{2,1,0:T(8,128)(2,1)S(1)}, u32[]{:S(2)}, u32[]{:S(2)}) %collective-permute-start.7) | collective-permute-done | bytes 262176 | tf_op jit(solution)/shard_map/ppermute | solution.py:214
  71.6 0.9 collective-permute-start.8
  72.4 0.5 collective-permute-done.5.h_ref
  72.9 0.8 collective-permute-start.6
  73.7 0.1 pad_add_fusion.where_ref
  73.7 0.0 collective-permute-done.cc_ref
  73.7 0.0 collective-permute-done.8.cg_ref
  73.8 0.0 copy-start.9
  73.8 0.0 collective-permute-done.4.cv_ref
  73.8 0.0 copy-start.5
  73.8 1.0 collective-permute-done.6.ch_ref
  74.8 0.0 copy-done.1
  74.8 0.0 copy-done.3
  74.8 0.0 collective-permute-done.2.cu_ref
  74.8 0.0 copy-done
  74.9 0.0 copy-done.2
  74.9 0.0 copy-done.7
  74.9 0.0 copy-done.8
  74.9 0.0 copy-done.4
  74.9 0.0 copy-done.9
  74.9 0.0 copy-done.5
  74.9 0.6 copy-done.10
  75.5 0.8 copy-done.6
  76.3 18.5 %attn.2.rest_0_ = bf16[128,64,128]{2,1,0:T(8,128)(2,1)S(1)} custom-call(s32[2]{0:T(128)S(1)} %pad_add_fusion.where_ref, bf16[128,32,128]{2,1,0:T(8,128)(2,1)} %copy-done.1, bf16[2,1024,128]{2,1,0:T(8,128)(2,1)} %copy-done, bf16[2,1024,128]{2,1,0:T(8,128)(2,1)} %copy-done.4, bf16[2,1024,128]{2,1,0:T(8,128)(2,1)} %copy-done.3, ...), custom_call_target="tpu_custom_call" | custom-call | tf_op jit(solution)/shard_map/attn/pallas_call | solution.py:174
  94.9 0.0 all-to-all-done.q_ref
  94.9 18.8 %attn.3 = bf16[128,64,128]{2,1,0:T(8,128)(2,1)S(1)} custom-call(s32[2]{0:T(128)S(1)} %pad_add_fusion.where_ref, bf16[128,32,128]{2,1,0:T(8,128)(2,1)} %all-to-all-done.q_ref, bf16[2,1024,128]{2,1,0:T(8,128)(2,1)} %copy-done, bf16[2,1024,128]{2,1,0:T(8,128)(2,1)} %copy-done.4, bf16[2,1024,128]{2,1,0:T(8,128)(2,1)} %copy-done.3, ...), custom_call_target="tpu_custom_call", output_to_operand_aliasing={{}: (12, {})} | custom-call | tf_op jit(solution)/shard_map/attn/pallas_call | solution.py:174
  113.7 62.2 %all_to_all.20 = bf16[64,128,128]{2,0,1:T(8,128)(2,1)S(1)} all-to-all(bf16[64,128,128]{2,0,1:T(8,128)(2,1)S(1)} %bitcast.15), channel_id=1, replica_groups=mesh['x'=4,'yl'=2,'core'=2,'sy'=8] {'x','yl','core','sy'}, dimensions={1} | all-to-all | bytes 4194304 | tf_op jit(solution)/shard_map/all_to_all | solution.py:227
  175.9 2.7 %copy.6 = bf16[64,8,16,128]{3,2,1,0:T(8,128)(2,1)} copy(bf16[64,8,16,128]{3,0,1,2:T(8,128)(2,1)S(1)} %bitcast.16) | data formatting | bytes 4194304 | tf_op jit(solution)/shard_map/transpose | solution.py:230
  (16 shorter events, 0.2 us)
Async XLA Ops:
  3.2 17.8 %all-to-all-start.1 = ((bf16[16,2,64,128]{3,2,1,0:T(8,128)(2,1)}), bf16[16,2,64,128]{3,2,1,0:T(8,128)(2,1)S(1)}, u32[]{:S(2)}, u32[]{:S(2)}) async-start(bf16[16,2,64,128]{3,2,1,0:T(8,128)(2,1)} %pair.1), calls=%async_computation.1 | async-start | bytes 1048576 | tf_op jit(solution)/shard_map/all_to_all | solution.py:203
  21.1 28.1 %all-to-all-start.2 = ((bf16[128,32,128]{2,1,0:T(8,128)(2,1)}), bf16[128,32,128]{2,1,0:T(8,128)(2,1)S(1)}, u32[]{:S(2)}, u32[]{:S(2)}) async-start(bf16[128,32,128]{2,1,0:T(8,128)(2,1)} %bitcast.19), calls=%async_computation.2 | async-start | bytes 2097152 | tf_op jit(solution)/shard_map/all_to_all | solution.py:223
  29.6 45.3 %copy-start = (bf16[2,1024,128]{2,1,0:T(8,128)(2,1)}, bf16[2,1024,128]{2,1,0:T(8,128)(2,1)S(1)}, u32[]{:S(2)}) copy-start(bf16[2,1024,128]{2,1,0:T(8,128)(2,1)S(1)} %pad_maximum_fusion.c_ref) | copy-start | bytes 1572868
  29.6 25.4 %collective-permute-start.3 = (bf16[2,1024,128]{2,1,0:T(8,128)(2,1)S(1)}, bf16[2,1024,128]{2,1,0:T(8,128)(2,1)S(1)}, u32[]{:S(2)}, u32[]{:S(2)}) collective-permute-start(bf16[2,1024,128]{2,1,0:T(8,128)(2,1)S(1)} %pad_maximum_fusion.c_ref), channel_id=1, source_target_pairs={{0,96},{32,0},{64,32},{96,64},{1,97},{33,1},{65,33},{97,65},{2,98}... | collective-permute-start | bytes 1572872 | tf_op jit(solution)/shard_map/ppermute | solution.py:212
  32.2 25.0 %collective-permute-start.1 = (bf16[2,1024,128]{2,1,0:T(8,128)(2,1)S(1)}, bf16[2,1024,128]{2,1,0:T(8,128)(2,1)S(1)}, u32[]{:S(2)}, u32[]{:S(2)}) collective-permute-start(bf16[2,1024,128]{2,1,0:T(8,128)(2,1)S(1)} %pad_maximum_fusion.c_ref), channel_id=1, source_target_pairs={{0,32},{32,64},{64,96},{96,0},{1,33},{33,65},{65,97},{97,1},{2,34}... | collective-permute-start | bytes 1572872 | tf_op jit(solution)/shard_map/ppermute | solution.py:211
  49.1 25.7 %copy-start.1 = (bf16[128,32,128]{2,1,0:T(8,128)(2,1)}, bf16[128,32,128]{2,1,0:T(8,128)(2,1)S(1)}, u32[]{:S(2)}) copy-start(bf16[128,32,128]{2,1,0:T(8,128)(2,1)S(1)} %all-to-all-done.2.q_ref) | copy-start | bytes 3145732
  49.1 45.8 %all-to-all-start = ((bf16[128,32,128]{2,1,0:T(8,128)(2,1)}), bf16[128,32,128]{2,1,0:T(8,128)(2,1)}, u32[]{:S(2)}, u32[]{:S(2)}) async-start(bf16[128,32,128]{2,1,0:T(8,128)(2,1)} %bitcast.18), calls=%async_computation | async-start | bytes 2097152 | tf_op jit(solution)/shard_map/all_to_all | solution.py:223
  53.8 19.9 %collective-permute-start = (bf16[2,1024,128]{2,1,0:T(8,128)(2,1)S(1)}, bf16[2,1024,128]{2,1,0:T(8,128)(2,1)S(1)}, u32[]{:S(2)}, u32[]{:S(2)}) collective-permute-start(bf16[2,1024,128]{2,1,0:T(8,128)(2,1)S(1)} %pad_maximum_fusion.c_ref), channel_id=1, source_target_pairs={{0,8},{8,0},{1,9},{9,1},{2,10},{10,2},{3,11},{11,3},{4,12},{12,4},... | collective-permute-start | bytes 1572872 | tf_op jit(solution)/shard_map/ppermute | solution.py:217
  55.0 19.8 %copy-start.2 = (bf16[2,1024,128]{2,1,0:T(8,128)(2,1)}, bf16[2,1024,128]{2,1,0:T(8,128)(2,1)S(1)}, u32[]{:S(2)}) copy-start(bf16[2,1024,128]{2,1,0:T(8,128)(2,1)S(1)} %collective-permute-done.3.v_ref) | copy-start | bytes 1572868
  55.1 16.5 %collective-permute-start.7 = (bf16[1,1024,128]{2,1,0:T(8,128)(2,1)S(1)}, bf16[1,1024,128]{2,1,0:T(8,128)(2,1)S(1)}, u32[]{:S(2)}, u32[]{:S(2)}) collective-permute-start(bf16[1,1024,128]{2,1,0:T(8,128)(2,1)S(1)} %slice.21), channel_id=1, source_target_pairs={{0,96},{32,0},{64,32},{96,64},{1,97},{33,1},{65,33},{97,65},{2,98}... | collective-permute-start | bytes 786440 | tf_op jit(solution)/shard_map/ppermute | solution.py:214
  56.9 16.9 %collective-permute-start.4 = (bf16[2,1024,128]{2,1,0:T(8,128)(2,1)S(1)}, bf16[2,1024,128]{2,1,0:T(8,128)(2,1)S(1)}, u32[]{:S(2)}, u32[]{:S(2)}) collective-permute-start(bf16[2,1024,128]{2,1,0:T(8,128)(2,1)S(1)} %collective-permute-done.3.v_ref), channel_id=1, source_target_pairs={{0,8},{8,0},{1,9},{9,1},{2,10},{10,2},{3,11},{11,3},{4,12},{12,4},... | collective-permute-start | bytes 1572872 | tf_op jit(solution)/shard_map/ppermute | solution.py:217
  57.3 17.6 %copy-start.3 = (bf16[2,1024,128]{2,1,0:T(8,128)(2,1)}, bf16[2,1024,128]{2,1,0:T(8,128)(2,1)S(1)}, u32[]{:S(2)}) copy-start(bf16[2,1024,128]{2,1,0:T(8,128)(2,1)S(1)} %collective-permute-done.1.u_ref) | copy-start | bytes 1572868
  57.3 15.6 %collective-permute-start.5 = (bf16[1,1024,128]{2,1,0:T(8,128)(2,1)S(1)}, bf16[1,1024,128]{2,1,0:T(8,128)(2,1)S(1)}, u32[]{:S(2)}, u32[]{:S(2)}) collective-permute-start(bf16[1,1024,128]{2,1,0:T(8,128)(2,1)S(1)} %slice.20), channel_id=1, source_target_pairs={{0,32},{32,64},{64,96},{96,0},{1,33},{33,65},{65,97},{97,1},{2,34}... | collective-permute-start | bytes 786440 | tf_op jit(solution)/shard_map/ppermute | solution.py:213
  57.4 17.5 %collective-permute-start.2 = (bf16[2,1024,128]{2,1,0:T(8,128)(2,1)S(1)}, bf16[2,1024,128]{2,1,0:T(8,128)(2,1)S(1)}, u32[]{:S(2)}, u32[]{:S(2)}) collective-permute-start(bf16[2,1024,128]{2,1,0:T(8,128)(2,1)S(1)} %collective-permute-done.1.u_ref), channel_id=1, source_target_pairs={{0,8},{8,0},{1,9},{9,1},{2,10},{10,2},{3,11},{11,3},{4,12},{12,4},... | collective-permute-start | bytes 1572872 | tf_op jit(solution)/shard_map/ppermute | solution.py:217
  71.6 3.3 %copy-start.7 = (bf16[1,1024,128]{2,1,0:T(8,128)(2,1)}, bf16[1,1024,128]{2,1,0:T(8,128)(2,1)S(1)}, u32[]{:S(2)}) copy-start(bf16[1,1024,128]{2,1,0:T(8,128)(2,1)S(1)} %collective-permute-done.7.g_ref) | copy-start | bytes 786436
  71.6 2.2 %collective-permute-start.8 = (bf16[1,1024,128]{2,1,0:T(8,128)(2,1)S(1)}, bf16[1,1024,128]{2,1,0:T(8,128)(2,1)S(1)}, u32[]{:S(2)}, u32[]{:S(2)}) collective-permute-start(bf16[1,1024,128]{2,1,0:T(8,128)(2,1)S(1)} %collective-permute-done.7.g_ref), channel_id=1, source_target_pairs={{0,8},{8,0},{1,9},{9,1},{2,10},{10,2},{3,11},{11,3},{4,12},{12,4},... | collective-permute-start | bytes 786440 | tf_op jit(solution)/shard_map/ppermute | solution.py:217
  72.9 2.0 %copy-start.8 = (bf16[1,1024,128]{2,1,0:T(8,128)(2,1)}, bf16[1,1024,128]{2,1,0:T(8,128)(2,1)S(1)}, u32[]{:S(2)}) copy-start(bf16[1,1024,128]{2,1,0:T(8,128)(2,1)S(1)} %collective-permute-done.5.h_ref) | copy-start | bytes 786436
  72.9 1.9 %collective-permute-start.6 = (bf16[1,1024,128]{2,1,0:T(8,128)(2,1)S(1)}, bf16[1,1024,128]{2,1,0:T(8,128)(2,1)S(1)}, u32[]{:S(2)}, u32[]{:S(2)}) collective-permute-start(bf16[1,1024,128]{2,1,0:T(8,128)(2,1)S(1)} %collective-permute-done.5.h_ref), channel_id=1, source_target_pairs={{0,8},{8,0},{1,9},{9,1},{2,10},{10,2},{3,11},{11,3},{4,12},{12,4},... | collective-permute-start | bytes 786440 | tf_op jit(solution)/shard_map/ppermute | solution.py:217
  73.7 1.1 copy-start.4
  73.8 1.1 copy-start.9
  73.8 1.1 copy-start.5
  74.8 0.7 copy-start.10
  75.5 0.8 copy-start.6

commit v2 on v1

--- a/solution.py
+++ b/solution.py
@@ -12,7 +12,7 @@
 LOW, HIGH = 2.0**-80, 2.0**100
 CHUNKS = 2
 TILE = 2048
-GROUPS = {8: {0: (0, 1), 1: tuple(range(2, 8))}}
+GROUPS = {8: {0: (0,), 1: tuple(range(1, 8))}}
 AXES = ("x", "yl", "core", "sy")
 
 
@@ -95,12 +95,16 @@
         def _():
             pltpu.make_async_copy(q_ref, qv_ref, sems.at[blocks]).start()
             x, core = where_ref[0], where_ref[1]
-            for step, refs in ((0, (c_ref, cc_ref)), (3, (u_ref, cu_ref)), (1, (v_ref, cv_ref)), (2, ((h_ref, g_ref), (ch_ref, cg_ref)))):
-                for other in (0, 1):
-                    for yl in (0, 1):
-                        src = refs[other][yl].at[0] if step == 2 else refs[other].at[yl]
-                        b = lax.rem(x + step, 4) * 4 + yl * 2 + lax.rem(core + other, 2)
-                        pltpu.make_async_copy(src, kv_ref.at[b], sems.at[b]).start()
+            for plane in range(4):
+                for step, refs in ((0, (c_ref, cc_ref)), (3, (u_ref, cu_ref)), (1, (v_ref, cv_ref)),
+                                   (2, ((h_ref, g_ref), (ch_ref, cg_ref)))):
+                    @pl.when(lax.rem(x + step, 4) == plane)
+                    def _():
+                        for yl in (0, 1):
+                            for other in (0, 1):
+                                src = refs[other][yl].at[0] if step == 2 else refs[other].at[yl]
+                                b = plane * 4 + yl * 2 + lax.rem(core + other, 2)
+                                pltpu.make_async_copy(src, kv_ref.at[b], sems.at[b]).start()
 
         @pl.when(qi == 0)
         def _():
@@ -109,16 +113,16 @@
         def landed(t):
             pltpu.make_async_copy(c_ref.at[0], kv_ref.at[first + t], sems.at[first + t]).wait()
 
-        qT_ref[...] = qv_ref[pl.ds(qi * devs, devs)].reshape(bq, D).astype(jnp.float32).T.astype(jnp.bfloat16)
 
         def values(blk, lo, n):
             return jnp.concatenate(
                 [kv_ref[blk, BK + lo + t * 128: BK + lo + (t + 1) * 128, :] for t in range(n // 128)], axis=1)
 
-        def block(blk, lo, masked):
+        def block(blk, lo, masked, fresh=False):
             for s in range(0, BK, sub):
                 k = kv_ref[blk, s:s + sub, :]
-                st = jnp.dot(k, qT_ref[:, lo:], preferred_element_type=jnp.float32)
+                rows = qv_ref[pl.ds(qi * devs + lo // strip, devs - lo // strip)].reshape(bq - lo, D)
+                st = lax.dot_general(k, rows, (((1,), (1,)), ((), ())), preferred_element_type=jnp.float32)
                 p = jnp.exp2(st * c)
                 if masked:
                     lane = lax.broadcasted_iota(jnp.int32, (1, w), 1)
@@ -126,29 +130,32 @@
                     row = s + lax.broadcasted_iota(jnp.int32, (sub, 1), 0)
                     head = jnp.where(row <= at, p[:, :w], 0.0)
                     p = jnp.concatenate([head, p[:, w:]], axis=1) if bq - lo > w else head
-                l_ref[:, lo:] += jnp.sum(p.reshape(sub // 8, 8, bq - lo), axis=0)
-                acc_ref[:, lo:] += jnp.dot(
-                    values(blk, s, sub), p.astype(jnp.bfloat16), preferred_element_type=jnp.float32)
-
-        acc_ref[...] = jnp.zeros_like(acc_ref)
-        l_ref[...] = jnp.zeros_like(l_ref)
+                mass = jnp.sum(p.reshape(sub // 8, 8, bq - lo), axis=0)
+                mixed = jnp.dot(values(blk, s, sub), p.astype(jnp.bfloat16), preferred_element_type=jnp.float32)
+                if fresh:
+                    l_ref[:, lo:] = mass
+                    acc_ref[:, lo:] = mixed
+                else:
+                    l_ref[:, lo:] += mass
+                    acc_ref[:, lo:] += mixed
 
         def body(j, _):
             for u in range(unroll):
                 block(j * unroll + u, 0, False)
             return 0
 
-        lax.fori_loop(0, first // unroll, body, 0)
         for t in range(nd):
             for later in groups.get(t, ()):
                 landed(later)
-            block(first + t, t * w, True)
+            block(first + t, t * w, True, t == 0)
+        lax.fori_loop(0, first // unroll, body, 0)
         total = jnp.sum(l_ref[...], axis=0, keepdims=True)
         o_ref[...] = (acc_ref[...] * (1.0 / total)).T.astype(jnp.bfloat16).reshape(o_ref.shape)
         fine = jnp.logical_and(jnp.min(total) > LOW, jnp.max(total) < HIGH)
 
         @pl.when(jnp.logical_not(fine))
         def _():
+            qT_ref[...] = qv_ref[pl.ds(qi * devs, devs)].reshape(bq, D).astype(jnp.float32).T.astype(jnp.bfloat16)
             lane = lax.broadcasted_iota(jnp.int32, (1, bq), 1)
             at = qi * devs * period + lane // strip * period + offset + lane % strip
 

time: 179 us -> 179 us (level)
  no operation moved by 1% of the time
where the time goes in v2:
time: 179 us; the launch traced here: 178 us
  blocking collectives  61.8 us (35%)
  Pallas kernels  47 us (26%)
  waiting for transfers between devices  34.5 us (19%)
  starting transfers between devices  29.5 us (16%)
  local copies, waits for them, and re-layouts  4.47 us (2%)
    all_to_all x1, blocking collectives, shards(): lax.all_to_all(out.swapaxes(0, 1), AXES, split_axis=1, concat_axis=1, til...  61.8 us
    pallas_call x2, Pallas kernels, attn(): pl.pallas_call(kernel, grid=(G // devs,), in_specs=[pl.BlockSpec(memory_s...  37.5 us
    all_to_all x2, waiting for transfers between devices, shards(): lax.all_to_all(ordered[n], AXES, split_axis=0, concat_axis=0, tiled=True)  16.9 us
    ppermute x1, waiting for transfers between devices, shards(): g = lax.ppermute(v[1:2], 'x', behind)  14 us
    all_to_all x2, starting transfers between devices, shards(): lax.all_to_all(ordered[n], AXES, split_axis=0, concat_axis=0, tiled=True)  12.9 us
    all_to_all x1, starting transfers between devices, shards(): lax.all_to_all(pair, ('yl', 'sy'), split_axis=0, concat_axis=0, tiled=True)  8.59 us
    pallas_call x1, Pallas kernels, prepare_queries(): pl.pallas_call(kernel, grid=(heads // group,), in_specs=[pl.BlockSpec((ro...  7.19 us
  transfers between devices with their start and end apart: 12, of which 5 were waited for; matrix products, arithmetic and copies ran while one was open for 0% of the time, Pallas kernels for 14%

profile of v2, /device:TPU:1, one launch (start us, length us, event | category | flops | bytes accessed | tf_op | source)
XLA Modules:
  0.0 178.4 jit_solution(4650842246202825921)
XLA Ops:
  0.1 0.1 mul.58
  0.1 0.8 fusion
  1.0 2.3 %pair.1 = bf16[16,2,64,128]{3,2,1,0:T(8,128)(2,1)} custom-call(bf16[64,8,128]{2,1,0:T(8,128)(2,1)} %k_ref.1, bf16[64,8,128]{2,1,0:T(8,128)(2,1)} %v_ref.1, f32[64,128]{1,0:T(8,128)} %get-tuple-element.12.cos_ref, f32[64,128]{1,0:T(8,128)} %get-tuple-element.11.sin_ref), custom_call_target="tpu_custom_call" | custom-call | tf_op jit(solution)/shard_map/pair/pallas_call | solution.py:48
  3.2 8.6 %all-to-all-start.1 = ((bf16[16,2,64,128]{3,2,1,0:T(8,128)(2,1)}), bf16[16,2,64,128]{3,2,1,0:T(8,128)(2,1)S(1)}, u32[]{:S(2)}, u32[]{:S(2)}) async-start(bf16[16,2,64,128]{3,2,1,0:T(8,128)(2,1)} %pair.1), calls=%async_computation.1 | async-start | bytes 1048576 | tf_op jit(solution)/shard_map/all_to_all | solution.py:210
  11.8 7.2 %queries.1 = (bf16[16,8,32,128]{3,2,1,0:T(8,128)(2,1)}, bf16[16,8,32,128]{3,2,1,0:T(8,128)(2,1)}) custom-call(bf16[64,128,128]{2,1,0:T(8,128)(2,1)} %q_ref.1, f32[64,128]{1,0:T(8,128)} %get-tuple-element.12.cos_ref, f32[64,128]{1,0:T(8,128)} %get-tuple-element.11.sin_ref), custom_call_target="tpu_custom_call" | custom-call | tf_op jit(solution)/shard_map/queries/pallas_call | solution.py:67
  19.0 2.0 %all-to-all-done.1 = bf16[16,2,64,128]{3,2,1,0:T(8,128)(2,1)S(1)} async-done(((bf16[16,2,64,128]{3,2,1,0:T(8,128)(2,1)}), bf16[16,2,64,128]{3,2,1,0:T(8,128)(2,1)S(1)}, u32[]{:S(2)}, u32[]{:S(2)}) %all-to-all-start.1) | async-done | bytes 524320 | tf_op jit(solution)/shard_map/all_to_all | solution.py:210
  21.1 8.3 %all-to-all-start.2 = ((bf16[128,32,128]{2,1,0:T(8,128)(2,1)}), bf16[128,32,128]{2,1,0:T(8,128)(2,1)S(1)}, u32[]{:S(2)}, u32[]{:S(2)}) async-start(bf16[128,32,128]{2,1,0:T(8,128)(2,1)} %bitcast.19), calls=%async_computation.2 | async-start | bytes 2097152 | tf_op jit(solution)/shard_map/all_to_all | solution.py:230
  29.4 0.2 copy.5
  29.6 0.0 copy-start
  29.6 2.6 %collective-permute-start.3 = (bf16[2,1024,128]{2,1,0:T(8,128)(2,1)S(1)}, bf16[2,1024,128]{2,1,0:T(8,128)(2,1)S(1)}, u32[]{:S(2)}, u32[]{:S(2)}) collective-permute-start(bf16[2,1024,128]{2,1,0:T(8,128)(2,1)S(1)} %pad_maximum_fusion.c_ref), channel_id=1, source_target_pairs={{0,96},{32,0},{64,32},{96,64},{1,97},{33,1},{65,33},{97,65},{2,98}... | collective-permute-start | bytes 1572872 | tf_op jit(solution)/shard_map/ppermute | solution.py:219
  32.2 0.0 collective-permute-start.1
  32.2 16.9 %all-to-all-done.2.q_ref = bf16[128,32,128]{2,1,0:T(8,128)(2,1)S(1)} async-done(((bf16[128,32,128]{2,1,0:T(8,128)(2,1)}), bf16[128,32,128]{2,1,0:T(8,128)(2,1)S(1)}, u32[]{:S(2)}, u32[]{:S(2)}) %all-to-all-start.2) | async-done | bytes 1048608 | tf_op jit(solution)/shard_map/all_to_all | solution.py:230
  49.1 4.7 %all-to-all-start = ((bf16[128,32,128]{2,1,0:T(8,128)(2,1)}), bf16[128,32,128]{2,1,0:T(8,128)(2,1)}, u32[]{:S(2)}, u32[]{:S(2)}) async-start(bf16[128,32,128]{2,1,0:T(8,128)(2,1)} %bitcast.18), calls=%async_computation | async-start | bytes 2097152 | tf_op jit(solution)/shard_map/all_to_all | solution.py:230
  53.8 1.2 collective-permute-start
  55.0 0.0 collective-permute-done.3.v_ref
  55.1 1.8 %collective-permute-start.7 = (bf16[1,1024,128]{2,1,0:T(8,128)(2,1)S(1)}, bf16[1,1024,128]{2,1,0:T(8,128)(2,1)S(1)}, u32[]{:S(2)}, u32[]{:S(2)}) collective-permute-start(bf16[1,1024,128]{2,1,0:T(8,128)(2,1)S(1)} %slice.21), channel_id=1, source_target_pairs={{0,96},{32,0},{64,32},{96,64},{1,97},{33,1},{65,33},{97,65},{2,98}... | collective-permute-start | bytes 786440 | tf_op jit(solution)/shard_map/ppermute | solution.py:221
  56.9 0.4 collective-permute-start.4
  57.3 0.0 collective-permute-done.1.u_ref
  57.3 0.1 collective-permute-start.5
  57.4 0.2 collective-permute-start.2
  57.6 14.0 %collective-permute-done.7.g_ref = bf16[1,1024,128]{2,1,0:T(8,128)(2,1)S(1)} collective-permute-done((bf16[1,1024,128]{2,1,0:T(8,128)(2,1)S(1)}, bf16[1,1024,128]{2,1,0:T(8,128)(2,1)S(1)}, u32[]{:S(2)}, u32[]{:S(2)}) %collective-permute-start.7) | collective-permute-done | bytes 262176 | tf_op jit(solution)/shard_map/ppermute | solution.py:221
  71.6 0.9 collective-permute-start.8
  72.4 0.5 collective-permute-done.5.h_ref
  72.9 0.8 collective-permute-start.6
  73.7 0.1 pad_add_fusion.where_ref
  73.7 0.0 collective-permute-done.cc_ref
  73.7 0.0 collective-permute-done.8.cg_ref
  73.8 0.0 copy-start.9
  73.8 0.0 collective-permute-done.4.cv_ref
  73.8 0.0 copy-start.5
  73.8 1.0 collective-permute-done.6.ch_ref
  74.8 0.0 copy-done.1
  74.8 0.0 copy-done.3
  74.8 0.0 collective-permute-done.2.cu_ref
  74.8 0.0 copy-done
  74.9 0.0 copy-done.2
  74.9 0.0 copy-done.7
  74.9 0.0 copy-done.8
  74.9 0.0 copy-done.4
  74.9 0.0 copy-done.9
  74.9 0.0 copy-done.5
  74.9 0.6 copy-done.10
  75.5 0.8 copy-done.6
  76.3 18.6 %attn.2.rest_0_ = bf16[128,64,128]{2,1,0:T(8,128)(2,1)S(1)} custom-call(s32[2]{0:T(128)S(1)} %pad_add_fusion.where_ref, bf16[128,32,128]{2,1,0:T(8,128)(2,1)} %copy-done.1, bf16[2,1024,128]{2,1,0:T(8,128)(2,1)} %copy-done, bf16[2,1024,128]{2,1,0:T(8,128)(2,1)} %copy-done.4, bf16[2,1024,128]{2,1,0:T(8,128)(2,1)} %copy-done.3, ...), custom_call_target="tpu_custom_call" | custom-call | tf_op jit(solution)/shard_map/attn/pallas_call | solution.py:181
  95.0 0.0 all-to-all-done.q_ref
  95.0 18.9 %attn.3 = bf16[128,64,128]{2,1,0:T(8,128)(2,1)S(1)} custom-call(s32[2]{0:T(128)S(1)} %pad_add_fusion.where_ref, bf16[128,32,128]{2,1,0:T(8,128)(2,1)} %all-to-all-done.q_ref, bf16[2,1024,128]{2,1,0:T(8,128)(2,1)} %copy-done, bf16[2,1024,128]{2,1,0:T(8,128)(2,1)} %copy-done.4, bf16[2,1024,128]{2,1,0:T(8,128)(2,1)} %copy-done.3, ...), custom_call_target="tpu_custom_call", output_to_operand_aliasing={{}: (12, {})} | custom-call | tf_op jit(solution)/shard_map/attn/pallas_call | solution.py:181
  113.9 61.8 %all_to_all.20 = bf16[64,128,128]{2,0,1:T(8,128)(2,1)S(1)} all-to-all(bf16[64,128,128]{2,0,1:T(8,128)(2,1)S(1)} %bitcast.15), channel_id=1, replica_groups=mesh['x'=4,'yl'=2,'core'=2,'sy'=8] {'x','yl','core','sy'}, dimensions={1} | all-to-all | bytes 4194304 | tf_op jit(solution)/shard_map/all_to_all | solution.py:234
  175.7 2.7 %copy.6 = bf16[64,8,16,128]{3,2,1,0:T(8,128)(2,1)} copy(bf16[64,8,16,128]{3,0,1,2:T(8,128)(2,1)S(1)} %bitcast.16) | data formatting | bytes 4194304 | tf_op jit(solution)/shard_map/transpose | solution.py:237
  (16 shorter events, 0.2 us)
Async XLA Ops:
  3.2 17.8 %all-to-all-start.1 = ((bf16[16,2,64,128]{3,2,1,0:T(8,128)(2,1)}), bf16[16,2,64,128]{3,2,1,0:T(8,128)(2,1)S(1)}, u32[]{:S(2)}, u32[]{:S(2)}) async-start(bf16[16,2,64,128]{3,2,1,0:T(8,128)(2,1)} %pair.1), calls=%async_computation.1 | async-start | bytes 1048576 | tf_op jit(solution)/shard_map/all_to_all | solution.py:210
  21.1 28.1 %all-to-all-start.2 = ((bf16[128,32,128]{2,1,0:T(8,128)(2,1)}), bf16[128,32,128]{2,1,0:T(8,128)(2,1)S(1)}, u32[]{:S(2)}, u32[]{:S(2)}) async-start(bf16[128,32,128]{2,1,0:T(8,128)(2,1)} %bitcast.19), calls=%async_computation.2 | async-start | bytes 2097152 | tf_op jit(solution)/shard_map/all_to_all | solution.py:230
  29.6 45.3 %copy-start = (bf16[2,1024,128]{2,1,0:T(8,128)(2,1)}, bf16[2,1024,128]{2,1,0:T(8,128)(2,1)S(1)}, u32[]{:S(2)}) copy-start(bf16[2,1024,128]{2,1,0:T(8,128)(2,1)S(1)} %pad_maximum_fusion.c_ref) | copy-start | bytes 1572868
  29.6 25.4 %collective-permute-start.3 = (bf16[2,1024,128]{2,1,0:T(8,128)(2,1)S(1)}, bf16[2,1024,128]{2,1,0:T(8,128)(2,1)S(1)}, u32[]{:S(2)}, u32[]{:S(2)}) collective-permute-start(bf16[2,1024,128]{2,1,0:T(8,128)(2,1)S(1)} %pad_maximum_fusion.c_ref), channel_id=1, source_target_pairs={{0,96},{32,0},{64,32},{96,64},{1,97},{33,1},{65,33},{97,65},{2,98}... | collective-permute-start | bytes 1572872 | tf_op jit(solution)/shard_map/ppermute | solution.py:219
  32.2 25.0 %collective-permute-start.1 = (bf16[2,1024,128]{2,1,0:T(8,128)(2,1)S(1)}, bf16[2,1024,128]{2,1,0:T(8,128)(2,1)S(1)}, u32[]{:S(2)}, u32[]{:S(2)}) collective-permute-start(bf16[2,1024,128]{2,1,0:T(8,128)(2,1)S(1)} %pad_maximum_fusion.c_ref), channel_id=1, source_target_pairs={{0,32},{32,64},{64,96},{96,0},{1,33},{33,65},{65,97},{97,1},{2,34}... | collective-permute-start | bytes 1572872 | tf_op jit(solution)/shard_map/ppermute | solution.py:218
  49.1 25.7 %copy-start.1 = (bf16[128,32,128]{2,1,0:T(8,128)(2,1)}, bf16[128,32,128]{2,1,0:T(8,128)(2,1)S(1)}, u32[]{:S(2)}) copy-start(bf16[128,32,128]{2,1,0:T(8,128)(2,1)S(1)} %all-to-all-done.2.q_ref) | copy-start | bytes 3145732
  49.1 45.9 %all-to-all-start = ((bf16[128,32,128]{2,1,0:T(8,128)(2,1)}), bf16[128,32,128]{2,1,0:T(8,128)(2,1)}, u32[]{:S(2)}, u32[]{:S(2)}) async-start(bf16[128,32,128]{2,1,0:T(8,128)(2,1)} %bitcast.18), calls=%async_computation | async-start | bytes 2097152 | tf_op jit(solution)/shard_map/all_to_all | solution.py:230
  53.8 19.9 %collective-permute-start = (bf16[2,1024,128]{2,1,0:T(8,128)(2,1)S(1)}, bf16[2,1024,128]{2,1,0:T(8,128)(2,1)S(1)}, u32[]{:S(2)}, u32[]{:S(2)}) collective-permute-start(bf16[2,1024,128]{2,1,0:T(8,128)(2,1)S(1)} %pad_maximum_fusion.c_ref), channel_id=1, source_target_pairs={{0,8},{8,0},{1,9},{9,1},{2,10},{10,2},{3,11},{11,3},{4,12},{12,4},... | collective-permute-start | bytes 1572872 | tf_op jit(solution)/shard_map/ppermute | solution.py:224
  55.0 19.8 %copy-start.2 = (bf16[2,1024,128]{2,1,0:T(8,128)(2,1)}, bf16[2,1024,128]{2,1,0:T(8,128)(2,1)S(1)}, u32[]{:S(2)}) copy-start(bf16[2,1024,128]{2,1,0:T(8,128)(2,1)S(1)} %collective-permute-done.3.v_ref) | copy-start | bytes 1572868
  55.1 16.5 %collective-permute-start.7 = (bf16[1,1024,128]{2,1,0:T(8,128)(2,1)S(1)}, bf16[1,1024,128]{2,1,0:T(8,128)(2,1)S(1)}, u32[]{:S(2)}, u32[]{:S(2)}) collective-permute-start(bf16[1,1024,128]{2,1,0:T(8,128)(2,1)S(1)} %slice.21), channel_id=1, source_target_pairs={{0,96},{32,0},{64,32},{96,64},{1,97},{33,1},{65,33},{97,65},{2,98}... | collective-permute-start | bytes 786440 | tf_op jit(solution)/shard_map/ppermute | solution.py:221
  56.9 16.9 %collective-permute-start.4 = (bf16[2,1024,128]{2,1,0:T(8,128)(2,1)S(1)}, bf16[2,1024,128]{2,1,0:T(8,128)(2,1)S(1)}, u32[]{:S(2)}, u32[]{:S(2)}) collective-permute-start(bf16[2,1024,128]{2,1,0:T(8,128)(2,1)S(1)} %collective-permute-done.3.v_ref), channel_id=1, source_target_pairs={{0,8},{8,0},{1,9},{9,1},{2,10},{10,2},{3,11},{11,3},{4,12},{12,4},... | collective-permute-start | bytes 1572872 | tf_op jit(solution)/shard_map/ppermute | solution.py:224
  57.3 17.6 %copy-start.3 = (bf16[2,1024,128]{2,1,0:T(8,128)(2,1)}, bf16[2,1024,128]{2,1,0:T(8,128)(2,1)S(1)}, u32[]{:S(2)}) copy-start(bf16[2,1024,128]{2,1,0:T(8,128)(2,1)S(1)} %collective-permute-done.1.u_ref) | copy-start | bytes 1572868
  57.3 15.6 %collective-permute-start.5 = (bf16[1,1024,128]{2,1,0:T(8,128)(2,1)S(1)}, bf16[1,1024,128]{2,1,0:T(8,128)(2,1)S(1)}, u32[]{:S(2)}, u32[]{:S(2)}) collective-permute-start(bf16[1,1024,128]{2,1,0:T(8,128)(2,1)S(1)} %slice.20), channel_id=1, source_target_pairs={{0,32},{32,64},{64,96},{96,0},{1,33},{33,65},{65,97},{97,1},{2,34}... | collective-permute-start | bytes 786440 | tf_op jit(solution)/shard_map/ppermute | solution.py:220
  57.4 17.5 %collective-permute-start.2 = (bf16[2,1024,128]{2,1,0:T(8,128)(2,1)S(1)}, bf16[2,1024,128]{2,1,0:T(8,128)(2,1)S(1)}, u32[]{:S(2)}, u32[]{:S(2)}) collective-permute-start(bf16[2,1024,128]{2,1,0:T(8,128)(2,1)S(1)} %collective-permute-done.1.u_ref), channel_id=1, source_target_pairs={{0,8},{8,0},{1,9},{9,1},{2,10},{10,2},{3,11},{11,3},{4,12},{12,4},... | collective-permute-start | bytes 1572872 | tf_op jit(solution)/shard_map/ppermute | solution.py:224
  71.6 3.3 %copy-start.7 = (bf16[1,1024,128]{2,1,0:T(8,128)(2,1)}, bf16[1,1024,128]{2,1,0:T(8,128)(2,1)S(1)}, u32[]{:S(2)}) copy-start(bf16[1,1024,128]{2,1,0:T(8,128)(2,1)S(1)} %collective-permute-done.7.g_ref) | copy-start | bytes 786436
  71.6 2.2 %collective-permute-start.8 = (bf16[1,1024,128]{2,1,0:T(8,128)(2,1)S(1)}, bf16[1,1024,128]{2,1,0:T(8,128)(2,1)S(1)}, u32[]{:S(2)}, u32[]{:S(2)}) collective-permute-start(bf16[1,1024,128]{2,1,0:T(8,128)(2,1)S(1)} %collective-permute-done.7.g_ref), channel_id=1, source_target_pairs={{0,8},{8,0},{1,9},{9,1},{2,10},{10,2},{3,11},{11,3},{4,12},{12,4},... | collective-permute-start | bytes 786440 | tf_op jit(solution)/shard_map/ppermute | solution.py:224
  72.9 2.0 %copy-start.8 = (bf16[1,1024,128]{2,1,0:T(8,128)(2,1)}, bf16[1,1024,128]{2,1,0:T(8,128)(2,1)S(1)}, u32[]{:S(2)}) copy-start(bf16[1,1024,128]{2,1,0:T(8,128)(2,1)S(1)} %collective-permute-done.5.h_ref) | copy-start | bytes 786436
  72.9 1.9 %collective-permute-start.6 = (bf16[1,1024,128]{2,1,0:T(8,128)(2,1)S(1)}, bf16[1,1024,128]{2,1,0:T(8,128)(2,1)S(1)}, u32[]{:S(2)}, u32[]{:S(2)}) collective-permute-start(bf16[1,1024,128]{2,1,0:T(8,128)(2,1)S(1)} %collective-permute-done.5.h_ref), channel_id=1, source_target_pairs={{0,8},{8,0},{1,9},{9,1},{2,10},{10,2},{3,11},{11,3},{4,12},{12,4},... | collective-permute-start | bytes 786440 | tf_op jit(solution)/shard_map/ppermute | solution.py:224
  73.7 1.1 copy-start.4
  73.8 1.1 copy-start.9
  73.8 1.1 copy-start.5
  74.8 0.7 copy-start.10
  75.5 0.8 copy-start.6

commit v3 on v2

--- a/solution.py
+++ b/solution.py
@@ -217,11 +217,13 @@
     swap = [(0, 1), (1, 0)]
     u = lax.ppermute(c, "x", ahead)
     v = lax.ppermute(c, "x", behind)
-    h = lax.ppermute(u[0:1], "x", ahead)
-    g = lax.ppermute(v[1:2], "x", behind)
-    pieces = []
-    for piece in (c, u, v, h, g):
-        pieces += [piece, lax.ppermute(piece, "core", swap)]
+    near = []
+    for piece in (c, u, v):
+        near += [piece, lax.ppermute(piece, "core", swap)]
+    far = []
+    for source, half, way in ((near[2], 0, ahead), (near[4], 1, behind), (near[3], 0, ahead), (near[5], 1, behind)):
+        far.append(lax.ppermute(source[half:half + 1], "x", way))
+    pieces = near + [far[0], far[2], far[1], far[3]]
     where = jnp.stack([x, core]).astype(jnp.int32)
 
     ordered = prepare_queries(queries, cosine, signed_sine, group)

time: 179 us -> 182 us (1.017)
  waiting for transfers between devices: 34.5 us -> 36.7 us
    ppermute x7, waiting for transfers between devices: 15.5 us -> 17.8 us  [the longest x4 17.8 us: shards(): far.append(lax.ppermute(source[half:half + 1], 'x', way))]
  transfers between devices with their start and end apart: 12 -> 12, of which waited for: 5 -> 6; matrix products, arithmetic and copies ran while one was open for 0% -> 0% of each run, Pallas kernels for 14% -> 14%
where the time goes in v3:
time: 182 us; the launch traced here: 181 us
  blocking collectives  62 us (34%)
  Pallas kernels  47 us (26%)
  waiting for transfers between devices  36.7 us (20%)
  starting transfers between devices  30.7 us (17%)
  local copies, waits for them, and re-layouts  3.78 us (2%)
    all_to_all x1, blocking collectives, shards(): lax.all_to_all(out.swapaxes(0, 1), AXES, split_axis=1, concat_axis=1, til...  62 us
    pallas_call x2, Pallas kernels, attn(): pl.pallas_call(kernel, grid=(G // devs,), in_specs=[pl.BlockSpec(memory_s...  37.5 us
    ppermute x4, waiting for transfers between devices, shards(): far.append(lax.ppermute(source[half:half + 1], 'x', way))  17.8 us
    all_to_all x2, waiting for transfers between devices, shards(): lax.all_to_all(ordered[n], AXES, split_axis=0, concat_axis=0, tiled=True)  16.9 us
    all_to_all x2, starting transfers between devices, shards(): lax.all_to_all(ordered[n], AXES, split_axis=0, concat_axis=0, tiled=True)  12.9 us
    all_to_all x1, starting transfers between devices, shards(): lax.all_to_all(pair, ('yl', 'sy'), split_axis=0, concat_axis=0, tiled=True)  8.59 us
    pallas_call x1, Pallas kernels, prepare_queries(): pl.pallas_call(kernel, grid=(heads // group,), in_specs=[pl.BlockSpec((ro...  7.19 us
    ppermute x4, starting transfers between devices, shards(): far.append(lax.ppermute(source[half:half + 1], 'x', way))  4.83 us
  transfers between devices with their start and end apart: 12, of which 6 were waited for; matrix products, arithmetic and copies ran while one was open for 0% of the time, Pallas kernels for 14%

profile of v3, /device:TPU:1, one launch (start us, length us, event | category | flops | bytes accessed | tf_op | source)
XLA Modules:
  0.0 181.4 jit_solution(2567153046881008041)
XLA Ops:
  0.1 0.1 mul.58
  0.1 0.8 fusion
  1.0 2.3 %pair.1 = bf16[16,2,64,128]{3,2,1,0:T(8,128)(2,1)} custom-call(bf16[64,8,128]{2,1,0:T(8,128)(2,1)} %k_ref.1, bf16[64,8,128]{2,1,0:T(8,128)(2,1)} %v_ref.1, f32[64,128]{1,0:T(8,128)} %get-tuple-element.12.cos_ref, f32[64,128]{1,0:T(8,128)} %get-tuple-element.11.sin_ref), custom_call_target="tpu_custom_call" | custom-call | tf_op jit(solution)/shard_map/pair/pallas_call | solution.py:48
  3.2 8.6 %all-to-all-start.1 = ((bf16[16,2,64,128]{3,2,1,0:T(8,128)(2,1)}), bf16[16,2,64,128]{3,2,1,0:T(8,128)(2,1)S(1)}, u32[]{:S(2)}, u32[]{:S(2)}) async-start(bf16[16,2,64,128]{3,2,1,0:T(8,128)(2,1)} %pair.1), calls=%async_computation.1 | async-start | bytes 1048576 | tf_op jit(solution)/shard_map/all_to_all | solution.py:210
  11.8 7.2 %queries.1 = (bf16[16,8,32,128]{3,2,1,0:T(8,128)(2,1)}, bf16[16,8,32,128]{3,2,1,0:T(8,128)(2,1)}) custom-call(bf16[64,128,128]{2,1,0:T(8,128)(2,1)} %q_ref.1, f32[64,128]{1,0:T(8,128)} %get-tuple-element.12.cos_ref, f32[64,128]{1,0:T(8,128)} %get-tuple-element.11.sin_ref), custom_call_target="tpu_custom_call" | custom-call | tf_op jit(solution)/shard_map/queries/pallas_call | solution.py:67
  19.0 2.0 %all-to-all-done.1 = bf16[16,2,64,128]{3,2,1,0:T(8,128)(2,1)S(1)} async-done(((bf16[16,2,64,128]{3,2,1,0:T(8,128)(2,1)}), bf16[16,2,64,128]{3,2,1,0:T(8,128)(2,1)S(1)}, u32[]{:S(2)}, u32[]{:S(2)}) %all-to-all-start.1) | async-done | bytes 524320 | tf_op jit(solution)/shard_map/all_to_all | solution.py:210
  21.1 8.3 %all-to-all-start.2 = ((bf16[128,32,128]{2,1,0:T(8,128)(2,1)}), bf16[128,32,128]{2,1,0:T(8,128)(2,1)S(1)}, u32[]{:S(2)}, u32[]{:S(2)}) async-start(bf16[128,32,128]{2,1,0:T(8,128)(2,1)} %bitcast.19), calls=%async_computation.2 | async-start | bytes 2097152 | tf_op jit(solution)/shard_map/all_to_all | solution.py:232
  29.4 0.2 copy.5
  29.6 0.0 copy-start
  29.6 2.6 %collective-permute-start.3 = (bf16[2,1024,128]{2,1,0:T(8,128)(2,1)S(1)}, bf16[2,1024,128]{2,1,0:T(8,128)(2,1)S(1)}, u32[]{:S(2)}, u32[]{:S(2)}) collective-permute-start(bf16[2,1024,128]{2,1,0:T(8,128)(2,1)S(1)} %pad_maximum_fusion.c_ref), channel_id=1, source_target_pairs={{0,96},{32,0},{64,32},{96,64},{1,97},{33,1},{65,33},{97,65},{2,98}... | collective-permute-start | bytes 1572872 | tf_op jit(solution)/shard_map/ppermute | solution.py:219
  32.2 0.0 collective-permute-start.1
  32.2 16.9 %all-to-all-done.2.q_ref = bf16[128,32,128]{2,1,0:T(8,128)(2,1)S(1)} async-done(((bf16[128,32,128]{2,1,0:T(8,128)(2,1)}), bf16[128,32,128]{2,1,0:T(8,128)(2,1)S(1)}, u32[]{:S(2)}, u32[]{:S(2)}) %all-to-all-start.2) | async-done | bytes 1048608 | tf_op jit(solution)/shard_map/all_to_all | solution.py:232
  49.1 4.7 %all-to-all-start = ((bf16[128,32,128]{2,1,0:T(8,128)(2,1)}), bf16[128,32,128]{2,1,0:T(8,128)(2,1)}, u32[]{:S(2)}, u32[]{:S(2)}) async-start(bf16[128,32,128]{2,1,0:T(8,128)(2,1)} %bitcast.18), calls=%async_computation | async-start | bytes 2097152 | tf_op jit(solution)/shard_map/all_to_all | solution.py:232
  53.8 0.0 collective-permute-done.3.v_ref
  53.8 0.0 copy-start.2
  53.8 1.2 collective-permute-start.4
  55.1 0.0 collective-permute-done.1.u_ref
  55.1 0.3 collective-permute-start.2
  55.3 0.2 collective-permute-start
  55.6 1.8 collective-permute-start.7
  57.4 0.1 collective-permute-start.5
  57.5 0.0 collective-permute-done.4.cv_ref
  57.5 0.0 copy-start.4
  57.5 2.7 %collective-permute-start.8 = (bf16[1,1024,128]{2,1,0:T(8,128)(2,1)S(1)}, bf16[1,1024,128]{2,1,0:T(8,128)(2,1)S(1)}, u32[]{:S(2)}, u32[]{:S(2)}) collective-permute-start(bf16[1,1024,128]{2,1,0:T(8,128)(2,1)S(1)} %slice.31), channel_id=1, source_target_pairs={{0,96},{32,0},{64,32},{96,64},{1,97},{33,1},{65,33},{97,65},{2,98}... | collective-permute-start | bytes 786440 | tf_op jit(solution)/shard_map/ppermute | solution.py:225
  60.3 0.0 collective-permute-done.2.cu_ref
  60.3 0.0 copy-done
  60.3 0.0 copy-done.1
  60.3 0.3 collective-permute-start.6
  60.6 0.1 pad_add_fusion.where_ref
  60.6 0.0 collective-permute-done.cc_ref
  60.6 10.9 %collective-permute-done.7.g_ref = bf16[1,1024,128]{2,1,0:T(8,128)(2,1)S(1)} collective-permute-done((bf16[1,1024,128]{2,1,0:T(8,128)(2,1)S(1)}, bf16[1,1024,128]{2,1,0:T(8,128)(2,1)S(1)}, u32[]{:S(2)}, u32[]{:S(2)}) %collective-permute-start.7) | collective-permute-done | bytes 262176 | tf_op jit(solution)/shard_map/ppermute | solution.py:225
  71.6 1.3 collective-permute-done.5.h_ref
  72.9 4.2 %collective-permute-done.8.cg_ref = bf16[1,1024,128]{2,1,0:T(8,128)(2,1)S(1)} collective-permute-done((bf16[1,1024,128]{2,1,0:T(8,128)(2,1)S(1)}, bf16[1,1024,128]{2,1,0:T(8,128)(2,1)S(1)}, u32[]{:S(2)}, u32[]{:S(2)}) %collective-permute-start.8) | collective-permute-done | bytes 262176 | tf_op jit(solution)/shard_map/ppermute | solution.py:225
  77.1 0.0 copy-done.3
  77.1 1.3 collective-permute-done.6.ch_ref
  78.4 0.0 copy-done.2
  78.4 0.0 copy-done.4
  78.4 0.0 copy-done.5
  78.4 0.0 copy-done.6
  78.4 0.0 copy-done.7
  78.5 0.0 copy-done.8
  78.5 0.0 copy-done.9
  78.5 0.7 copy-done.10
  79.2 18.6 %attn.2.rest_0_ = bf16[128,64,128]{2,1,0:T(8,128)(2,1)S(1)} custom-call(s32[2]{0:T(128)S(1)} %pad_add_fusion.where_ref, bf16[128,32,128]{2,1,0:T(8,128)(2,1)} %copy-done.1, bf16[2,1024,128]{2,1,0:T(8,128)(2,1)} %copy-done, bf16[2,1024,128]{2,1,0:T(8,128)(2,1)} %copy-done.6, bf16[2,1024,128]{2,1,0:T(8,128)(2,1)} %copy-done.3, ...), custom_call_target="tpu_custom_call" | custom-call | tf_op jit(solution)/shard_map/attn/pallas_call | solution.py:181
  97.8 0.0 all-to-all-done.q_ref
  97.8 18.9 %attn.3 = bf16[128,64,128]{2,1,0:T(8,128)(2,1)S(1)} custom-call(s32[2]{0:T(128)S(1)} %pad_add_fusion.where_ref, bf16[128,32,128]{2,1,0:T(8,128)(2,1)} %all-to-all-done.q_ref, bf16[2,1024,128]{2,1,0:T(8,128)(2,1)} %copy-done, bf16[2,1024,128]{2,1,0:T(8,128)(2,1)} %copy-done.6, bf16[2,1024,128]{2,1,0:T(8,128)(2,1)} %copy-done.3, ...), custom_call_target="tpu_custom_call", output_to_operand_aliasing={{}: (12, {})} | custom-call | tf_op jit(solution)/shard_map/attn/pallas_call | solution.py:181
  116.7 62.0 %all_to_all.20 = bf16[64,128,128]{2,0,1:T(8,128)(2,1)S(1)} all-to-all(bf16[64,128,128]{2,0,1:T(8,128)(2,1)S(1)} %bitcast.15), channel_id=1, replica_groups=mesh['x'=4,'yl'=2,'core'=2,'sy'=8] {'x','yl','core','sy'}, dimensions={1} | all-to-all | bytes 4194304 | tf_op jit(solution)/shard_map/all_to_all | solution.py:236
  178.7 2.7 %copy.6 = bf16[64,8,16,128]{3,2,1,0:T(8,128)(2,1)} copy(bf16[64,8,16,128]{3,0,1,2:T(8,128)(2,1)S(1)} %bitcast.16) | data formatting | bytes 4194304 | tf_op jit(solution)/shard_map/transpose | solution.py:239
  (18 shorter events, 0.2 us)
Async XLA Ops:
  3.2 17.8 %all-to-all-start.1 = ((bf16[16,2,64,128]{3,2,1,0:T(8,128)(2,1)}), bf16[16,2,64,128]{3,2,1,0:T(8,128)(2,1)S(1)}, u32[]{:S(2)}, u32[]{:S(2)}) async-start(bf16[16,2,64,128]{3,2,1,0:T(8,128)(2,1)} %pair.1), calls=%async_computation.1 | async-start | bytes 1048576 | tf_op jit(solution)/shard_map/all_to_all | solution.py:210
  21.1 28.1 %all-to-all-start.2 = ((bf16[128,32,128]{2,1,0:T(8,128)(2,1)}), bf16[128,32,128]{2,1,0:T(8,128)(2,1)S(1)}, u32[]{:S(2)}, u32[]{:S(2)}) async-start(bf16[128,32,128]{2,1,0:T(8,128)(2,1)} %bitcast.19), calls=%async_computation.2 | async-start | bytes 2097152 | tf_op jit(solution)/shard_map/all_to_all | solution.py:232
  29.6 30.7 %copy-start = (bf16[2,1024,128]{2,1,0:T(8,128)(2,1)}, bf16[2,1024,128]{2,1,0:T(8,128)(2,1)S(1)}, u32[]{:S(2)}) copy-start(bf16[2,1024,128]{2,1,0:T(8,128)(2,1)S(1)} %pad_maximum_fusion.c_ref) | copy-start | bytes 1572868
  29.6 24.2 %collective-permute-start.3 = (bf16[2,1024,128]{2,1,0:T(8,128)(2,1)S(1)}, bf16[2,1024,128]{2,1,0:T(8,128)(2,1)S(1)}, u32[]{:S(2)}, u32[]{:S(2)}) collective-permute-start(bf16[2,1024,128]{2,1,0:T(8,128)(2,1)S(1)} %pad_maximum_fusion.c_ref), channel_id=1, source_target_pairs={{0,96},{32,0},{64,32},{96,64},{1,97},{33,1},{65,33},{97,65},{2,98}... | collective-permute-start | bytes 1572872 | tf_op jit(solution)/shard_map/ppermute | solution.py:219
  32.2 22.8 %collective-permute-start.1 = (bf16[2,1024,128]{2,1,0:T(8,128)(2,1)S(1)}, bf16[2,1024,128]{2,1,0:T(8,128)(2,1)S(1)}, u32[]{:S(2)}, u32[]{:S(2)}) collective-permute-start(bf16[2,1024,128]{2,1,0:T(8,128)(2,1)S(1)} %pad_maximum_fusion.c_ref), channel_id=1, source_target_pairs={{0,32},{32,64},{64,96},{96,0},{1,33},{33,65},{65,97},{97,1},{2,34}... | collective-permute-start | bytes 1572872 | tf_op jit(solution)/shard_map/ppermute | solution.py:218
  49.1 11.2 %copy-start.1 = (bf16[128,32,128]{2,1,0:T(8,128)(2,1)}, bf16[128,32,128]{2,1,0:T(8,128)(2,1)S(1)}, u32[]{:S(2)}) copy-start(bf16[128,32,128]{2,1,0:T(8,128)(2,1)S(1)} %all-to-all-done.2.q_ref) | copy-start | bytes 3145732
  49.1 48.7 %all-to-all-start = ((bf16[128,32,128]{2,1,0:T(8,128)(2,1)}), bf16[128,32,128]{2,1,0:T(8,128)(2,1)}, u32[]{:S(2)}, u32[]{:S(2)}) async-start(bf16[128,32,128]{2,1,0:T(8,128)(2,1)} %bitcast.18), calls=%async_computation | async-start | bytes 2097152 | tf_op jit(solution)/shard_map/all_to_all | solution.py:232
  53.8 24.6 %copy-start.2 = (bf16[2,1024,128]{2,1,0:T(8,128)(2,1)}, bf16[2,1024,128]{2,1,0:T(8,128)(2,1)S(1)}, u32[]{:S(2)}) copy-start(bf16[2,1024,128]{2,1,0:T(8,128)(2,1)S(1)} %collective-permute-done.3.v_ref) | copy-start | bytes 1572868
  53.8 3.7 %collective-permute-start.4 = (bf16[2,1024,128]{2,1,0:T(8,128)(2,1)S(1)}, bf16[2,1024,128]{2,1,0:T(8,128)(2,1)S(1)}, u32[]{:S(2)}, u32[]{:S(2)}) collective-permute-start(bf16[2,1024,128]{2,1,0:T(8,128)(2,1)S(1)} %collective-permute-done.3.v_ref), channel_id=1, source_target_pairs={{0,8},{8,0},{1,9},{9,1},{2,10},{10,2},{3,11},{11,3},{4,12},{12,4},... | collective-permute-start | bytes 1572872 | tf_op jit(solution)/shard_map/ppermute | solution.py:222
  55.1 22.0 %copy-start.3 = (bf16[2,1024,128]{2,1,0:T(8,128)(2,1)}, bf16[2,1024,128]{2,1,0:T(8,128)(2,1)S(1)}, u32[]{:S(2)}) copy-start(bf16[2,1024,128]{2,1,0:T(8,128)(2,1)S(1)} %collective-permute-done.1.u_ref) | copy-start | bytes 1572868
  55.1 5.2 %collective-permute-start.2 = (bf16[2,1024,128]{2,1,0:T(8,128)(2,1)S(1)}, bf16[2,1024,128]{2,1,0:T(8,128)(2,1)S(1)}, u32[]{:S(2)}, u32[]{:S(2)}) collective-permute-start(bf16[2,1024,128]{2,1,0:T(8,128)(2,1)S(1)} %collective-permute-done.1.u_ref), channel_id=1, source_target_pairs={{0,8},{8,0},{1,9},{9,1},{2,10},{10,2},{3,11},{11,3},{4,12},{12,4},... | collective-permute-start | bytes 1572872 | tf_op jit(solution)/shard_map/ppermute | solution.py:222
  55.3 5.3 %collective-permute-start = (bf16[2,1024,128]{2,1,0:T(8,128)(2,1)S(1)}, bf16[2,1024,128]{2,1,0:T(8,128)(2,1)S(1)}, u32[]{:S(2)}, u32[]{:S(2)}) collective-permute-start(bf16[2,1024,128]{2,1,0:T(8,128)(2,1)S(1)} %pad_maximum_fusion.c_ref), channel_id=1, source_target_pairs={{0,8},{8,0},{1,9},{9,1},{2,10},{10,2},{3,11},{11,3},{4,12},{12,4},... | collective-permute-start | bytes 1572872 | tf_op jit(solution)/shard_map/ppermute | solution.py:222
  55.6 16.0 %collective-permute-start.7 = (bf16[1,1024,128]{2,1,0:T(8,128)(2,1)S(1)}, bf16[1,1024,128]{2,1,0:T(8,128)(2,1)S(1)}, u32[]{:S(2)}, u32[]{:S(2)}) collective-permute-start(bf16[1,1024,128]{2,1,0:T(8,128)(2,1)S(1)} %slice.30), channel_id=1, source_target_pairs={{0,96},{32,0},{64,32},{96,64},{1,97},{33,1},{65,33},{97,65},{2,98}... | collective-permute-start | bytes 786440 | tf_op jit(solution)/shard_map/ppermute | solution.py:225
  57.4 15.5 %collective-permute-start.5 = (bf16[1,1024,128]{2,1,0:T(8,128)(2,1)S(1)}, bf16[1,1024,128]{2,1,0:T(8,128)(2,1)S(1)}, u32[]{:S(2)}, u32[]{:S(2)}) collective-permute-start(bf16[1,1024,128]{2,1,0:T(8,128)(2,1)S(1)} %slice.28), channel_id=1, source_target_pairs={{0,32},{32,64},{64,96},{96,0},{1,33},{33,65},{65,97},{97,1},{2,34}... | collective-permute-start | bytes 786440 | tf_op jit(solution)/shard_map/ppermute | solution.py:225
  57.5 20.9 %copy-start.4 = (bf16[2,1024,128]{2,1,0:T(8,128)(2,1)}, bf16[2,1024,128]{2,1,0:T(8,128)(2,1)S(1)}, u32[]{:S(2)}) copy-start(bf16[2,1024,128]{2,1,0:T(8,128)(2,1)S(1)} %collective-permute-done.4.cv_ref) | copy-start | bytes 1572868
  57.5 19.5 %collective-permute-start.8 = (bf16[1,1024,128]{2,1,0:T(8,128)(2,1)S(1)}, bf16[1,1024,128]{2,1,0:T(8,128)(2,1)S(1)}, u32[]{:S(2)}, u32[]{:S(2)}) collective-permute-start(bf16[1,1024,128]{2,1,0:T(8,128)(2,1)S(1)} %slice.31), channel_id=1, source_target_pairs={{0,96},{32,0},{64,32},{96,64},{1,97},{33,1},{65,33},{97,65},{2,98}... | collective-permute-start | bytes 786440 | tf_op jit(solution)/shard_map/ppermute | solution.py:225
  60.3 18.2 %copy-start.5 = (bf16[2,1024,128]{2,1,0:T(8,128)(2,1)}, bf16[2,1024,128]{2,1,0:T(8,128)(2,1)S(1)}, u32[]{:S(2)}) copy-start(bf16[2,1024,128]{2,1,0:T(8,128)(2,1)S(1)} %collective-permute-done.2.cu_ref) | copy-start | bytes 1572868
  60.3 18.1 %collective-permute-start.6 = (bf16[1,1024,128]{2,1,0:T(8,128)(2,1)S(1)}, bf16[1,1024,128]{2,1,0:T(8,128)(2,1)S(1)}, u32[]{:S(2)}, u32[]{:S(2)}) collective-permute-start(bf16[1,1024,128]{2,1,0:T(8,128)(2,1)S(1)} %slice.29), channel_id=1, source_target_pairs={{0,32},{32,64},{64,96},{96,0},{1,33},{33,65},{65,97},{97,1},{2,34}... | collective-permute-start | bytes 786440 | tf_op jit(solution)/shard_map/ppermute | solution.py:225
  60.6 17.8 %copy-start.6 = (bf16[2,1024,128]{2,1,0:T(8,128)(2,1)}, bf16[2,1024,128]{2,1,0:T(8,128)(2,1)S(1)}, u32[]{:S(2)}) copy-start(bf16[2,1024,128]{2,1,0:T(8,128)(2,1)S(1)} %collective-permute-done.cc_ref) | copy-start | bytes 1572868
  71.6 6.9 %copy-start.7 = (bf16[1,1024,128]{2,1,0:T(8,128)(2,1)}, bf16[1,1024,128]{2,1,0:T(8,128)(2,1)S(1)}, u32[]{:S(2)}) copy-start(bf16[1,1024,128]{2,1,0:T(8,128)(2,1)S(1)} %collective-permute-done.7.g_ref) | copy-start | bytes 786436
  72.9 5.5 %copy-start.8 = (bf16[1,1024,128]{2,1,0:T(8,128)(2,1)}, bf16[1,1024,128]{2,1,0:T(8,128)(2,1)S(1)}, u32[]{:S(2)}) copy-start(bf16[1,1024,128]{2,1,0:T(8,128)(2,1)S(1)} %collective-permute-done.5.h_ref) | copy-start | bytes 786436
  77.1 1.4 copy-start.9
  78.5 0.7 copy-start.10

commit v4 on v3

--- a/solution.py
+++ b/solution.py
@@ -74,7 +74,7 @@
     return [part.reshape(heads, strip, width) for part in parts]
 
 
-def attn(q, pieces, where, out, *, bq, period, which, sub=512, unroll=4):
+def attn(q, pieces, where, *, bq, period, which, sub=512, unroll=4):
     G, strip, D = q.shape
     BK = pieces[0].shape[1] // 2
     blocks = G * period // BK
@@ -176,22 +176,20 @@
             l, _ = lax.fori_loop(0, first + nd, slow, start)
             o_ref[...] = (acc_ref[...] / l).T.astype(jnp.bfloat16).reshape(o_ref.shape)
 
-    extra = () if out is None else (out,)
     anywhere = pl.BlockSpec(memory_space=pl.ANY)
     return pl.pallas_call(
         kernel, grid=(G // devs,),
         in_specs=[pl.BlockSpec(memory_space=pltpu.SMEM),
-                  anywhere] + [anywhere] * (len(pieces) + len(extra)),
-        out_specs=pl.BlockSpec((devs, strip, D), lambda i: (i, which, 0)),
-        out_shape=jax.ShapeDtypeStruct((G, period, D), jnp.bfloat16),
-        input_output_aliases={2 + len(pieces): 0} if extra else {},
+                  anywhere] + [anywhere] * len(pieces),
+        out_specs=pl.BlockSpec((devs, strip, D), lambda i: (i, 0, 0)),
+        out_shape=jax.ShapeDtypeStruct((G, strip, D), jnp.bfloat16),
         scratch_shapes=[pltpu.VMEM((D, bq), jnp.bfloat16), pltpu.VMEM((D, bq), jnp.float32),
                         pltpu.VMEM((8, bq), jnp.float32), pltpu.VMEM((blocks, 2 * BK, D), jnp.bfloat16),
                         pltpu.VMEM((G, strip, D), jnp.bfloat16),
                         pltpu.SemaphoreType.DMA((blocks + 1,))],
         compiler_params=pltpu.CompilerParams(vmem_limit_bytes=24 * 2**20),
         name="attn",
-    )(where, *(pltpu.with_memory_space_constraint(piece, pltpu.HBM) for piece in (q, *pieces)), *extra)
+    )(where, *(pltpu.with_memory_space_constraint(piece, pltpu.HBM) for piece in (q, *pieces)))
 
 
 def shards(queries, keys, values):
@@ -230,15 +228,13 @@
     arrived = []
     for n in range(CHUNKS):
         arrived.append(lax.all_to_all(ordered[n], AXES, split_axis=0, concat_axis=0, tiled=True))
-    out = None
+    halves = []
     for n in range(CHUNKS):
-        out = attn(arrived[n], pieces, where, out, bq=TILE, period=rows, which=n)
-    merged = lax.all_to_all(out.swapaxes(0, 1), AXES, split_axis=1, concat_axis=1, tiled=True)
-    return (
-        merged.reshape(rows, group, key_heads, width)
-        .transpose(0, 2, 1, 3)
-        .reshape(rows, heads_all, width)
-    )
+        done = attn(arrived[n], pieces, where, bq=TILE, period=rows, which=n)
+        back = lax.all_to_all(done, AXES, split_axis=0, concat_axis=0, tiled=True)
+        back = back.reshape(group, key_heads, -1, width).transpose(2, 1, 0, 3)
+        halves.append(back.reshape(-1, heads_all, width))
+    return jnp.concatenate(halves, axis=0)
 
 
 def solution(mesh):

time: 182 us -> 182 us (level)
  blocking collectives: 62 us -> 0 us
  starting transfers between devices: 30.7 us -> 70.9 us
  waiting for transfers between devices: 36.7 us -> 55.6 us
    all_to_all x1 -> x0, blocking collectives: 62 us -> none  [shards(): lax.all_to_all(out.swapaxes(0, 1), AXES, split_axis=1, concat_axis=1, til...]
    all_to_all x0 -> x2, starting transfers between devices: none -> 41.3 us  [shards(): back = lax.all_to_all(done, AXES, split_axis=0, concat_axis=0, tiled=True)]
    all_to_all x0 -> x2, waiting for transfers between devices: none -> 18.9 us  [shards(): back = lax.all_to_all(done, AXES, split_axis=0, concat_axis=0, tiled=True)]
  transfers between devices with their start and end apart: 12 -> 14, of which waited for: 6 -> 10; matrix products, arithmetic and copies ran while one was open for 0% -> 1% of each run, Pallas kernels for 14% -> 25%
where the time goes in v4:
time: 182 us; the launch traced here: 181 us
  starting transfers between devices  70.9 us (39%)
  waiting for transfers between devices  55.6 us (31%)
  Pallas kernels  48.2 us (26%)
  local copies, waits for them, and re-layouts  3.44 us (2%)
  other arithmetic  2.47 us (1%)
    all_to_all x2, starting transfers between devices, shards(): back = lax.all_to_all(done, AXES, split_axis=0, concat_axis=0, tiled=True)  41.3 us
    pallas_call x2, Pallas kernels, attn(): pl.pallas_call(kernel, grid=(G // devs,), in_specs=[pl.BlockSpec(memory_s...  38.8 us
    all_to_all x2, waiting for transfers between devices, shards(): back = lax.all_to_all(done, AXES, split_axis=0, concat_axis=0, tiled=True)  18.9 us
    ppermute x4, waiting for transfers between devices, shards(): far.append(lax.ppermute(source[half:half + 1], 'x', way))  17.3 us
    all_to_all x2, waiting for transfers between devices, shards(): lax.all_to_all(ordered[n], AXES, split_axis=0, concat_axis=0, tiled=True)  16.9 us
    all_to_all x2, starting transfers between devices, shards(): lax.all_to_all(ordered[n], AXES, split_axis=0, concat_axis=0, tiled=True)  12.2 us
    all_to_all x1, starting transfers between devices, shards(): lax.all_to_all(pair, ('yl', 'sy'), split_axis=0, concat_axis=0, tiled=True)  8.59 us
    pallas_call x1, Pallas kernels, prepare_queries(): pl.pallas_call(kernel, grid=(heads // group,), in_specs=[pl.BlockSpec((ro...  7.2 us
  transfers between devices with their start and end apart: 14, of which 10 were waited for; matrix products, arithmetic and copies ran while one was open for 1% of the time, Pallas kernels for 25%

profile of v4, /device:TPU:1, one launch (start us, length us, event | category | flops | bytes accessed | tf_op | source)
XLA Modules:
  0.0 180.8 jit_solution(309917704329341416)
XLA Ops:
  0.1 0.1 mul.58
  0.1 0.8 fusion
  1.0 2.3 %pair.1 = bf16[16,2,64,128]{3,2,1,0:T(8,128)(2,1)} custom-call(bf16[64,8,128]{2,1,0:T(8,128)(2,1)} %k_ref.1, bf16[64,8,128]{2,1,0:T(8,128)(2,1)} %v_ref.1, f32[64,128]{1,0:T(8,128)} %get-tuple-element.12.cos_ref, f32[64,128]{1,0:T(8,128)} %get-tuple-element.11.sin_ref), custom_call_target="tpu_custom_call" | custom-call | tf_op jit(solution)/shard_map/pair/pallas_call | solution.py:48
  3.3 8.6 %all-to-all-start.1 = ((bf16[16,2,64,128]{3,2,1,0:T(8,128)(2,1)}), bf16[16,2,64,128]{3,2,1,0:T(8,128)(2,1)S(1)}, u32[]{:S(2)}, u32[]{:S(2)}) async-start(bf16[16,2,64,128]{3,2,1,0:T(8,128)(2,1)} %pair.1), calls=%async_computation.1 | async-start | bytes 1048576 | tf_op jit(solution)/shard_map/all_to_all | solution.py:208
  11.8 7.2 %queries.1 = (bf16[16,8,32,128]{3,2,1,0:T(8,128)(2,1)}, bf16[16,8,32,128]{3,2,1,0:T(8,128)(2,1)}) custom-call(bf16[64,128,128]{2,1,0:T(8,128)(2,1)} %q_ref.1, f32[64,128]{1,0:T(8,128)} %get-tuple-element.12.cos_ref, f32[64,128]{1,0:T(8,128)} %get-tuple-element.11.sin_ref), custom_call_target="tpu_custom_call" | custom-call | tf_op jit(solution)/shard_map/queries/pallas_call | solution.py:67
  19.0 2.0 %all-to-all-done.1 = bf16[16,2,64,128]{3,2,1,0:T(8,128)(2,1)S(1)} async-done(((bf16[16,2,64,128]{3,2,1,0:T(8,128)(2,1)}), bf16[16,2,64,128]{3,2,1,0:T(8,128)(2,1)S(1)}, u32[]{:S(2)}, u32[]{:S(2)}) %all-to-all-start.1) | async-done | bytes 524320 | tf_op jit(solution)/shard_map/all_to_all | solution.py:208
  21.1 8.3 %all-to-all-start.3 = ((bf16[128,32,128]{2,1,0:T(8,128)(2,1)}), bf16[128,32,128]{2,1,0:T(8,128)(2,1)S(1)}, u32[]{:S(2)}, u32[]{:S(2)}) async-start(bf16[128,32,128]{2,1,0:T(8,128)(2,1)} %bitcast.24), calls=%async_computation.3 | async-start | bytes 2097152 | tf_op jit(solution)/shard_map/all_to_all | solution.py:230
  29.4 0.2 copy.4
  29.6 0.0 copy-start
  29.6 2.6 %collective-permute-start.3 = (bf16[2,1024,128]{2,1,0:T(8,128)(2,1)S(1)}, bf16[2,1024,128]{2,1,0:T(8,128)(2,1)S(1)}, u32[]{:S(2)}, u32[]{:S(2)}) collective-permute-start(bf16[2,1024,128]{2,1,0:T(8,128)(2,1)S(1)} %pad_maximum_fusion.1.c_ref), channel_id=1, source_target_pairs={{0,96},{32,0},{64,32},{96,64},{1,97},{33,1},{65,33},{97,65},{2,98}... | collective-permute-start | bytes 1572872 | tf_op jit(solution)/shard_map/ppermute | solution.py:217
  32.3 0.0 collective-permute-start.1
  32.3 16.9 %all-to-all-done.3.q_ref = bf16[128,32,128]{2,1,0:T(8,128)(2,1)S(1)} async-done(((bf16[128,32,128]{2,1,0:T(8,128)(2,1)}), bf16[128,32,128]{2,1,0:T(8,128)(2,1)S(1)}, u32[]{:S(2)}, u32[]{:S(2)}) %all-to-all-start.3) | async-done | bytes 1048608 | tf_op jit(solution)/shard_map/all_to_all | solution.py:230
  49.1 3.9 %all-to-all-start = ((bf16[128,32,128]{2,1,0:T(8,128)(2,1)}), bf16[128,32,128]{2,1,0:T(8,128)(2,1)S(1)}, u32[]{:S(2)}, u32[]{:S(2)}) async-start(bf16[128,32,128]{2,1,0:T(8,128)(2,1)} %bitcast.23), calls=%async_computation | async-start | bytes 2097152 | tf_op jit(solution)/shard_map/all_to_all | solution.py:230
  53.1 0.2 collective-permute-done.3.v_ref
  53.3 1.0 collective-permute-start.4
  54.2 0.3 collective-permute-done.1.u_ref
  54.6 0.9 collective-permute-start.2
  55.5 0.0 collective-permute-start
  55.5 1.3 collective-permute-start.7
  56.7 1.0 slice.28
  57.7 0.3 collective-permute-start.5
  58.1 0.0 collective-permute-done.4.cv_ref
  58.1 2.5 %collective-permute-start.8 = (bf16[1,1024,128]{2,1,0:T(8,128)(2,1)S(1)}, bf16[1,1024,128]{2,1,0:T(8,128)(2,1)S(1)}, u32[]{:S(2)}, u32[]{:S(2)}) collective-permute-start(bf16[1,1024,128]{2,1,0:T(8,128)(2,1)S(1)} %slice.31), channel_id=1, source_target_pairs={{0,96},{32,0},{64,32},{96,64},{1,97},{33,1},{65,33},{97,65},{2,98}... | collective-permute-start | bytes 786440 | tf_op jit(solution)/shard_map/ppermute | solution.py:223
  60.6 0.0 collective-permute-done.2.cu_ref
  60.6 0.0 copy-done
  60.6 0.0 copy-done.1
  60.6 0.3 collective-permute-start.6
  60.9 0.1 pad_add_fusion.where_ref
  60.9 0.0 collective-permute-done.cc_ref
  60.9 10.3 %collective-permute-done.7.g_ref = bf16[1,1024,128]{2,1,0:T(8,128)(2,1)S(1)} collective-permute-done((bf16[1,1024,128]{2,1,0:T(8,128)(2,1)S(1)}, bf16[1,1024,128]{2,1,0:T(8,128)(2,1)S(1)}, u32[]{:S(2)}, u32[]{:S(2)}) %collective-permute-start.7) | collective-permute-done | bytes 262176 | tf_op jit(solution)/shard_map/ppermute | solution.py:223
  71.3 1.3 collective-permute-done.5.h_ref
  72.6 4.3 %collective-permute-done.8.cg_ref = bf16[1,1024,128]{2,1,0:T(8,128)(2,1)S(1)} collective-permute-done((bf16[1,1024,128]{2,1,0:T(8,128)(2,1)S(1)}, bf16[1,1024,128]{2,1,0:T(8,128)(2,1)S(1)}, u32[]{:S(2)}, u32[]{:S(2)}) %collective-permute-start.8) | collective-permute-done | bytes 262176 | tf_op jit(solution)/shard_map/ppermute | solution.py:223
  76.9 1.3 collective-permute-done.6.ch_ref
  78.2 0.0 copy-done.3
  78.2 0.0 copy-done.5
  78.3 0.7 copy-done.10
  79.0 19.4 %attn.3 = bf16[128,32,128]{2,1,0:T(8,128)(2,1)} custom-call(s32[2]{0:T(128)S(1)} %pad_add_fusion.where_ref, bf16[128,32,128]{2,1,0:T(8,128)(2,1)} %copy-done.1, bf16[2,1024,128]{2,1,0:T(8,128)(2,1)} %copy-done, bf16[2,1024,128]{2,1,0:T(8,128)(2,1)} %copy-done.6, bf16[2,1024,128]{2,1,0:T(8,128)(2,1)} %collective-permute-done.1.u_ref, ...), custom_call_target="tpu_custom_call" | custom-call | tf_op jit(solution)/shard_map/attn/pallas_call | solution.py:180
  98.4 0.0 all-to-all-done.q_ref
  98.4 0.0 copy-start.2
  98.4 31.7 %all-to-all-start.4 = ((bf16[128,32,128]{2,1,0:T(8,128)(2,1)}), bf16[128,32,128]{2,1,0:T(8,128)(2,1)S(1)}, u32[]{:S(2)}, u32[]{:S(2)}) async-start(bf16[128,32,128]{2,1,0:T(8,128)(2,1)} %attn.3), calls=%async_computation.4 | async-start | bytes 2097152 | tf_op jit(solution)/shard_map/all_to_all | solution.py:234
  130.0 0.0 copy-done.2
  130.1 19.4 %attn.2 = bf16[128,32,128]{2,1,0:T(8,128)(2,1)} custom-call(s32[2]{0:T(128)S(1)} %pad_add_fusion.where_ref, bf16[128,32,128]{2,1,0:T(8,128)(2,1)} %copy-done.2, bf16[2,1024,128]{2,1,0:T(8,128)(2,1)} %copy-done, bf16[2,1024,128]{2,1,0:T(8,128)(2,1)} %copy-done.6, bf16[2,1024,128]{2,1,0:T(8,128)(2,1)} %collective-permute-done.1.u_ref, ...), custom_call_target="tpu_custom_call" | custom-call | tf_op jit(solution)/shard_map/attn/pallas_call | solution.py:180
  149.5 0.1 all-to-all-done.4
  149.5 9.6 %all-to-all-start.2 = ((bf16[128,32,128]{2,1,0:T(8,128)(2,1)}), bf16[128,32,128]{2,1,0:T(8,128)(2,1)S(1)}, u32[]{:S(2)}, u32[]{:S(2)}) async-start(bf16[128,32,128]{2,1,0:T(8,128)(2,1)} %attn.2), calls=%async_computation.2 | async-start | bytes 2097152 | tf_op jit(solution)/shard_map/all_to_all | solution.py:234
  159.2 0.7 copy.6
  159.9 18.8 %all-to-all-done.2 = bf16[128,32,128]{2,1,0:T(8,128)(2,1)S(1)} async-done(((bf16[128,32,128]{2,1,0:T(8,128)(2,1)}), bf16[128,32,128]{2,1,0:T(8,128)(2,1)S(1)}, u32[]{:S(2)}, u32[]{:S(2)}) %all-to-all-start.2) | async-done | bytes 1048608 | tf_op jit(solution)/shard_map/all_to_all | solution.py:234
  178.7 0.7 copy.5
  179.3 1.5 pad_maximum_fusion
  (23 shorter events, 0.2 us)
Async XLA Ops:
  3.3 17.8 %all-to-all-start.1 = ((bf16[16,2,64,128]{3,2,1,0:T(8,128)(2,1)}), bf16[16,2,64,128]{3,2,1,0:T(8,128)(2,1)S(1)}, u32[]{:S(2)}, u32[]{:S(2)}) async-start(bf16[16,2,64,128]{3,2,1,0:T(8,128)(2,1)} %pair.1), calls=%async_computation.1 | async-start | bytes 1048576 | tf_op jit(solution)/shard_map/all_to_all | solution.py:208
  21.1 28.1 %all-to-all-start.3 = ((bf16[128,32,128]{2,1,0:T(8,128)(2,1)}), bf16[128,32,128]{2,1,0:T(8,128)(2,1)S(1)}, u32[]{:S(2)}, u32[]{:S(2)}) async-start(bf16[128,32,128]{2,1,0:T(8,128)(2,1)} %bitcast.24), calls=%async_computation.3 | async-start | bytes 2097152 | tf_op jit(solution)/shard_map/all_to_all | solution.py:230
  29.6 31.0 %copy-start = (bf16[2,1024,128]{2,1,0:T(8,128)(2,1)}, bf16[2,1024,128]{2,1,0:T(8,128)(2,1)S(1)}, u32[]{:S(2)}) copy-start(bf16[2,1024,128]{2,1,0:T(8,128)(2,1)S(1)} %pad_maximum_fusion.1.c_ref) | copy-start | bytes 1572868
  29.6 23.7 %collective-permute-start.3 = (bf16[2,1024,128]{2,1,0:T(8,128)(2,1)S(1)}, bf16[2,1024,128]{2,1,0:T(8,128)(2,1)S(1)}, u32[]{:S(2)}, u32[]{:S(2)}) collective-permute-start(bf16[2,1024,128]{2,1,0:T(8,128)(2,1)S(1)} %pad_maximum_fusion.1.c_ref), channel_id=1, source_target_pairs={{0,96},{32,0},{64,32},{96,64},{1,97},{33,1},{65,33},{97,65},{2,98}... | collective-permute-start | bytes 1572872 | tf_op jit(solution)/shard_map/ppermute | solution.py:217
  32.3 22.3 %collective-permute-start.1 = (bf16[2,1024,128]{2,1,0:T(8,128)(2,1)S(1)}, bf16[2,1024,128]{2,1,0:T(8,128)(2,1)}, u32[]{:S(2)}, u32[]{:S(2)}) collective-permute-start(bf16[2,1024,128]{2,1,0:T(8,128)(2,1)S(1)} %pad_maximum_fusion.1.c_ref), channel_id=1, source_target_pairs={{0,32},{32,64},{64,96},{96,0},{1,33},{33,65},{65,97},{97,1},{2,34}... | collective-permute-start | bytes 1572872 | tf_op jit(solution)/shard_map/ppermute | solution.py:216
  49.1 11.5 %copy-start.1 = (bf16[128,32,128]{2,1,0:T(8,128)(2,1)}, bf16[128,32,128]{2,1,0:T(8,128)(2,1)S(1)}, u32[]{:S(2)}) copy-start(bf16[128,32,128]{2,1,0:T(8,128)(2,1)S(1)} %all-to-all-done.3.q_ref) | copy-start | bytes 3145732
  49.1 49.2 %all-to-all-start = ((bf16[128,32,128]{2,1,0:T(8,128)(2,1)}), bf16[128,32,128]{2,1,0:T(8,128)(2,1)S(1)}, u32[]{:S(2)}, u32[]{:S(2)}) async-start(bf16[128,32,128]{2,1,0:T(8,128)(2,1)} %bitcast.23), calls=%async_computation | async-start | bytes 2097152 | tf_op jit(solution)/shard_map/all_to_all | solution.py:230
  53.3 24.9 %copy-start.3 = (bf16[2,1024,128]{2,1,0:T(8,128)(2,1)}, bf16[2,1024,128]{2,1,0:T(8,128)(2,1)S(1)}, u32[]{:S(2)}) copy-start(bf16[2,1024,128]{2,1,0:T(8,128)(2,1)S(1)} %collective-permute-done.3.v_ref) | copy-start | bytes 1572868
  53.3 4.8 %collective-permute-start.4 = (bf16[2,1024,128]{2,1,0:T(8,128)(2,1)S(1)}, bf16[2,1024,128]{2,1,0:T(8,128)(2,1)S(1)}, u32[]{:S(2)}, u32[]{:S(2)}) collective-permute-start(bf16[2,1024,128]{2,1,0:T(8,128)(2,1)S(1)} %collective-permute-done.3.v_ref), channel_id=1, source_target_pairs={{0,8},{8,0},{1,9},{9,1},{2,10},{10,2},{3,11},{11,3},{4,12},{12,4},... | collective-permute-start | bytes 1572872 | tf_op jit(solution)/shard_map/ppermute | solution.py:220
  54.6 6.0 %collective-permute-start.2 = (bf16[2,1024,128]{2,1,0:T(8,128)(2,1)}, bf16[2,1024,128]{2,1,0:T(8,128)(2,1)S(1)}, u32[]{:S(2)}, u32[]{:S(2)}) collective-permute-start(bf16[2,1024,128]{2,1,0:T(8,128)(2,1)} %collective-permute-done.1.u_ref), channel_id=1, source_target_pairs={{0,8},{8,0},{1,9},{9,1},{2,10},{10,2},{3,11},{11,3},{4,12},{12,4},... | collective-permute-start | bytes 1572872 | tf_op jit(solution)/shard_map/ppermute | solution.py:220
  55.5 5.5 %collective-permute-start = (bf16[2,1024,128]{2,1,0:T(8,128)(2,1)S(1)}, bf16[2,1024,128]{2,1,0:T(8,128)(2,1)S(1)}, u32[]{:S(2)}, u32[]{:S(2)}) collective-permute-start(bf16[2,1024,128]{2,1,0:T(8,128)(2,1)S(1)} %pad_maximum_fusion.1.c_ref), channel_id=1, source_target_pairs={{0,8},{8,0},{1,9},{9,1},{2,10},{10,2},{3,11},{11,3},{4,12},{12,4},... | collective-permute-start | bytes 1572872 | tf_op jit(solution)/shard_map/ppermute | solution.py:220
  55.5 15.8 %collective-permute-start.7 = (bf16[1,1024,128]{2,1,0:T(8,128)(2,1)S(1)}, bf16[1,1024,128]{2,1,0:T(8,128)(2,1)S(1)}, u32[]{:S(2)}, u32[]{:S(2)}) collective-permute-start(bf16[1,1024,128]{2,1,0:T(8,128)(2,1)S(1)} %slice.30), channel_id=1, source_target_pairs={{0,96},{32,0},{64,32},{96,64},{1,97},{33,1},{65,33},{97,65},{2,98}... | collective-permute-start | bytes 786440 | tf_op jit(solution)/shard_map/ppermute | solution.py:223
  57.7 14.9 %collective-permute-start.5 = (bf16[1,1024,128]{2,1,0:T(8,128)(2,1)S(1)}, bf16[1,1024,128]{2,1,0:T(8,128)(2,1)S(1)}, u32[]{:S(2)}, u32[]{:S(2)}) collective-permute-start(bf16[1,1024,128]{2,1,0:T(8,128)(2,1)S(1)} %slice.28), channel_id=1, source_target_pairs={{0,32},{32,64},{64,96},{96,0},{1,33},{33,65},{65,97},{97,1},{2,34}... | collective-permute-start | bytes 786440 | tf_op jit(solution)/shard_map/ppermute | solution.py:223
  58.1 20.2 %copy-start.4 = (bf16[2,1024,128]{2,1,0:T(8,128)(2,1)}, bf16[2,1024,128]{2,1,0:T(8,128)(2,1)S(1)}, u32[]{:S(2)}) copy-start(bf16[2,1024,128]{2,1,0:T(8,128)(2,1)S(1)} %collective-permute-done.4.cv_ref) | copy-start | bytes 1572868
  58.1 18.8 %collective-permute-start.8 = (bf16[1,1024,128]{2,1,0:T(8,128)(2,1)S(1)}, bf16[1,1024,128]{2,1,0:T(8,128)(2,1)S(1)}, u32[]{:S(2)}, u32[]{:S(2)}) collective-permute-start(bf16[1,1024,128]{2,1,0:T(8,128)(2,1)S(1)} %slice.31), channel_id=1, source_target_pairs={{0,96},{32,0},{64,32},{96,64},{1,97},{33,1},{65,33},{97,65},{2,98}... | collective-permute-start | bytes 786440 | tf_op jit(solution)/shard_map/ppermute | solution.py:223
  60.6 17.7 %copy-start.5 = (bf16[2,1024,128]{2,1,0:T(8,128)(2,1)}, bf16[2,1024,128]{2,1,0:T(8,128)(2,1)S(1)}, u32[]{:S(2)}) copy-start(bf16[2,1024,128]{2,1,0:T(8,128)(2,1)S(1)} %collective-permute-done.2.cu_ref) | copy-start | bytes 1572868
  60.6 17.6 %collective-permute-start.6 = (bf16[1,1024,128]{2,1,0:T(8,128)(2,1)S(1)}, bf16[1,1024,128]{2,1,0:T(8,128)(2,1)S(1)}, u32[]{:S(2)}, u32[]{:S(2)}) collective-permute-start(bf16[1,1024,128]{2,1,0:T(8,128)(2,1)S(1)} %slice.29), channel_id=1, source_target_pairs={{0,32},{32,64},{64,96},{96,0},{1,33},{33,65},{65,97},{97,1},{2,34}... | collective-permute-start | bytes 786440 | tf_op jit(solution)/shard_map/ppermute | solution.py:223
  60.9 17.3 %copy-start.6 = (bf16[2,1024,128]{2,1,0:T(8,128)(2,1)}, bf16[2,1024,128]{2,1,0:T(8,128)(2,1)S(1)}, u32[]{:S(2)}) copy-start(bf16[2,1024,128]{2,1,0:T(8,128)(2,1)S(1)} %collective-permute-done.cc_ref) | copy-start | bytes 1572868
  71.3 6.9 %copy-start.7 = (bf16[1,1024,128]{2,1,0:T(8,128)(2,1)}, bf16[1,1024,128]{2,1,0:T(8,128)(2,1)S(1)}, u32[]{:S(2)}) copy-start(bf16[1,1024,128]{2,1,0:T(8,128)(2,1)S(1)} %collective-permute-done.7.g_ref) | copy-start | bytes 786436
  72.6 5.7 %copy-start.8 = (bf16[1,1024,128]{2,1,0:T(8,128)(2,1)}, bf16[1,1024,128]{2,1,0:T(8,128)(2,1)S(1)}, u32[]{:S(2)}) copy-start(bf16[1,1024,128]{2,1,0:T(8,128)(2,1)S(1)} %collective-permute-done.5.h_ref) | copy-start | bytes 786436
  76.9 1.3 copy-start.9
  78.3 0.7 copy-start.10
  98.4 31.7 %copy-start.2 = (bf16[128,32,128]{2,1,0:T(8,128)(2,1)}, bf16[128,32,128]{2,1,0:T(8,128)(2,1)S(1)}, u32[]{:S(2)}) copy-start(bf16[128,32,128]{2,1,0:T(8,128)(2,1)S(1)} %all-to-all-done.q_ref) | copy-start | bytes 3145732
  98.4 51.2 %all-to-all-start.4 = ((bf16[128,32,128]{2,1,0:T(8,128)(2,1)}), bf16[128,32,128]{2,1,0:T(8,128)(2,1)S(1)}, u32[]{:S(2)}, u32[]{:S(2)}) async-start(bf16[128,32,128]{2,1,0:T(8,128)(2,1)} %attn.3), calls=%async_computation.4 | async-start | bytes 2097152 | tf_op jit(solution)/shard_map/all_to_all | solution.py:234
  149.5 29.1 %all-to-all-start.2 = ((bf16[128,32,128]{2,1,0:T(8,128)(2,1)}), bf16[128,32,128]{2,1,0:T(8,128)(2,1)S(1)}, u32[]{:S(2)}, u32[]{:S(2)}) async-start(bf16[128,32,128]{2,1,0:T(8,128)(2,1)} %attn.2), calls=%async_computation.2 | async-start | bytes 2097152 | tf_op jit(solution)/shard_map/all_to_all | solution.py:234

commit v5 on v4

--- a/solution.py
+++ b/solution.py
@@ -234,7 +234,10 @@
         back = lax.all_to_all(done, AXES, split_axis=0, concat_axis=0, tiled=True)
         back = back.reshape(group, key_heads, -1, width).transpose(2, 1, 0, 3)
         halves.append(back.reshape(-1, heads_all, width))
-    return jnp.concatenate(halves, axis=0)
+    whole = lax.optimization_barrier(jnp.pad(halves[0], ((0, rows - rows // CHUNKS), (0, 0), (0, 0))))
+    for n in range(1, CHUNKS):
+        whole = lax.dynamic_update_slice(whole, halves[n], (n * (rows // CHUNKS), 0, 0))
+    return whole
 
 
 def solution(mesh):

time: 182 us -> 183 us (level)
  local copies, waits for them, and re-layouts: 3.44 us -> 6.2 us
where the time goes in v5:
time: 183 us; the launch traced here: 182 us
  starting transfers between devices  70.9 us (39%)
  waiting for transfers between devices  55.6 us (30%)
  Pallas kernels  48.2 us (26%)
  local copies, waits for them, and re-layouts  6.2 us (3%)
    all_to_all x2, starting transfers between devices, shards(): back = lax.all_to_all(done, AXES, split_axis=0, concat_axis=0, tiled=True)  41.3 us
    pallas_call x2, Pallas kernels, attn(): pl.pallas_call(kernel, grid=(G // devs,), in_specs=[pl.BlockSpec(memory_s...  38.8 us
    all_to_all x2, waiting for transfers between devices, shards(): back = lax.all_to_all(done, AXES, split_axis=0, concat_axis=0, tiled=True)  18.9 us
    ppermute x4, waiting for transfers between devices, shards(): far.append(lax.ppermute(source[half:half + 1], 'x', way))  17.3 us
    all_to_all x2, waiting for transfers between devices, shards(): lax.all_to_all(ordered[n], AXES, split_axis=0, concat_axis=0, tiled=True)  16.9 us
    all_to_all x2, starting transfers between devices, shards(): lax.all_to_all(ordered[n], AXES, split_axis=0, concat_axis=0, tiled=True)  12.2 us
    all_to_all x1, starting transfers between devices, shards(): lax.all_to_all(pair, ('yl', 'sy'), split_axis=0, concat_axis=0, tiled=True)  8.59 us
    pallas_call x1, Pallas kernels, prepare_queries(): pl.pallas_call(kernel, grid=(heads // group,), in_specs=[pl.BlockSpec((ro...  7.2 us
  transfers between devices with their start and end apart: 14, of which 10 were waited for; matrix products, arithmetic and copies ran while one was open for 1% of the time, Pallas kernels for 25%

profile of v5, /device:TPU:1, one launch (start us, length us, event | category | flops | bytes accessed | tf_op | source)
XLA Modules:
  0.0 182.1 jit_solution(17999754484890207001)
XLA Ops:
  0.1 0.1 mul.58
  0.1 0.8 fusion
  1.0 2.3 %pair.1 = bf16[16,2,64,128]{3,2,1,0:T(8,128)(2,1)} custom-call(bf16[64,8,128]{2,1,0:T(8,128)(2,1)} %k_ref.1, bf16[64,8,128]{2,1,0:T(8,128)(2,1)} %v_ref.1, f32[64,128]{1,0:T(8,128)} %get-tuple-element.12.cos_ref, f32[64,128]{1,0:T(8,128)} %get-tuple-element.11.sin_ref), custom_call_target="tpu_custom_call" | custom-call | tf_op jit(solution)/shard_map/pair/pallas_call | solution.py:48
  3.3 8.6 %all-to-all-start.1 = ((bf16[16,2,64,128]{3,2,1,0:T(8,128)(2,1)}), bf16[16,2,64,128]{3,2,1,0:T(8,128)(2,1)S(1)}, u32[]{:S(2)}, u32[]{:S(2)}) async-start(bf16[16,2,64,128]{3,2,1,0:T(8,128)(2,1)} %pair.1), calls=%async_computation.1 | async-start | bytes 1048576 | tf_op jit(solution)/shard_map/all_to_all | solution.py:208
  11.8 7.2 %queries.1 = (bf16[16,8,32,128]{3,2,1,0:T(8,128)(2,1)}, bf16[16,8,32,128]{3,2,1,0:T(8,128)(2,1)}) custom-call(bf16[64,128,128]{2,1,0:T(8,128)(2,1)} %q_ref.1, f32[64,128]{1,0:T(8,128)} %get-tuple-element.12.cos_ref, f32[64,128]{1,0:T(8,128)} %get-tuple-element.11.sin_ref), custom_call_target="tpu_custom_call" | custom-call | tf_op jit(solution)/shard_map/queries/pallas_call | solution.py:67
  19.0 2.0 %all-to-all-done.1 = bf16[16,2,64,128]{3,2,1,0:T(8,128)(2,1)S(1)} async-done(((bf16[16,2,64,128]{3,2,1,0:T(8,128)(2,1)}), bf16[16,2,64,128]{3,2,1,0:T(8,128)(2,1)S(1)}, u32[]{:S(2)}, u32[]{:S(2)}) %all-to-all-start.1) | async-done | bytes 524320 | tf_op jit(solution)/shard_map/all_to_all | solution.py:208
  21.1 8.3 %all-to-all-start.3 = ((bf16[128,32,128]{2,1,0:T(8,128)(2,1)}), bf16[128,32,128]{2,1,0:T(8,128)(2,1)S(1)}, u32[]{:S(2)}, u32[]{:S(2)}) async-start(bf16[128,32,128]{2,1,0:T(8,128)(2,1)} %bitcast.24), calls=%async_computation.3 | async-start | bytes 2097152 | tf_op jit(solution)/shard_map/all_to_all | solution.py:230
  29.4 0.2 copy.4
  29.6 2.6 %collective-permute-start.3 = (bf16[2,1024,128]{2,1,0:T(8,128)(2,1)S(1)}, bf16[2,1024,128]{2,1,0:T(8,128)(2,1)S(1)}, u32[]{:S(2)}, u32[]{:S(2)}) collective-permute-start(bf16[2,1024,128]{2,1,0:T(8,128)(2,1)S(1)} %pad_maximum_fusion.c_ref), channel_id=1, source_target_pairs={{0,96},{32,0},{64,32},{96,64},{1,97},{33,1},{65,33},{97,65},{2,98}... | collective-permute-start | bytes 1572872 | tf_op jit(solution)/shard_map/ppermute | solution.py:217
  32.3 0.0 collective-permute-start.1
  32.3 16.9 %all-to-all-done.3.q_ref = bf16[128,32,128]{2,1,0:T(8,128)(2,1)S(1)} async-done(((bf16[128,32,128]{2,1,0:T(8,128)(2,1)}), bf16[128,32,128]{2,1,0:T(8,128)(2,1)S(1)}, u32[]{:S(2)}, u32[]{:S(2)}) %all-to-all-start.3) | async-done | bytes 1048608 | tf_op jit(solution)/shard_map/all_to_all | solution.py:230
  49.1 3.9 %all-to-all-start = ((bf16[128,32,128]{2,1,0:T(8,128)(2,1)}), bf16[128,32,128]{2,1,0:T(8,128)(2,1)S(1)}, u32[]{:S(2)}, u32[]{:S(2)}) async-start(bf16[128,32,128]{2,1,0:T(8,128)(2,1)} %bitcast.23), calls=%async_computation | async-start | bytes 2097152 | tf_op jit(solution)/shard_map/all_to_all | solution.py:230
  53.1 0.2 collective-permute-done.3.v_ref
  53.3 1.0 collective-permute-start.4
  54.2 0.3 collective-permute-done.1.u_ref
  54.6 0.9 collective-permute-start.2
  55.5 0.0 collective-permute-start
  55.5 1.3 collective-permute-start.7
  56.7 1.0 slice.28
  57.7 0.3 collective-permute-start.5
  58.1 0.0 collective-permute-done.4.cv_ref
  58.1 2.5 %collective-permute-start.8 = (bf16[1,1024,128]{2,1,0:T(8,128)(2,1)S(1)}, bf16[1,1024,128]{2,1,0:T(8,128)(2,1)S(1)}, u32[]{:S(2)}, u32[]{:S(2)}) collective-permute-start(bf16[1,1024,128]{2,1,0:T(8,128)(2,1)S(1)} %slice.31), channel_id=1, source_target_pairs={{0,96},{32,0},{64,32},{96,64},{1,97},{33,1},{65,33},{97,65},{2,98}... | collective-permute-start | bytes 786440 | tf_op jit(solution)/shard_map/ppermute | solution.py:223
  60.6 0.0 collective-permute-done.2.cu_ref
  60.6 0.0 copy-done
  60.6 0.0 copy-done.1
  60.6 0.3 collective-permute-start.6
  60.9 0.1 pad_add_fusion.where_ref
  60.9 0.0 collective-permute-done.cc_ref
  60.9 10.3 %collective-permute-done.7.g_ref = bf16[1,1024,128]{2,1,0:T(8,128)(2,1)S(1)} collective-permute-done((bf16[1,1024,128]{2,1,0:T(8,128)(2,1)S(1)}, bf16[1,1024,128]{2,1,0:T(8,128)(2,1)S(1)}, u32[]{:S(2)}, u32[]{:S(2)}) %collective-permute-start.7) | collective-permute-done | bytes 262176 | tf_op jit(solution)/shard_map/ppermute | solution.py:223
  71.3 1.3 collective-permute-done.5.h_ref
  72.6 4.3 %collective-permute-done.8.cg_ref = bf16[1,1024,128]{2,1,0:T(8,128)(2,1)S(1)} collective-permute-done((bf16[1,1024,128]{2,1,0:T(8,128)(2,1)S(1)}, bf16[1,1024,128]{2,1,0:T(8,128)(2,1)S(1)}, u32[]{:S(2)}, u32[]{:S(2)}) %collective-permute-start.8) | collective-permute-done | bytes 262176 | tf_op jit(solution)/shard_map/ppermute | solution.py:223
  76.9 1.3 collective-permute-done.6.ch_ref
  78.2 0.0 copy-done.3
  78.2 0.0 copy-done.5
  78.3 0.7 copy-done.10
  79.0 19.4 %attn.3 = bf16[128,32,128]{2,1,0:T(8,128)(2,1)} custom-call(s32[2]{0:T(128)S(1)} %pad_add_fusion.where_ref, bf16[128,32,128]{2,1,0:T(8,128)(2,1)} %copy-done.1, bf16[2,1024,128]{2,1,0:T(8,128)(2,1)} %copy-done, bf16[2,1024,128]{2,1,0:T(8,128)(2,1)} %copy-done.6, bf16[2,1024,128]{2,1,0:T(8,128)(2,1)} %collective-permute-done.1.u_ref, ...), custom_call_target="tpu_custom_call" | custom-call | tf_op jit(solution)/shard_map/attn/pallas_call | solution.py:180
  98.4 0.0 all-to-all-done.q_ref
  98.4 0.0 copy-start.2
  98.4 31.7 %all-to-all-start.4 = ((bf16[128,32,128]{2,1,0:T(8,128)(2,1)}), bf16[128,32,128]{2,1,0:T(8,128)(2,1)S(1)}, u32[]{:S(2)}, u32[]{:S(2)}) async-start(bf16[128,32,128]{2,1,0:T(8,128)(2,1)} %attn.3), calls=%async_computation.4 | async-start | bytes 2097152 | tf_op jit(solution)/shard_map/all_to_all | solution.py:234
  130.0 0.0 copy-done.2
  130.1 19.4 %attn.2 = bf16[128,32,128]{2,1,0:T(8,128)(2,1)} custom-call(s32[2]{0:T(128)S(1)} %pad_add_fusion.where_ref, bf16[128,32,128]{2,1,0:T(8,128)(2,1)} %copy-done.2, bf16[2,1024,128]{2,1,0:T(8,128)(2,1)} %copy-done, bf16[2,1024,128]{2,1,0:T(8,128)(2,1)} %copy-done.6, bf16[2,1024,128]{2,1,0:T(8,128)(2,1)} %collective-permute-done.1.u_ref, ...), custom_call_target="tpu_custom_call" | custom-call | tf_op jit(solution)/shard_map/attn/pallas_call | solution.py:180
  149.5 0.1 all-to-all-done.4
  149.5 9.6 %all-to-all-start.2 = ((bf16[128,32,128]{2,1,0:T(8,128)(2,1)}), bf16[128,32,128]{2,1,0:T(8,128)(2,1)S(1)}, u32[]{:S(2)}, u32[]{:S(2)}) async-start(bf16[128,32,128]{2,1,0:T(8,128)(2,1)} %attn.2), calls=%async_computation.2 | async-start | bytes 2097152 | tf_op jit(solution)/shard_map/all_to_all | solution.py:234
  159.2 0.7 copy.6
  159.9 18.8 %all-to-all-done.2 = bf16[128,32,128]{2,1,0:T(8,128)(2,1)S(1)} async-done(((bf16[128,32,128]{2,1,0:T(8,128)(2,1)}), bf16[128,32,128]{2,1,0:T(8,128)(2,1)S(1)}, u32[]{:S(2)}, u32[]{:S(2)}) %all-to-all-start.2) | async-done | bytes 1048608 | tf_op jit(solution)/shard_map/all_to_all | solution.py:234
  178.7 0.7 copy.5
  179.3 1.7 pad.4
  181.1 1.0 constant_dynamic-update-slice_fusion
  (24 shorter events, 0.2 us)
Async XLA Ops:
  3.3 17.8 %all-to-all-start.1 = ((bf16[16,2,64,128]{3,2,1,0:T(8,128)(2,1)}), bf16[16,2,64,128]{3,2,1,0:T(8,128)(2,1)S(1)}, u32[]{:S(2)}, u32[]{:S(2)}) async-start(bf16[16,2,64,128]{3,2,1,0:T(8,128)(2,1)} %pair.1), calls=%async_computation.1 | async-start | bytes 1048576 | tf_op jit(solution)/shard_map/all_to_all | solution.py:208
  21.1 28.1 %all-to-all-start.3 = ((bf16[128,32,128]{2,1,0:T(8,128)(2,1)}), bf16[128,32,128]{2,1,0:T(8,128)(2,1)S(1)}, u32[]{:S(2)}, u32[]{:S(2)}) async-start(bf16[128,32,128]{2,1,0:T(8,128)(2,1)} %bitcast.24), calls=%async_computation.3 | async-start | bytes 2097152 | tf_op jit(solution)/shard_map/all_to_all | solution.py:230
  29.6 31.0 %copy-start = (bf16[2,1024,128]{2,1,0:T(8,128)(2,1)}, bf16[2,1024,128]{2,1,0:T(8,128)(2,1)S(1)}, u32[]{:S(2)}) copy-start(bf16[2,1024,128]{2,1,0:T(8,128)(2,1)S(1)} %pad_maximum_fusion.c_ref) | copy-start | bytes 1572868
  29.6 23.7 %collective-permute-start.3 = (bf16[2,1024,128]{2,1,0:T(8,128)(2,1)S(1)}, bf16[2,1024,128]{2,1,0:T(8,128)(2,1)S(1)}, u32[]{:S(2)}, u32[]{:S(2)}) collective-permute-start(bf16[2,1024,128]{2,1,0:T(8,128)(2,1)S(1)} %pad_maximum_fusion.c_ref), channel_id=1, source_target_pairs={{0,96},{32,0},{64,32},{96,64},{1,97},{33,1},{65,33},{97,65},{2,98}... | collective-permute-start | bytes 1572872 | tf_op jit(solution)/shard_map/ppermute | solution.py:217
  32.3 22.3 %collective-permute-start.1 = (bf16[2,1024,128]{2,1,0:T(8,128)(2,1)S(1)}, bf16[2,1024,128]{2,1,0:T(8,128)(2,1)}, u32[]{:S(2)}, u32[]{:S(2)}) collective-permute-start(bf16[2,1024,128]{2,1,0:T(8,128)(2,1)S(1)} %pad_maximum_fusion.c_ref), channel_id=1, source_target_pairs={{0,32},{32,64},{64,96},{96,0},{1,33},{33,65},{65,97},{97,1},{2,34}... | collective-permute-start | bytes 1572872 | tf_op jit(solution)/shard_map/ppermute | solution.py:216
  49.1 11.5 %copy-start.1 = (bf16[128,32,128]{2,1,0:T(8,128)(2,1)}, bf16[128,32,128]{2,1,0:T(8,128)(2,1)S(1)}, u32[]{:S(2)}) copy-start(bf16[128,32,128]{2,1,0:T(8,128)(2,1)S(1)} %all-to-all-done.3.q_ref) | copy-start | bytes 3145732
  49.1 49.2 %all-to-all-start = ((bf16[128,32,128]{2,1,0:T(8,128)(2,1)}), bf16[128,32,128]{2,1,0:T(8,128)(2,1)S(1)}, u32[]{:S(2)}, u32[]{:S(2)}) async-start(bf16[128,32,128]{2,1,0:T(8,128)(2,1)} %bitcast.23), calls=%async_computation | async-start | bytes 2097152 | tf_op jit(solution)/shard_map/all_to_all | solution.py:230
  53.3 24.9 %copy-start.3 = (bf16[2,1024,128]{2,1,0:T(8,128)(2,1)}, bf16[2,1024,128]{2,1,0:T(8,128)(2,1)S(1)}, u32[]{:S(2)}) copy-start(bf16[2,1024,128]{2,1,0:T(8,128)(2,1)S(1)} %collective-permute-done.3.v_ref) | copy-start | bytes 1572868
  53.3 4.8 %collective-permute-start.4 = (bf16[2,1024,128]{2,1,0:T(8,128)(2,1)S(1)}, bf16[2,1024,128]{2,1,0:T(8,128)(2,1)S(1)}, u32[]{:S(2)}, u32[]{:S(2)}) collective-permute-start(bf16[2,1024,128]{2,1,0:T(8,128)(2,1)S(1)} %collective-permute-done.3.v_ref), channel_id=1, source_target_pairs={{0,8},{8,0},{1,9},{9,1},{2,10},{10,2},{3,11},{11,3},{4,12},{12,4},... | collective-permute-start | bytes 1572872 | tf_op jit(solution)/shard_map/ppermute | solution.py:220
  54.6 6.0 %collective-permute-start.2 = (bf16[2,1024,128]{2,1,0:T(8,128)(2,1)}, bf16[2,1024,128]{2,1,0:T(8,128)(2,1)S(1)}, u32[]{:S(2)}, u32[]{:S(2)}) collective-permute-start(bf16[2,1024,128]{2,1,0:T(8,128)(2,1)} %collective-permute-done.1.u_ref), channel_id=1, source_target_pairs={{0,8},{8,0},{1,9},{9,1},{2,10},{10,2},{3,11},{11,3},{4,12},{12,4},... | collective-permute-start | bytes 1572872 | tf_op jit(solution)/shard_map/ppermute | solution.py:220
  55.5 5.5 %collective-permute-start = (bf16[2,1024,128]{2,1,0:T(8,128)(2,1)S(1)}, bf16[2,1024,128]{2,1,0:T(8,128)(2,1)S(1)}, u32[]{:S(2)}, u32[]{:S(2)}) collective-permute-start(bf16[2,1024,128]{2,1,0:T(8,128)(2,1)S(1)} %pad_maximum_fusion.c_ref), channel_id=1, source_target_pairs={{0,8},{8,0},{1,9},{9,1},{2,10},{10,2},{3,11},{11,3},{4,12},{12,4},... | collective-permute-start | bytes 1572872 | tf_op jit(solution)/shard_map/ppermute | solution.py:220
  55.5 15.8 %collective-permute-start.7 = (bf16[1,1024,128]{2,1,0:T(8,128)(2,1)S(1)}, bf16[1,1024,128]{2,1,0:T(8,128)(2,1)S(1)}, u32[]{:S(2)}, u32[]{:S(2)}) collective-permute-start(bf16[1,1024,128]{2,1,0:T(8,128)(2,1)S(1)} %slice.30), channel_id=1, source_target_pairs={{0,96},{32,0},{64,32},{96,64},{1,97},{33,1},{65,33},{97,65},{2,98}... | collective-permute-start | bytes 786440 | tf_op jit(solution)/shard_map/ppermute | solution.py:223
  57.7 14.9 %collective-permute-start.5 = (bf16[1,1024,128]{2,1,0:T(8,128)(2,1)S(1)}, bf16[1,1024,128]{2,1,0:T(8,128)(2,1)S(1)}, u32[]{:S(2)}, u32[]{:S(2)}) collective-permute-start(bf16[1,1024,128]{2,1,0:T(8,128)(2,1)S(1)} %slice.28), channel_id=1, source_target_pairs={{0,32},{32,64},{64,96},{96,0},{1,33},{33,65},{65,97},{97,1},{2,34}... | collective-permute-start | bytes 786440 | tf_op jit(solution)/shard_map/ppermute | solution.py:223
  58.1 20.2 %copy-start.4 = (bf16[2,1024,128]{2,1,0:T(8,128)(2,1)}, bf16[2,1024,128]{2,1,0:T(8,128)(2,1)S(1)}, u32[]{:S(2)}) copy-start(bf16[2,1024,128]{2,1,0:T(8,128)(2,1)S(1)} %collective-permute-done.4.cv_ref) | copy-start | bytes 1572868
  58.1 18.8 %collective-permute-start.8 = (bf16[1,1024,128]{2,1,0:T(8,128)(2,1)S(1)}, bf16[1,1024,128]{2,1,0:T(8,128)(2,1)S(1)}, u32[]{:S(2)}, u32[]{:S(2)}) collective-permute-start(bf16[1,1024,128]{2,1,0:T(8,128)(2,1)S(1)} %slice.31), channel_id=1, source_target_pairs={{0,96},{32,0},{64,32},{96,64},{1,97},{33,1},{65,33},{97,65},{2,98}... | collective-permute-start | bytes 786440 | tf_op jit(solution)/shard_map/ppermute | solution.py:223
  60.6 17.7 %copy-start.5 = (bf16[2,1024,128]{2,1,0:T(8,128)(2,1)}, bf16[2,1024,128]{2,1,0:T(8,128)(2,1)S(1)}, u32[]{:S(2)}) copy-start(bf16[2,1024,128]{2,1,0:T(8,128)(2,1)S(1)} %collective-permute-done.2.cu_ref) | copy-start | bytes 1572868
  60.6 17.6 %collective-permute-start.6 = (bf16[1,1024,128]{2,1,0:T(8,128)(2,1)S(1)}, bf16[1,1024,128]{2,1,0:T(8,128)(2,1)S(1)}, u32[]{:S(2)}, u32[]{:S(2)}) collective-permute-start(bf16[1,1024,128]{2,1,0:T(8,128)(2,1)S(1)} %slice.29), channel_id=1, source_target_pairs={{0,32},{32,64},{64,96},{96,0},{1,33},{33,65},{65,97},{97,1},{2,34}... | collective-permute-start | bytes 786440 | tf_op jit(solution)/shard_map/ppermute | solution.py:223
  60.9 17.3 %copy-start.6 = (bf16[2,1024,128]{2,1,0:T(8,128)(2,1)}, bf16[2,1024,128]{2,1,0:T(8,128)(2,1)S(1)}, u32[]{:S(2)}) copy-start(bf16[2,1024,128]{2,1,0:T(8,128)(2,1)S(1)} %collective-permute-done.cc_ref) | copy-start | bytes 1572868
  71.3 6.9 %copy-start.7 = (bf16[1,1024,128]{2,1,0:T(8,128)(2,1)}, bf16[1,1024,128]{2,1,0:T(8,128)(2,1)S(1)}, u32[]{:S(2)}) copy-start(bf16[1,1024,128]{2,1,0:T(8,128)(2,1)S(1)} %collective-permute-done.7.g_ref) | copy-start | bytes 786436
  72.6 5.7 %copy-start.8 = (bf16[1,1024,128]{2,1,0:T(8,128)(2,1)}, bf16[1,1024,128]{2,1,0:T(8,128)(2,1)S(1)}, u32[]{:S(2)}) copy-start(bf16[1,1024,128]{2,1,0:T(8,128)(2,1)S(1)} %collective-permute-done.5.h_ref) | copy-start | bytes 786436
  76.9 1.3 copy-start.9
  78.3 0.7 copy-start.10
  98.4 31.7 %copy-start.2 = (bf16[128,32,128]{2,1,0:T(8,128)(2,1)}, bf16[128,32,128]{2,1,0:T(8,128)(2,1)S(1)}, u32[]{:S(2)}) copy-start(bf16[128,32,128]{2,1,0:T(8,128)(2,1)S(1)} %all-to-all-done.q_ref) | copy-start | bytes 3145732
  98.4 51.2 %all-to-all-start.4 = ((bf16[128,32,128]{2,1,0:T(8,128)(2,1)}), bf16[128,32,128]{2,1,0:T(8,128)(2,1)S(1)}, u32[]{:S(2)}, u32[]{:S(2)}) async-start(bf16[128,32,128]{2,1,0:T(8,128)(2,1)} %attn.3), calls=%async_computation.4 | async-start | bytes 2097152 | tf_op jit(solution)/shard_map/all_to_all | solution.py:234
  149.5 29.1 %all-to-all-start.2 = ((bf16[128,32,128]{2,1,0:T(8,128)(2,1)}), bf16[128,32,128]{2,1,0:T(8,128)(2,1)S(1)}, u32[]{:S(2)}, u32[]{:S(2)}) async-start(bf16[128,32,128]{2,1,0:T(8,128)(2,1)} %attn.2), calls=%async_computation.2 | async-start | bytes 2097152 | tf_op jit(solution)/shard_map/all_to_all | solution.py:234

commit v6 on v5

--- a/solution.py
+++ b/solution.py
@@ -27,18 +27,24 @@
     )
 
 
+def doubled(cos_ref, sin_ref):
+    cosine, sine = cos_ref[...], sin_ref[...]
+    return jnp.concatenate([cosine, cosine], axis=1), jnp.concatenate([-sine, sine], axis=1)
+
+
 def turned(head, cosine, signed_sine):
     return head * cosine + pltpu.roll(head, head.shape[-1] // 2, 1) * signed_sine
 
 
-def prepare_pair(keys, values, cosine, signed_sine):
+def prepare_pair(keys, values, cosine, sine):
     rows, heads, width = keys.shape
 
     def kernel(k_ref, v_ref, cos_ref, sin_ref, o_ref, kf_ref, vf_ref):
+        tables = doubled(cos_ref, sin_ref)
         kf_ref[...] = k_ref[...].astype(jnp.float32)
         vf_ref[...] = v_ref[...].astype(jnp.float32)
         for h in range(heads):
-            key = turned(kf_ref[:, h, :], cos_ref[...], sin_ref[...]).astype(jnp.bfloat16)
+            key = turned(kf_ref[:, h, :], *tables).astype(jnp.bfloat16)
             value = vf_ref[:, h, :].astype(jnp.bfloat16)
             for half in (0, heads):
                 o_ref[half + h, 0] = key
@@ -48,29 +54,30 @@
     return pl.pallas_call(
         kernel, out_shape=jax.ShapeDtypeStruct((2 * heads, 2, rows, width), jnp.bfloat16),
         scratch_shapes=[wide, wide], name="pair",
-    )(keys, values, cosine, signed_sine)
-
-
-def prepare_queries(queries, cosine, signed_sine, group):
+    )(keys, values, cosine, sine)
+
+
+def prepare_queries(queries, cosine, sine, group):
     rows, heads, width = queries.shape
     strip = rows // CHUNKS
 
     def kernel(q_ref, cos_ref, sin_ref, *rest):
         outs, wide_ref = rest[:-1], rest[-1]
+        tables = doubled(cos_ref, sin_ref)
         wide_ref[...] = q_ref[...].astype(jnp.float32)
         for h in range(group):
-            head = turned(wide_ref[:, h, :], cos_ref[...], sin_ref[...]).astype(jnp.bfloat16)
+            head = turned(wide_ref[:, h, :], *tables).astype(jnp.bfloat16)
             for n, o_ref in enumerate(outs):
                 o_ref[h, 0] = head[n * strip:(n + 1) * strip]
 
-    table = pl.BlockSpec((rows, width), lambda g: (0, 0))
+    table = pl.BlockSpec((rows, width // 2), lambda g: (0, 0))
     parts = pl.pallas_call(
         kernel, grid=(heads // group,),
         in_specs=[pl.BlockSpec((rows, group, width), lambda g: (0, g, 0)), table, table],
         out_specs=[pl.BlockSpec((group, 1, strip, width), lambda g: (0, g, 0, 0))] * CHUNKS,
         out_shape=[jax.ShapeDtypeStruct((group, heads // group, strip, width), jnp.bfloat16)] * CHUNKS,
         scratch_shapes=[pltpu.VMEM((rows, group, width), jnp.float32)], name="queries",
-    )(queries, cosine, signed_sine)
+    )(queries, cosine, sine)
     return [part.reshape(heads, strip, width) for part in parts]
 
 
@@ -200,11 +207,10 @@
     start_row = lax.axis_index(AXES) * rows
     positions = start_row + jnp.arange(rows, dtype=jnp.int32)
 
-    angles = positions.astype(jnp.float32)[:, None] * jnp.tile(frequencies(width), 2)[None, :]
-    cosine = jnp.cos(angles)
-    signed_sine = jnp.sin(angles) * jnp.where(jnp.arange(width) < width // 2, -1.0, 1.0)
-
-    pair = prepare_pair(keys, values, cosine, signed_sine)
+    angles = positions.astype(jnp.float32)[:, None] * frequencies(width)[None, :]
+    cosine, sine = jnp.cos(angles), jnp.sin(angles)
+
+    pair = prepare_pair(keys, values, cosine, sine)
     pair = lax.all_to_all(pair, ("yl", "sy"), split_axis=0, concat_axis=0, tiled=True)
     pair = pair.swapaxes(0, 1).reshape(2, 2, -1, width)
     block = pair.shape[2]
@@ -224,7 +230,7 @@
     pieces = near + [far[0], far[2], far[1], far[3]]
     where = jnp.stack([x, core]).astype(jnp.int32)
 
-    ordered = prepare_queries(queries, cosine, signed_sine, group)
+    ordered = prepare_queries(queries, cosine, sine, group)
     arrived = []
     for n in range(CHUNKS):
         arrived.append(lax.all_to_all(ordered[n], AXES, split_axis=0, concat_axis=0, tiled=True))

time: 183 us -> 183 us (level)
  no operation moved by 1% of the time
where the time goes in v6:
time: 183 us; the launch traced here: 182 us
  starting transfers between devices  70.9 us (39%)
  waiting for transfers between devices  55.5 us (30%)
  Pallas kernels  48.3 us (26%)
  local copies, waits for them, and re-layouts  6.11 us (3%)
    all_to_all x2, starting transfers between devices, shards(): back = lax.all_to_all(done, AXES, split_axis=0, concat_axis=0, tiled=True)  41.3 us
    pallas_call x2, Pallas kernels, attn(): pl.pallas_call(kernel, grid=(G // devs,), in_specs=[pl.BlockSpec(memory_s...  38.8 us
    all_to_all x2, waiting for transfers between devices, shards(): back = lax.all_to_all(done, AXES, split_axis=0, concat_axis=0, tiled=True)  18.9 us
    ppermute x4, waiting for transfers between devices, shards(): far.append(lax.ppermute(source[half:half + 1], 'x', way))  17.3 us
    all_to_all x2, waiting for transfers between devices, shards(): lax.all_to_all(ordered[n], AXES, split_axis=0, concat_axis=0, tiled=True)  16.9 us
    all_to_all x2, starting transfers between devices, shards(): lax.all_to_all(ordered[n], AXES, split_axis=0, concat_axis=0, tiled=True)  12.2 us
    all_to_all x1, starting transfers between devices, shards(): lax.all_to_all(pair, ('yl', 'sy'), split_axis=0, concat_axis=0, tiled=True)  8.59 us
    pallas_call x1, Pallas kernels, prepare_queries(): pl.pallas_call(kernel, grid=(heads // group,), in_specs=[pl.BlockSpec((ro...  7.22 us
  transfers between devices with their start and end apart: 14, of which 10 were waited for; matrix products, arithmetic and copies ran while one was open for 1% of the time, Pallas kernels for 25%

profile of v6, /device:TPU:1, one launch (start us, length us, event | category | flops | bytes accessed | tf_op | source)
XLA Modules:
  0.0 182.0 jit_solution(6562473417691337912)
XLA Ops:
  0.0 0.8 multiply_sine_fusion
  0.9 2.3 %pair.1 = bf16[16,2,64,128]{3,2,1,0:T(8,128)(2,1)} custom-call(bf16[64,8,128]{2,1,0:T(8,128)(2,1)} %k_ref.1, bf16[64,8,128]{2,1,0:T(8,128)(2,1)} %v_ref.1, f32[64,64]{1,0:T(8,128)} %get-tuple-element.12.cos_ref, f32[64,64]{1,0:T(8,128)} %get-tuple-element.11.sin_ref), custom_call_target="tpu_custom_call" | custom-call | tf_op jit(solution)/shard_map/pair/pallas_call | solution.py:54
  3.2 8.6 %all-to-all-start.1 = ((bf16[16,2,64,128]{3,2,1,0:T(8,128)(2,1)}), bf16[16,2,64,128]{3,2,1,0:T(8,128)(2,1)S(1)}, u32[]{:S(2)}, u32[]{:S(2)}) async-start(bf16[16,2,64,128]{3,2,1,0:T(8,128)(2,1)} %pair.1), calls=%async_computation.1 | async-start | bytes 1048576 | tf_op jit(solution)/shard_map/all_to_all | solution.py:214
  11.8 7.2 %queries.1 = (bf16[16,8,32,128]{3,2,1,0:T(8,128)(2,1)}, bf16[16,8,32,128]{3,2,1,0:T(8,128)(2,1)}) custom-call(bf16[64,128,128]{2,1,0:T(8,128)(2,1)} %q_ref.1, f32[64,64]{1,0:T(8,128)} %get-tuple-element.12.cos_ref, f32[64,64]{1,0:T(8,128)} %get-tuple-element.11.sin_ref), custom_call_target="tpu_custom_call" | custom-call | tf_op jit(solution)/shard_map/queries/pallas_call | solution.py:74
  19.0 2.0 %all-to-all-done.1 = bf16[16,2,64,128]{3,2,1,0:T(8,128)(2,1)S(1)} async-done(((bf16[16,2,64,128]{3,2,1,0:T(8,128)(2,1)}), bf16[16,2,64,128]{3,2,1,0:T(8,128)(2,1)S(1)}, u32[]{:S(2)}, u32[]{:S(2)}) %all-to-all-start.1) | async-done | bytes 524320 | tf_op jit(solution)/shard_map/all_to_all | solution.py:214
  21.0 8.3 %all-to-all-start.3 = ((bf16[128,32,128]{2,1,0:T(8,128)(2,1)}), bf16[128,32,128]{2,1,0:T(8,128)(2,1)S(1)}, u32[]{:S(2)}, u32[]{:S(2)}) async-start(bf16[128,32,128]{2,1,0:T(8,128)(2,1)} %bitcast.24), calls=%async_computation.3 | async-start | bytes 2097152 | tf_op jit(solution)/shard_map/all_to_all | solution.py:236
  29.3 0.2 copy.4
  29.5 0.0 copy-start
  29.5 2.6 %collective-permute-start.3 = (bf16[2,1024,128]{2,1,0:T(8,128)(2,1)S(1)}, bf16[2,1024,128]{2,1,0:T(8,128)(2,1)S(1)}, u32[]{:S(2)}, u32[]{:S(2)}) collective-permute-start(bf16[2,1024,128]{2,1,0:T(8,128)(2,1)S(1)} %pad_maximum_fusion.c_ref), channel_id=1, source_target_pairs={{0,96},{32,0},{64,32},{96,64},{1,97},{33,1},{65,33},{97,65},{2,98}... | collective-permute-start | bytes 1572872 | tf_op jit(solution)/shard_map/ppermute | solution.py:223
  32.2 0.0 collective-permute-start.1
  32.2 16.9 %all-to-all-done.3.q_ref = bf16[128,32,128]{2,1,0:T(8,128)(2,1)S(1)} async-done(((bf16[128,32,128]{2,1,0:T(8,128)(2,1)}), bf16[128,32,128]{2,1,0:T(8,128)(2,1)S(1)}, u32[]{:S(2)}, u32[]{:S(2)}) %all-to-all-start.3) | async-done | bytes 1048608 | tf_op jit(solution)/shard_map/all_to_all | solution.py:236
  49.0 3.9 %all-to-all-start = ((bf16[128,32,128]{2,1,0:T(8,128)(2,1)}), bf16[128,32,128]{2,1,0:T(8,128)(2,1)S(1)}, u32[]{:S(2)}, u32[]{:S(2)}) async-start(bf16[128,32,128]{2,1,0:T(8,128)(2,1)} %bitcast.23), calls=%async_computation | async-start | bytes 2097152 | tf_op jit(solution)/shard_map/all_to_all | solution.py:236
  53.0 0.2 collective-permute-done.3.v_ref
  53.2 1.0 collective-permute-start.4
  54.2 0.3 collective-permute-done.1.u_ref
  54.5 0.9 collective-permute-start.2
  55.4 0.0 collective-permute-start
  55.4 1.3 collective-permute-start.7
  56.7 1.0 slice.28
  57.6 0.3 collective-permute-start.5
  58.0 0.0 collective-permute-done.4.cv_ref
  58.0 2.5 %collective-permute-start.8 = (bf16[1,1024,128]{2,1,0:T(8,128)(2,1)S(1)}, bf16[1,1024,128]{2,1,0:T(8,128)(2,1)S(1)}, u32[]{:S(2)}, u32[]{:S(2)}) collective-permute-start(bf16[1,1024,128]{2,1,0:T(8,128)(2,1)S(1)} %slice.31), channel_id=1, source_target_pairs={{0,96},{32,0},{64,32},{96,64},{1,97},{33,1},{65,33},{97,65},{2,98}... | collective-permute-start | bytes 786440 | tf_op jit(solution)/shard_map/ppermute | solution.py:229
  60.5 0.0 collective-permute-done.2.cu_ref
  60.5 0.3 collective-permute-start.6
  60.8 0.1 pad_add_fusion.where_ref
  60.9 0.0 collective-permute-done.cc_ref
  60.9 10.3 %collective-permute-done.7.g_ref = bf16[1,1024,128]{2,1,0:T(8,128)(2,1)S(1)} collective-permute-done((bf16[1,1024,128]{2,1,0:T(8,128)(2,1)S(1)}, bf16[1,1024,128]{2,1,0:T(8,128)(2,1)S(1)}, u32[]{:S(2)}, u32[]{:S(2)}) %collective-permute-start.7) | collective-permute-done | bytes 262176 | tf_op jit(solution)/shard_map/ppermute | solution.py:229
  71.2 1.3 collective-permute-done.5.h_ref
  72.5 4.3 %collective-permute-done.8.cg_ref = bf16[1,1024,128]{2,1,0:T(8,128)(2,1)S(1)} collective-permute-done((bf16[1,1024,128]{2,1,0:T(8,128)(2,1)S(1)}, bf16[1,1024,128]{2,1,0:T(8,128)(2,1)S(1)}, u32[]{:S(2)}, u32[]{:S(2)}) %collective-permute-start.8) | collective-permute-done | bytes 262176 | tf_op jit(solution)/shard_map/ppermute | solution.py:229
  76.8 1.3 collective-permute-done.6.ch_ref
  78.1 0.0 copy-done.6
  78.1 0.0 copy-done.7
  78.2 0.0 copy-done.8
  78.2 0.0 copy-done.9
  78.2 0.0 copy-start.10
  78.2 0.7 copy-done.10
  78.9 19.4 %attn.3 = bf16[128,32,128]{2,1,0:T(8,128)(2,1)} custom-call(s32[2]{0:T(128)S(1)} %pad_add_fusion.where_ref, bf16[128,32,128]{2,1,0:T(8,128)(2,1)} %copy-done.1, bf16[2,1024,128]{2,1,0:T(8,128)(2,1)} %copy-done, bf16[2,1024,128]{2,1,0:T(8,128)(2,1)} %copy-done.6, bf16[2,1024,128]{2,1,0:T(8,128)(2,1)} %collective-permute-done.1.u_ref, ...), custom_call_target="tpu_custom_call" | custom-call | tf_op jit(solution)/shard_map/attn/pallas_call | solution.py:187
  98.3 0.0 all-to-all-done.q_ref
  98.3 0.0 copy-start.2
  98.3 31.7 %all-to-all-start.4 = ((bf16[128,32,128]{2,1,0:T(8,128)(2,1)}), bf16[128,32,128]{2,1,0:T(8,128)(2,1)S(1)}, u32[]{:S(2)}, u32[]{:S(2)}) async-start(bf16[128,32,128]{2,1,0:T(8,128)(2,1)} %attn.3), calls=%async_computation.4 | async-start | bytes 2097152 | tf_op jit(solution)/shard_map/all_to_all | solution.py:240
  130.0 19.4 %attn.2 = bf16[128,32,128]{2,1,0:T(8,128)(2,1)} custom-call(s32[2]{0:T(128)S(1)} %pad_add_fusion.where_ref, bf16[128,32,128]{2,1,0:T(8,128)(2,1)} %copy-done.2, bf16[2,1024,128]{2,1,0:T(8,128)(2,1)} %copy-done, bf16[2,1024,128]{2,1,0:T(8,128)(2,1)} %copy-done.6, bf16[2,1024,128]{2,1,0:T(8,128)(2,1)} %collective-permute-done.1.u_ref, ...), custom_call_target="tpu_custom_call" | custom-call | tf_op jit(solution)/shard_map/attn/pallas_call | solution.py:187
  149.4 0.1 all-to-all-done.4
  149.4 9.6 %all-to-all-start.2 = ((bf16[128,32,128]{2,1,0:T(8,128)(2,1)}), bf16[128,32,128]{2,1,0:T(8,128)(2,1)S(1)}, u32[]{:S(2)}, u32[]{:S(2)}) async-start(bf16[128,32,128]{2,1,0:T(8,128)(2,1)} %attn.2), calls=%async_computation.2 | async-start | bytes 2097152 | tf_op jit(solution)/shard_map/all_to_all | solution.py:240
  159.1 0.7 copy.6
  159.8 18.8 %all-to-all-done.2 = bf16[128,32,128]{2,1,0:T(8,128)(2,1)S(1)} async-done(((bf16[128,32,128]{2,1,0:T(8,128)(2,1)}), bf16[128,32,128]{2,1,0:T(8,128)(2,1)S(1)}, u32[]{:S(2)}, u32[]{:S(2)}) %all-to-all-start.2) | async-done | bytes 1048608 | tf_op jit(solution)/shard_map/all_to_all | solution.py:240
  178.6 0.7 copy.5
  179.3 1.7 pad.4
  181.0 1.0 constant_dynamic-update-slice_fusion
  (21 shorter events, 0.2 us)
Async XLA Ops:
  3.2 17.8 %all-to-all-start.1 = ((bf16[16,2,64,128]{3,2,1,0:T(8,128)(2,1)}), bf16[16,2,64,128]{3,2,1,0:T(8,128)(2,1)S(1)}, u32[]{:S(2)}, u32[]{:S(2)}) async-start(bf16[16,2,64,128]{3,2,1,0:T(8,128)(2,1)} %pair.1), calls=%async_computation.1 | async-start | bytes 1048576 | tf_op jit(solution)/shard_map/all_to_all | solution.py:214
  21.0 28.1 %all-to-all-start.3 = ((bf16[128,32,128]{2,1,0:T(8,128)(2,1)}), bf16[128,32,128]{2,1,0:T(8,128)(2,1)S(1)}, u32[]{:S(2)}, u32[]{:S(2)}) async-start(bf16[128,32,128]{2,1,0:T(8,128)(2,1)} %bitcast.24), calls=%async_computation.3 | async-start | bytes 2097152 | tf_op jit(solution)/shard_map/all_to_all | solution.py:236
  29.5 31.0 %copy-start = (bf16[2,1024,128]{2,1,0:T(8,128)(2,1)}, bf16[2,1024,128]{2,1,0:T(8,128)(2,1)S(1)}, u32[]{:S(2)}) copy-start(bf16[2,1024,128]{2,1,0:T(8,128)(2,1)S(1)} %pad_maximum_fusion.c_ref) | copy-start | bytes 1572868
  29.5 23.7 %collective-permute-start.3 = (bf16[2,1024,128]{2,1,0:T(8,128)(2,1)S(1)}, bf16[2,1024,128]{2,1,0:T(8,128)(2,1)S(1)}, u32[]{:S(2)}, u32[]{:S(2)}) collective-permute-start(bf16[2,1024,128]{2,1,0:T(8,128)(2,1)S(1)} %pad_maximum_fusion.c_ref), channel_id=1, source_target_pairs={{0,96},{32,0},{64,32},{96,64},{1,97},{33,1},{65,33},{97,65},{2,98}... | collective-permute-start | bytes 1572872 | tf_op jit(solution)/shard_map/ppermute | solution.py:223
  32.2 22.3 %collective-permute-start.1 = (bf16[2,1024,128]{2,1,0:T(8,128)(2,1)S(1)}, bf16[2,1024,128]{2,1,0:T(8,128)(2,1)}, u32[]{:S(2)}, u32[]{:S(2)}) collective-permute-start(bf16[2,1024,128]{2,1,0:T(8,128)(2,1)S(1)} %pad_maximum_fusion.c_ref), channel_id=1, source_target_pairs={{0,32},{32,64},{64,96},{96,0},{1,33},{33,65},{65,97},{97,1},{2,34}... | collective-permute-start | bytes 1572872 | tf_op jit(solution)/shard_map/ppermute | solution.py:222
  49.0 11.5 %copy-start.1 = (bf16[128,32,128]{2,1,0:T(8,128)(2,1)}, bf16[128,32,128]{2,1,0:T(8,128)(2,1)S(1)}, u32[]{:S(2)}) copy-start(bf16[128,32,128]{2,1,0:T(8,128)(2,1)S(1)} %all-to-all-done.3.q_ref) | copy-start | bytes 3145732
  49.0 49.2 %all-to-all-start = ((bf16[128,32,128]{2,1,0:T(8,128)(2,1)}), bf16[128,32,128]{2,1,0:T(8,128)(2,1)S(1)}, u32[]{:S(2)}, u32[]{:S(2)}) async-start(bf16[128,32,128]{2,1,0:T(8,128)(2,1)} %bitcast.23), calls=%async_computation | async-start | bytes 2097152 | tf_op jit(solution)/shard_map/all_to_all | solution.py:236
  53.2 24.9 %copy-start.3 = (bf16[2,1024,128]{2,1,0:T(8,128)(2,1)}, bf16[2,1024,128]{2,1,0:T(8,128)(2,1)S(1)}, u32[]{:S(2)}) copy-start(bf16[2,1024,128]{2,1,0:T(8,128)(2,1)S(1)} %collective-permute-done.3.v_ref) | copy-start | bytes 1572868
  53.2 4.8 %collective-permute-start.4 = (bf16[2,1024,128]{2,1,0:T(8,128)(2,1)S(1)}, bf16[2,1024,128]{2,1,0:T(8,128)(2,1)S(1)}, u32[]{:S(2)}, u32[]{:S(2)}) collective-permute-start(bf16[2,1024,128]{2,1,0:T(8,128)(2,1)S(1)} %collective-permute-done.3.v_ref), channel_id=1, source_target_pairs={{0,8},{8,0},{1,9},{9,1},{2,10},{10,2},{3,11},{11,3},{4,12},{12,4},... | collective-permute-start | bytes 1572872 | tf_op jit(solution)/shard_map/ppermute | solution.py:226
  54.5 6.0 %collective-permute-start.2 = (bf16[2,1024,128]{2,1,0:T(8,128)(2,1)}, bf16[2,1024,128]{2,1,0:T(8,128)(2,1)S(1)}, u32[]{:S(2)}, u32[]{:S(2)}) collective-permute-start(bf16[2,1024,128]{2,1,0:T(8,128)(2,1)} %collective-permute-done.1.u_ref), channel_id=1, source_target_pairs={{0,8},{8,0},{1,9},{9,1},{2,10},{10,2},{3,11},{11,3},{4,12},{12,4},... | collective-permute-start | bytes 1572872 | tf_op jit(solution)/shard_map/ppermute | solution.py:226
  55.4 5.5 %collective-permute-start = (bf16[2,1024,128]{2,1,0:T(8,128)(2,1)S(1)}, bf16[2,1024,128]{2,1,0:T(8,128)(2,1)S(1)}, u32[]{:S(2)}, u32[]{:S(2)}) collective-permute-start(bf16[2,1024,128]{2,1,0:T(8,128)(2,1)S(1)} %pad_maximum_fusion.c_ref), channel_id=1, source_target_pairs={{0,8},{8,0},{1,9},{9,1},{2,10},{10,2},{3,11},{11,3},{4,12},{12,4},... | collective-permute-start | bytes 1572872 | tf_op jit(solution)/shard_map/ppermute | solution.py:226
  55.4 15.8 %collective-permute-start.7 = (bf16[1,1024,128]{2,1,0:T(8,128)(2,1)S(1)}, bf16[1,1024,128]{2,1,0:T(8,128)(2,1)S(1)}, u32[]{:S(2)}, u32[]{:S(2)}) collective-permute-start(bf16[1,1024,128]{2,1,0:T(8,128)(2,1)S(1)} %slice.30), channel_id=1, source_target_pairs={{0,96},{32,0},{64,32},{96,64},{1,97},{33,1},{65,33},{97,65},{2,98}... | collective-permute-start | bytes 786440 | tf_op jit(solution)/shard_map/ppermute | solution.py:229
  57.6 14.9 %collective-permute-start.5 = (bf16[1,1024,128]{2,1,0:T(8,128)(2,1)S(1)}, bf16[1,1024,128]{2,1,0:T(8,128)(2,1)S(1)}, u32[]{:S(2)}, u32[]{:S(2)}) collective-permute-start(bf16[1,1024,128]{2,1,0:T(8,128)(2,1)S(1)} %slice.28), channel_id=1, source_target_pairs={{0,32},{32,64},{64,96},{96,0},{1,33},{33,65},{65,97},{97,1},{2,34}... | collective-permute-start | bytes 786440 | tf_op jit(solution)/shard_map/ppermute | solution.py:229
  58.0 20.2 %copy-start.4 = (bf16[2,1024,128]{2,1,0:T(8,128)(2,1)}, bf16[2,1024,128]{2,1,0:T(8,128)(2,1)S(1)}, u32[]{:S(2)}) copy-start(bf16[2,1024,128]{2,1,0:T(8,128)(2,1)S(1)} %collective-permute-done.4.cv_ref) | copy-start | bytes 1572868
  58.0 18.8 %collective-permute-start.8 = (bf16[1,1024,128]{2,1,0:T(8,128)(2,1)S(1)}, bf16[1,1024,128]{2,1,0:T(8,128)(2,1)S(1)}, u32[]{:S(2)}, u32[]{:S(2)}) collective-permute-start(bf16[1,1024,128]{2,1,0:T(8,128)(2,1)S(1)} %slice.31), channel_id=1, source_target_pairs={{0,96},{32,0},{64,32},{96,64},{1,97},{33,1},{65,33},{97,65},{2,98}... | collective-permute-start | bytes 786440 | tf_op jit(solution)/shard_map/ppermute | solution.py:229
  60.5 17.7 %copy-start.5 = (bf16[2,1024,128]{2,1,0:T(8,128)(2,1)}, bf16[2,1024,128]{2,1,0:T(8,128)(2,1)S(1)}, u32[]{:S(2)}) copy-start(bf16[2,1024,128]{2,1,0:T(8,128)(2,1)S(1)} %collective-permute-done.2.cu_ref) | copy-start | bytes 1572868
  60.5 17.6 %collective-permute-start.6 = (bf16[1,1024,128]{2,1,0:T(8,128)(2,1)S(1)}, bf16[1,1024,128]{2,1,0:T(8,128)(2,1)S(1)}, u32[]{:S(2)}, u32[]{:S(2)}) collective-permute-start(bf16[1,1024,128]{2,1,0:T(8,128)(2,1)S(1)} %slice.29), channel_id=1, source_target_pairs={{0,32},{32,64},{64,96},{96,0},{1,33},{33,65},{65,97},{97,1},{2,34}... | collective-permute-start | bytes 786440 | tf_op jit(solution)/shard_map/ppermute | solution.py:229
  60.9 17.3 %copy-start.6 = (bf16[2,1024,128]{2,1,0:T(8,128)(2,1)}, bf16[2,1024,128]{2,1,0:T(8,128)(2,1)S(1)}, u32[]{:S(2)}) copy-start(bf16[2,1024,128]{2,1,0:T(8,128)(2,1)S(1)} %collective-permute-done.cc_ref) | copy-start | bytes 1572868
  71.2 6.9 %copy-start.7 = (bf16[1,1024,128]{2,1,0:T(8,128)(2,1)}, bf16[1,1024,128]{2,1,0:T(8,128)(2,1)S(1)}, u32[]{:S(2)}) copy-start(bf16[1,1024,128]{2,1,0:T(8,128)(2,1)S(1)} %collective-permute-done.7.g_ref) | copy-start | bytes 786436
  72.5 5.7 %copy-start.8 = (bf16[1,1024,128]{2,1,0:T(8,128)(2,1)}, bf16[1,1024,128]{2,1,0:T(8,128)(2,1)S(1)}, u32[]{:S(2)}) copy-start(bf16[1,1024,128]{2,1,0:T(8,128)(2,1)S(1)} %collective-permute-done.5.h_ref) | copy-start | bytes 786436
  76.8 1.3 copy-start.9
  78.2 0.7 copy-start.10
  98.3 31.7 %copy-start.2 = (bf16[128,32,128]{2,1,0:T(8,128)(2,1)}, bf16[128,32,128]{2,1,0:T(8,128)(2,1)S(1)}, u32[]{:S(2)}) copy-start(bf16[128,32,128]{2,1,0:T(8,128)(2,1)S(1)} %all-to-all-done.q_ref) | copy-start | bytes 3145732
  98.3 51.1 %all-to-all-start.4 = ((bf16[128,32,128]{2,1,0:T(8,128)(2,1)}), bf16[128,32,128]{2,1,0:T(8,128)(2,1)S(1)}, u32[]{:S(2)}, u32[]{:S(2)}) async-start(bf16[128,32,128]{2,1,0:T(8,128)(2,1)} %attn.3), calls=%async_computation.4 | async-start | bytes 2097152 | tf_op jit(solution)/shard_map/all_to_all | solution.py:240
  149.4 29.1 %all-to-all-start.2 = ((bf16[128,32,128]{2,1,0:T(8,128)(2,1)}), bf16[128,32,128]{2,1,0:T(8,128)(2,1)S(1)}, u32[]{:S(2)}, u32[]{:S(2)}) async-start(bf16[128,32,128]{2,1,0:T(8,128)(2,1)} %attn.2), calls=%async_computation.2 | async-start | bytes 2097152 | tf_op jit(solution)/shard_map/all_to_all | solution.py:240

commit v7 on v5

--- a/solution.py
+++ b/solution.py
@@ -48,7 +48,8 @@
     return pl.pallas_call(
         kernel, out_shape=jax.ShapeDtypeStruct((2 * heads, 2, rows, width), jnp.bfloat16),
         scratch_shapes=[wide, wide], name="pair",
-    )(keys, values, cosine, signed_sine)
+        compiler_params=pltpu.CompilerParams(vmem_limit_bytes=16 * 2**20),
+    )(*(pltpu.with_memory_space_constraint(a, pltpu.HBM) for a in (keys, values)), cosine, signed_sine)
 
 
 def prepare_queries(queries, cosine, signed_sine, group):
@@ -81,6 +82,7 @@
     c = LOG2E / math.sqrt(D)
     devs = bq // strip
     nd = devs * period // BK
+    tiles = G // devs
     w = bq // nd
     offset = which * strip
     groups = GROUPS[nd]
@@ -91,9 +93,13 @@
         qi = pl.program_id(0)
         first = qi * nd
 
+        def queries_in(n):
+            part = pl.ds(n * devs, devs)
+            return pltpu.make_async_copy(q_ref.at[part], qv_ref.at[part], sems.at[blocks + n])
+
         @pl.when(qi == 0)
         def _():
-            pltpu.make_async_copy(q_ref, qv_ref, sems.at[blocks]).start()
+            queries_in(0).start()
             x, core = where_ref[0], where_ref[1]
             for plane in range(4):
                 for step, refs in ((0, (c_ref, cc_ref)), (3, (u_ref, cu_ref)), (1, (v_ref, cv_ref)),
@@ -106,9 +112,10 @@
                                 b = plane * 4 + yl * 2 + lax.rem(core + other, 2)
                                 pltpu.make_async_copy(src, kv_ref.at[b], sems.at[b]).start()
 
-        @pl.when(qi == 0)
-        def _():
-            pltpu.make_async_copy(q_ref, qv_ref, sems.at[blocks]).wait()
+            for n in range(1, tiles):
+                queries_in(n).start()
+
+        queries_in(qi).wait()
 
         def landed(t):
             pltpu.make_async_copy(c_ref.at[0], kv_ref.at[first + t], sems.at[first + t]).wait()
@@ -186,7 +193,7 @@
         scratch_shapes=[pltpu.VMEM((D, bq), jnp.bfloat16), pltpu.VMEM((D, bq), jnp.float32),
                         pltpu.VMEM((8, bq), jnp.float32), pltpu.VMEM((blocks, 2 * BK, D), jnp.bfloat16),
                         pltpu.VMEM((G, strip, D), jnp.bfloat16),
-                        pltpu.SemaphoreType.DMA((blocks + 1,))],
+                        pltpu.SemaphoreType.DMA((blocks + tiles,))],
         compiler_params=pltpu.CompilerParams(vmem_limit_bytes=24 * 2**20),
         name="attn",
     )(where, *(pltpu.with_memory_space_constraint(piece, pltpu.HBM) for piece in (q, *pieces)))

time: 183 us -> 182 us (level)
  no operation moved by 1% of the time
where the time goes in v7:
time: 182 us; the launch traced here: 181 us
  starting transfers between devices  70.7 us (39%)
  waiting for transfers between devices  55.7 us (31%)
  Pallas kernels  47.9 us (26%)
  local copies, waits for them, and re-layouts  6.2 us (3%)
    all_to_all x2, starting transfers between devices, shards(): back = lax.all_to_all(done, AXES, split_axis=0, concat_axis=0, tiled=True)  41.1 us
    pallas_call x2, Pallas kernels, attn(): pl.pallas_call(kernel, grid=(G // devs,), in_specs=[pl.BlockSpec(memory_s...  38.4 us
    all_to_all x2, waiting for transfers between devices, shards(): back = lax.all_to_all(done, AXES, split_axis=0, concat_axis=0, tiled=True)  19 us
    ppermute x4, waiting for transfers between devices, shards(): far.append(lax.ppermute(source[half:half + 1], 'x', way))  17.3 us
    all_to_all x2, waiting for transfers between devices, shards(): lax.all_to_all(ordered[n], AXES, split_axis=0, concat_axis=0, tiled=True)  16.9 us
    all_to_all x2, starting transfers between devices, shards(): lax.all_to_all(ordered[n], AXES, split_axis=0, concat_axis=0, tiled=True)  12.2 us
    all_to_all x1, starting transfers between devices, shards(): lax.all_to_all(pair, ('yl', 'sy'), split_axis=0, concat_axis=0, tiled=True)  8.59 us
    pallas_call x1, Pallas kernels, prepare_queries(): pl.pallas_call(kernel, grid=(heads // group,), in_specs=[pl.BlockSpec((ro...  7.2 us
  transfers between devices with their start and end apart: 14, of which 10 were waited for; matrix products, arithmetic and copies ran while one was open for 1% of the time, Pallas kernels for 25%

profile of v7, /device:TPU:1, one launch (start us, length us, event | category | flops | bytes accessed | tf_op | source)
XLA Modules:
  0.0 181.2 jit_solution(11052759904396919846)
XLA Ops:
  0.1 0.1 mul.58
  0.1 0.2 fusion
  0.4 2.3 %pair.1 = bf16[16,2,64,128]{3,2,1,0:T(8,128)(2,1)} custom-call(bf16[64,8,128]{2,1,0:T(8,128)(2,1)} %k_ref.1, bf16[64,8,128]{2,1,0:T(8,128)(2,1)} %v_ref.1, f32[64,128]{1,0:T(8,128)S(1)} %get-tuple-element.12.cos_ref, f32[64,128]{1,0:T(8,128)S(1)} %get-tuple-element.11.sin_ref), custom_call_target="tpu_custom_call" | custom-call | tf_op jit(solution)/shard_map/pair/pallas_call | solution.py:48
  2.7 8.6 %all-to-all-start.1 = ((bf16[16,2,64,128]{3,2,1,0:T(8,128)(2,1)}), bf16[16,2,64,128]{3,2,1,0:T(8,128)(2,1)S(1)}, u32[]{:S(2)}, u32[]{:S(2)}) async-start(bf16[16,2,64,128]{3,2,1,0:T(8,128)(2,1)} %pair.1), calls=%async_computation.1 | async-start | bytes 1048576 | tf_op jit(solution)/shard_map/all_to_all | solution.py:215
  11.3 7.2 %queries.1 = (bf16[16,8,32,128]{3,2,1,0:T(8,128)(2,1)}, bf16[16,8,32,128]{3,2,1,0:T(8,128)(2,1)}) custom-call(bf16[64,128,128]{2,1,0:T(8,128)(2,1)} %q_ref.1, f32[64,128]{1,0:T(8,128)} %copy-done.1, f32[64,128]{1,0:T(8,128)} %copy-done), custom_call_target="tpu_custom_call" | custom-call | tf_op jit(solution)/shard_map/queries/pallas_call | solution.py:68
  18.5 2.0 %all-to-all-done.1 = bf16[16,2,64,128]{3,2,1,0:T(8,128)(2,1)S(1)} async-done(((bf16[16,2,64,128]{3,2,1,0:T(8,128)(2,1)}), bf16[16,2,64,128]{3,2,1,0:T(8,128)(2,1)S(1)}, u32[]{:S(2)}, u32[]{:S(2)}) %all-to-all-start.1) | async-done | bytes 524320 | tf_op jit(solution)/shard_map/all_to_all | solution.py:215
  20.5 8.3 %all-to-all-start.3 = ((bf16[128,32,128]{2,1,0:T(8,128)(2,1)}), bf16[128,32,128]{2,1,0:T(8,128)(2,1)S(1)}, u32[]{:S(2)}, u32[]{:S(2)}) async-start(bf16[128,32,128]{2,1,0:T(8,128)(2,1)} %bitcast.24), calls=%async_computation.3 | async-start | bytes 2097152 | tf_op jit(solution)/shard_map/all_to_all | solution.py:237
  28.8 0.2 copy.4
  29.0 2.6 %collective-permute-start.3 = (bf16[2,1024,128]{2,1,0:T(8,128)(2,1)S(1)}, bf16[2,1024,128]{2,1,0:T(8,128)(2,1)S(1)}, u32[]{:S(2)}, u32[]{:S(2)}) collective-permute-start(bf16[2,1024,128]{2,1,0:T(8,128)(2,1)S(1)} %pad_maximum_fusion.c_ref), channel_id=1, source_target_pairs={{0,96},{32,0},{64,32},{96,64},{1,97},{33,1},{65,33},{97,65},{2,98}... | collective-permute-start | bytes 1572872 | tf_op jit(solution)/shard_map/ppermute | solution.py:224
  31.7 0.0 collective-permute-start.1
  31.7 16.9 %all-to-all-done.3.q_ref = bf16[128,32,128]{2,1,0:T(8,128)(2,1)S(1)} async-done(((bf16[128,32,128]{2,1,0:T(8,128)(2,1)}), bf16[128,32,128]{2,1,0:T(8,128)(2,1)S(1)}, u32[]{:S(2)}, u32[]{:S(2)}) %all-to-all-start.3) | async-done | bytes 1048608 | tf_op jit(solution)/shard_map/all_to_all | solution.py:237
  48.5 3.9 %all-to-all-start = ((bf16[128,32,128]{2,1,0:T(8,128)(2,1)}), bf16[128,32,128]{2,1,0:T(8,128)(2,1)S(1)}, u32[]{:S(2)}, u32[]{:S(2)}) async-start(bf16[128,32,128]{2,1,0:T(8,128)(2,1)} %bitcast.23), calls=%async_computation | async-start | bytes 2097152 | tf_op jit(solution)/shard_map/all_to_all | solution.py:237
  52.5 0.2 collective-permute-done.3.v_ref
  52.7 1.0 collective-permute-start.4
  53.7 0.3 collective-permute-done.1.u_ref
  54.0 0.9 collective-permute-start.2
  54.9 0.0 collective-permute-start
  54.9 1.3 collective-permute-start.7
  56.1 1.0 slice.28
  57.1 0.3 collective-permute-start.5
  57.5 0.0 collective-permute-done.4.cv_ref
  57.5 2.5 %collective-permute-start.8 = (bf16[1,1024,128]{2,1,0:T(8,128)(2,1)S(1)}, bf16[1,1024,128]{2,1,0:T(8,128)(2,1)S(1)}, u32[]{:S(2)}, u32[]{:S(2)}) collective-permute-start(bf16[1,1024,128]{2,1,0:T(8,128)(2,1)S(1)} %slice.31), channel_id=1, source_target_pairs={{0,96},{32,0},{64,32},{96,64},{1,97},{33,1},{65,33},{97,65},{2,98}... | collective-permute-start | bytes 786440 | tf_op jit(solution)/shard_map/ppermute | solution.py:230
  60.0 0.0 collective-permute-done.2.cu_ref
  60.0 0.3 collective-permute-start.6
  60.3 0.1 pad_add_fusion.where_ref
  60.4 0.0 collective-permute-done.cc_ref
  60.4 10.3 %collective-permute-done.7.g_ref = bf16[1,1024,128]{2,1,0:T(8,128)(2,1)S(1)} collective-permute-done((bf16[1,1024,128]{2,1,0:T(8,128)(2,1)S(1)}, bf16[1,1024,128]{2,1,0:T(8,128)(2,1)S(1)}, u32[]{:S(2)}, u32[]{:S(2)}) %collective-permute-start.7) | collective-permute-done | bytes 262176 | tf_op jit(solution)/shard_map/ppermute | solution.py:230
  70.7 1.3 collective-permute-done.5.h_ref
  72.0 4.3 %collective-permute-done.8.cg_ref = bf16[1,1024,128]{2,1,0:T(8,128)(2,1)S(1)} collective-permute-done((bf16[1,1024,128]{2,1,0:T(8,128)(2,1)S(1)}, bf16[1,1024,128]{2,1,0:T(8,128)(2,1)S(1)}, u32[]{:S(2)}, u32[]{:S(2)}) %collective-permute-start.8) | collective-permute-done | bytes 262176 | tf_op jit(solution)/shard_map/ppermute | solution.py:230
  76.3 1.3 collective-permute-done.6.ch_ref
  77.6 0.0 copy-done.8
  77.6 0.0 copy-done.9
  77.6 0.0 copy-done.10
  77.7 0.0 copy-done.11
  77.7 0.0 copy-start.12
  77.7 0.7 copy-done.12
  78.4 19.2 %attn.3 = bf16[128,32,128]{2,1,0:T(8,128)(2,1)} custom-call(s32[2]{0:T(128)S(1)} %pad_add_fusion.where_ref, bf16[128,32,128]{2,1,0:T(8,128)(2,1)} %copy-done.3, bf16[2,1024,128]{2,1,0:T(8,128)(2,1)} %copy-done.2, bf16[2,1024,128]{2,1,0:T(8,128)(2,1)} %copy-done.8, bf16[2,1024,128]{2,1,0:T(8,128)(2,1)} %collective-permute-done.1.u_ref, ...), custom_call_target="tpu_custom_call" | custom-call | tf_op jit(solution)/shard_map/attn/pallas_call | solution.py:187
  97.6 0.0 all-to-all-done.q_ref
  97.6 0.0 copy-start.4
  97.6 31.7 %all-to-all-start.4 = ((bf16[128,32,128]{2,1,0:T(8,128)(2,1)}), bf16[128,32,128]{2,1,0:T(8,128)(2,1)S(1)}, u32[]{:S(2)}, u32[]{:S(2)}) async-start(bf16[128,32,128]{2,1,0:T(8,128)(2,1)} %attn.3), calls=%async_computation.4 | async-start | bytes 2097152 | tf_op jit(solution)/shard_map/all_to_all | solution.py:241
  129.3 19.2 %attn.2 = bf16[128,32,128]{2,1,0:T(8,128)(2,1)} custom-call(s32[2]{0:T(128)S(1)} %pad_add_fusion.where_ref, bf16[128,32,128]{2,1,0:T(8,128)(2,1)} %copy-done.4, bf16[2,1024,128]{2,1,0:T(8,128)(2,1)} %copy-done.2, bf16[2,1024,128]{2,1,0:T(8,128)(2,1)} %copy-done.8, bf16[2,1024,128]{2,1,0:T(8,128)(2,1)} %collective-permute-done.1.u_ref, ...), custom_call_target="tpu_custom_call" | custom-call | tf_op jit(solution)/shard_map/attn/pallas_call | solution.py:187
  148.6 0.2 all-to-all-done.4
  148.8 9.5 %all-to-all-start.2 = ((bf16[128,32,128]{2,1,0:T(8,128)(2,1)}), bf16[128,32,128]{2,1,0:T(8,128)(2,1)S(1)}, u32[]{:S(2)}, u32[]{:S(2)}) async-start(bf16[128,32,128]{2,1,0:T(8,128)(2,1)} %attn.2), calls=%async_computation.2 | async-start | bytes 2097152 | tf_op jit(solution)/shard_map/all_to_all | solution.py:241
  158.3 0.7 copy.6
  158.9 18.8 %all-to-all-done.2 = bf16[128,32,128]{2,1,0:T(8,128)(2,1)S(1)} async-done(((bf16[128,32,128]{2,1,0:T(8,128)(2,1)}), bf16[128,32,128]{2,1,0:T(8,128)(2,1)S(1)}, u32[]{:S(2)}, u32[]{:S(2)}) %all-to-all-start.2) | async-done | bytes 1048608 | tf_op jit(solution)/shard_map/all_to_all | solution.py:241
  177.7 0.7 copy.5
  178.4 1.7 pad.4
  180.1 1.0 constant_dynamic-update-slice_fusion
  (28 shorter events, 0.2 us)
Async XLA Ops:
  0.4 10.9 %copy-start = (f32[64,128]{1,0:T(8,128)}, f32[64,128]{1,0:T(8,128)S(1)}, u32[]{:S(2)}) copy-start(f32[64,128]{1,0:T(8,128)S(1)} %get-tuple-element.11.sin_ref) | copy-start | bytes 98308
  0.4 10.9 %copy-start.1 = (f32[64,128]{1,0:T(8,128)}, f32[64,128]{1,0:T(8,128)S(1)}, u32[]{:S(2)}) copy-start(f32[64,128]{1,0:T(8,128)S(1)} %get-tuple-element.12.cos_ref) | copy-start | bytes 98308
  2.7 17.8 %all-to-all-start.1 = ((bf16[16,2,64,128]{3,2,1,0:T(8,128)(2,1)}), bf16[16,2,64,128]{3,2,1,0:T(8,128)(2,1)S(1)}, u32[]{:S(2)}, u32[]{:S(2)}) async-start(bf16[16,2,64,128]{3,2,1,0:T(8,128)(2,1)} %pair.1), calls=%async_computation.1 | async-start | bytes 1048576 | tf_op jit(solution)/shard_map/all_to_all | solution.py:215
  20.5 28.1 %all-to-all-start.3 = ((bf16[128,32,128]{2,1,0:T(8,128)(2,1)}), bf16[128,32,128]{2,1,0:T(8,128)(2,1)S(1)}, u32[]{:S(2)}, u32[]{:S(2)}) async-start(bf16[128,32,128]{2,1,0:T(8,128)(2,1)} %bitcast.24), calls=%async_computation.3 | async-start | bytes 2097152 | tf_op jit(solution)/shard_map/all_to_all | solution.py:237
  29.0 31.0 %copy-start.2 = (bf16[2,1024,128]{2,1,0:T(8,128)(2,1)}, bf16[2,1024,128]{2,1,0:T(8,128)(2,1)S(1)}, u32[]{:S(2)}) copy-start(bf16[2,1024,128]{2,1,0:T(8,128)(2,1)S(1)} %pad_maximum_fusion.c_ref) | copy-start | bytes 1572868
  29.0 23.7 %collective-permute-start.3 = (bf16[2,1024,128]{2,1,0:T(8,128)(2,1)S(1)}, bf16[2,1024,128]{2,1,0:T(8,128)(2,1)S(1)}, u32[]{:S(2)}, u32[]{:S(2)}) collective-permute-start(bf16[2,1024,128]{2,1,0:T(8,128)(2,1)S(1)} %pad_maximum_fusion.c_ref), channel_id=1, source_target_pairs={{0,96},{32,0},{64,32},{96,64},{1,97},{33,1},{65,33},{97,65},{2,98}... | collective-permute-start | bytes 1572872 | tf_op jit(solution)/shard_map/ppermute | solution.py:224
  31.7 22.3 %collective-permute-start.1 = (bf16[2,1024,128]{2,1,0:T(8,128)(2,1)S(1)}, bf16[2,1024,128]{2,1,0:T(8,128)(2,1)}, u32[]{:S(2)}, u32[]{:S(2)}) collective-permute-start(bf16[2,1024,128]{2,1,0:T(8,128)(2,1)S(1)} %pad_maximum_fusion.c_ref), channel_id=1, source_target_pairs={{0,32},{32,64},{64,96},{96,0},{1,33},{33,65},{65,97},{97,1},{2,34}... | collective-permute-start | bytes 1572872 | tf_op jit(solution)/shard_map/ppermute | solution.py:223
  48.5 11.5 %copy-start.3 = (bf16[128,32,128]{2,1,0:T(8,128)(2,1)}, bf16[128,32,128]{2,1,0:T(8,128)(2,1)S(1)}, u32[]{:S(2)}) copy-start(bf16[128,32,128]{2,1,0:T(8,128)(2,1)S(1)} %all-to-all-done.3.q_ref) | copy-start | bytes 3145732
  48.5 49.0 %all-to-all-start = ((bf16[128,32,128]{2,1,0:T(8,128)(2,1)}), bf16[128,32,128]{2,1,0:T(8,128)(2,1)S(1)}, u32[]{:S(2)}, u32[]{:S(2)}) async-start(bf16[128,32,128]{2,1,0:T(8,128)(2,1)} %bitcast.23), calls=%async_computation | async-start | bytes 2097152 | tf_op jit(solution)/shard_map/all_to_all | solution.py:237
  52.7 24.9 %copy-start.5 = (bf16[2,1024,128]{2,1,0:T(8,128)(2,1)}, bf16[2,1024,128]{2,1,0:T(8,128)(2,1)S(1)}, u32[]{:S(2)}) copy-start(bf16[2,1024,128]{2,1,0:T(8,128)(2,1)S(1)} %collective-permute-done.3.v_ref) | copy-start | bytes 1572868
  52.7 4.8 %collective-permute-start.4 = (bf16[2,1024,128]{2,1,0:T(8,128)(2,1)S(1)}, bf16[2,1024,128]{2,1,0:T(8,128)(2,1)S(1)}, u32[]{:S(2)}, u32[]{:S(2)}) collective-permute-start(bf16[2,1024,128]{2,1,0:T(8,128)(2,1)S(1)} %collective-permute-done.3.v_ref), channel_id=1, source_target_pairs={{0,8},{8,0},{1,9},{9,1},{2,10},{10,2},{3,11},{11,3},{4,12},{12,4},... | collective-permute-start | bytes 1572872 | tf_op jit(solution)/shard_map/ppermute | solution.py:227
  54.0 6.0 %collective-permute-start.2 = (bf16[2,1024,128]{2,1,0:T(8,128)(2,1)}, bf16[2,1024,128]{2,1,0:T(8,128)(2,1)S(1)}, u32[]{:S(2)}, u32[]{:S(2)}) collective-permute-start(bf16[2,1024,128]{2,1,0:T(8,128)(2,1)} %collective-permute-done.1.u_ref), channel_id=1, source_target_pairs={{0,8},{8,0},{1,9},{9,1},{2,10},{10,2},{3,11},{11,3},{4,12},{12,4},... | collective-permute-start | bytes 1572872 | tf_op jit(solution)/shard_map/ppermute | solution.py:227
  54.9 5.5 %collective-permute-start = (bf16[2,1024,128]{2,1,0:T(8,128)(2,1)S(1)}, bf16[2,1024,128]{2,1,0:T(8,128)(2,1)S(1)}, u32[]{:S(2)}, u32[]{:S(2)}) collective-permute-start(bf16[2,1024,128]{2,1,0:T(8,128)(2,1)S(1)} %pad_maximum_fusion.c_ref), channel_id=1, source_target_pairs={{0,8},{8,0},{1,9},{9,1},{2,10},{10,2},{3,11},{11,3},{4,12},{12,4},... | collective-permute-start | bytes 1572872 | tf_op jit(solution)/shard_map/ppermute | solution.py:227
  54.9 15.8 %collective-permute-start.7 = (bf16[1,1024,128]{2,1,0:T(8,128)(2,1)S(1)}, bf16[1,1024,128]{2,1,0:T(8,128)(2,1)S(1)}, u32[]{:S(2)}, u32[]{:S(2)}) collective-permute-start(bf16[1,1024,128]{2,1,0:T(8,128)(2,1)S(1)} %slice.30), channel_id=1, source_target_pairs={{0,96},{32,0},{64,32},{96,64},{1,97},{33,1},{65,33},{97,65},{2,98}... | collective-permute-start | bytes 786440 | tf_op jit(solution)/shard_map/ppermute | solution.py:230
  57.1 14.9 %collective-permute-start.5 = (bf16[1,1024,128]{2,1,0:T(8,128)(2,1)S(1)}, bf16[1,1024,128]{2,1,0:T(8,128)(2,1)S(1)}, u32[]{:S(2)}, u32[]{:S(2)}) collective-permute-start(bf16[1,1024,128]{2,1,0:T(8,128)(2,1)S(1)} %slice.28), channel_id=1, source_target_pairs={{0,32},{32,64},{64,96},{96,0},{1,33},{33,65},{65,97},{97,1},{2,34}... | collective-permute-start | bytes 786440 | tf_op jit(solution)/shard_map/ppermute | solution.py:230
  57.5 20.2 %copy-start.6 = (bf16[2,1024,128]{2,1,0:T(8,128)(2,1)}, bf16[2,1024,128]{2,1,0:T(8,128)(2,1)S(1)}, u32[]{:S(2)}) copy-start(bf16[2,1024,128]{2,1,0:T(8,128)(2,1)S(1)} %collective-permute-done.4.cv_ref) | copy-start | bytes 1572868
  57.5 18.8 %collective-permute-start.8 = (bf16[1,1024,128]{2,1,0:T(8,128)(2,1)S(1)}, bf16[1,1024,128]{2,1,0:T(8,128)(2,1)S(1)}, u32[]{:S(2)}, u32[]{:S(2)}) collective-permute-start(bf16[1,1024,128]{2,1,0:T(8,128)(2,1)S(1)} %slice.31), channel_id=1, source_target_pairs={{0,96},{32,0},{64,32},{96,64},{1,97},{33,1},{65,33},{97,65},{2,98}... | collective-permute-start | bytes 786440 | tf_op jit(solution)/shard_map/ppermute | solution.py:230
  60.0 17.7 %copy-start.7 = (bf16[2,1024,128]{2,1,0:T(8,128)(2,1)}, bf16[2,1024,128]{2,1,0:T(8,128)(2,1)S(1)}, u32[]{:S(2)}) copy-start(bf16[2,1024,128]{2,1,0:T(8,128)(2,1)S(1)} %collective-permute-done.2.cu_ref) | copy-start | bytes 1572868
  60.0 17.6 %collective-permute-start.6 = (bf16[1,1024,128]{2,1,0:T(8,128)(2,1)S(1)}, bf16[1,1024,128]{2,1,0:T(8,128)(2,1)S(1)}, u32[]{:S(2)}, u32[]{:S(2)}) collective-permute-start(bf16[1,1024,128]{2,1,0:T(8,128)(2,1)S(1)} %slice.29), channel_id=1, source_target_pairs={{0,32},{32,64},{64,96},{96,0},{1,33},{33,65},{65,97},{97,1},{2,34}... | collective-permute-start | bytes 786440 | tf_op jit(solution)/shard_map/ppermute | solution.py:230
  60.4 17.3 %copy-start.8 = (bf16[2,1024,128]{2,1,0:T(8,128)(2,1)}, bf16[2,1024,128]{2,1,0:T(8,128)(2,1)S(1)}, u32[]{:S(2)}) copy-start(bf16[2,1024,128]{2,1,0:T(8,128)(2,1)S(1)} %collective-permute-done.cc_ref) | copy-start | bytes 1572868
  70.7 6.9 %copy-start.9 = (bf16[1,1024,128]{2,1,0:T(8,128)(2,1)}, bf16[1,1024,128]{2,1,0:T(8,128)(2,1)S(1)}, u32[]{:S(2)}) copy-start(bf16[1,1024,128]{2,1,0:T(8,128)(2,1)S(1)} %collective-permute-done.7.g_ref) | copy-start | bytes 786436
  72.0 5.7 %copy-start.10 = (bf16[1,1024,128]{2,1,0:T(8,128)(2,1)}, bf16[1,1024,128]{2,1,0:T(8,128)(2,1)S(1)}, u32[]{:S(2)}) copy-start(bf16[1,1024,128]{2,1,0:T(8,128)(2,1)S(1)} %collective-permute-done.5.h_ref) | copy-start | bytes 786436
  76.3 1.3 copy-start.11
  77.7 0.7 copy-start.12
  97.6 31.7 %copy-start.4 = (bf16[128,32,128]{2,1,0:T(8,128)(2,1)}, bf16[128,32,128]{2,1,0:T(8,128)(2,1)S(1)}, u32[]{:S(2)}) copy-start(bf16[128,32,128]{2,1,0:T(8,128)(2,1)S(1)} %all-to-all-done.q_ref) | copy-start | bytes 3145732
  97.6 51.2 %all-to-all-start.4 = ((bf16[128,32,128]{2,1,0:T(8,128)(2,1)}), bf16[128,32,128]{2,1,0:T(8,128)(2,1)S(1)}, u32[]{:S(2)}, u32[]{:S(2)}) async-start(bf16[128,32,128]{2,1,0:T(8,128)(2,1)} %attn.3), calls=%async_computation.4 | async-start | bytes 2097152 | tf_op jit(solution)/shard_map/all_to_all | solution.py:241
  148.8 29.0 %all-to-all-start.2 = ((bf16[128,32,128]{2,1,0:T(8,128)(2,1)}), bf16[128,32,128]{2,1,0:T(8,128)(2,1)S(1)}, u32[]{:S(2)}, u32[]{:S(2)}) async-start(bf16[128,32,128]{2,1,0:T(8,128)(2,1)} %attn.2), calls=%async_computation.2 | async-start | bytes 2097152 | tf_op jit(solution)/shard_map/all_to_all | solution.py:241

commit v8 on v6

--- a/solution.py
+++ b/solution.py
@@ -54,7 +54,8 @@
     return pl.pallas_call(
         kernel, out_shape=jax.ShapeDtypeStruct((2 * heads, 2, rows, width), jnp.bfloat16),
         scratch_shapes=[wide, wide], name="pair",
-    )(keys, values, cosine, sine)
+        compiler_params=pltpu.CompilerParams(vmem_limit_bytes=16 * 2**20),
+    )(*(pltpu.with_memory_space_constraint(a, pltpu.HBM) for a in (keys, values)), cosine, sine)
 
 
 def prepare_queries(queries, cosine, sine, group):
@@ -88,6 +89,7 @@
     c = LOG2E / math.sqrt(D)
     devs = bq // strip
     nd = devs * period // BK
+    tiles = G // devs
     w = bq // nd
     offset = which * strip
     groups = GROUPS[nd]
@@ -98,9 +100,13 @@
         qi = pl.program_id(0)
         first = qi * nd
 
+        def queries_in(n):
+            part = pl.ds(n * devs, devs)
+            return pltpu.make_async_copy(q_ref.at[part], qv_ref.at[part], sems.at[blocks + n])
+
         @pl.when(qi == 0)
         def _():
-            pltpu.make_async_copy(q_ref, qv_ref, sems.at[blocks]).start()
+            queries_in(0).start()
             x, core = where_ref[0], where_ref[1]
             for plane in range(4):
                 for step, refs in ((0, (c_ref, cc_ref)), (3, (u_ref, cu_ref)), (1, (v_ref, cv_ref)),
@@ -113,9 +119,10 @@
                                 b = plane * 4 + yl * 2 + lax.rem(core + other, 2)
                                 pltpu.make_async_copy(src, kv_ref.at[b], sems.at[b]).start()
 
-        @pl.when(qi == 0)
-        def _():
-            pltpu.make_async_copy(q_ref, qv_ref, sems.at[blocks]).wait()
+            for n in range(1, tiles):
+                queries_in(n).start()
+
+        queries_in(qi).wait()
 
         def landed(t):
             pltpu.make_async_copy(c_ref.at[0], kv_ref.at[first + t], sems.at[first + t]).wait()
@@ -193,7 +200,7 @@
         scratch_shapes=[pltpu.VMEM((D, bq), jnp.bfloat16), pltpu.VMEM((D, bq), jnp.float32),
                         pltpu.VMEM((8, bq), jnp.float32), pltpu.VMEM((blocks, 2 * BK, D), jnp.bfloat16),
                         pltpu.VMEM((G, strip, D), jnp.bfloat16),
-                        pltpu.SemaphoreType.DMA((blocks + 1,))],
+                        pltpu.SemaphoreType.DMA((blocks + tiles,))],
         compiler_params=pltpu.CompilerParams(vmem_limit_bytes=24 * 2**20),
         name="attn",
     )(where, *(pltpu.with_memory_space_constraint(piece, pltpu.HBM) for piece in (q, *pieces)))

time: 183 us -> 182 us (level)
  no operation moved by 1% of the time
where the time goes in v8:
time: 182 us; the launch traced here: 181 us
  starting transfers between devices  70.7 us (39%)
  waiting for transfers between devices  55.7 us (31%)
  Pallas kernels  47.9 us (26%)
  local copies, waits for them, and re-layouts  6.11 us (3%)
    all_to_all x2, starting transfers between devices, shards(): back = lax.all_to_all(done, AXES, split_axis=0, concat_axis=0, tiled=True)  41.1 us
    pallas_call x2, Pallas kernels, attn(): pl.pallas_call(kernel, grid=(G // devs,), in_specs=[pl.BlockSpec(memory_s...  38.4 us
    all_to_all x2, waiting for transfers between devices, shards(): back = lax.all_to_all(done, AXES, split_axis=0, concat_axis=0, tiled=True)  19 us
    ppermute x4, waiting for transfers between devices, shards(): far.append(lax.ppermute(source[half:half + 1], 'x', way))  17.3 us
    all_to_all x2, waiting for transfers between devices, shards(): lax.all_to_all(ordered[n], AXES, split_axis=0, concat_axis=0, tiled=True)  16.9 us
    all_to_all x2, starting transfers between devices, shards(): lax.all_to_all(ordered[n], AXES, split_axis=0, concat_axis=0, tiled=True)  12.2 us
    all_to_all x1, starting transfers between devices, shards(): lax.all_to_all(pair, ('yl', 'sy'), split_axis=0, concat_axis=0, tiled=True)  8.59 us
    pallas_call x1, Pallas kernels, prepare_queries(): pl.pallas_call(kernel, grid=(heads // group,), in_specs=[pl.BlockSpec((ro...  7.22 us
  transfers between devices with their start and end apart: 14, of which 10 were waited for; matrix products, arithmetic and copies ran while one was open for 1% of the time, Pallas kernels for 25%

profile of v8, /device:TPU:1, one launch (start us, length us, event | category | flops | bytes accessed | tf_op | source)
XLA Modules:
  0.0 181.1 jit_solution(4390844443877380053)
XLA Ops:
  0.0 0.2 multiply_sine_fusion
  0.2 0.0 copy-start
  0.3 0.0 copy-start.1
  0.3 2.3 %pair.1 = bf16[16,2,64,128]{3,2,1,0:T(8,128)(2,1)} custom-call(bf16[64,8,128]{2,1,0:T(8,128)(2,1)} %k_ref.1, bf16[64,8,128]{2,1,0:T(8,128)(2,1)} %v_ref.1, f32[64,64]{1,0:T(8,128)S(1)} %get-tuple-element.12.cos_ref, f32[64,64]{1,0:T(8,128)S(1)} %get-tuple-element.11.sin_ref), custom_call_target="tpu_custom_call" | custom-call | tf_op jit(solution)/shard_map/pair/pallas_call | solution.py:54
  2.6 8.6 %all-to-all-start.1 = ((bf16[16,2,64,128]{3,2,1,0:T(8,128)(2,1)}), bf16[16,2,64,128]{3,2,1,0:T(8,128)(2,1)S(1)}, u32[]{:S(2)}, u32[]{:S(2)}) async-start(bf16[16,2,64,128]{3,2,1,0:T(8,128)(2,1)} %pair.1), calls=%async_computation.1 | async-start | bytes 1048576 | tf_op jit(solution)/shard_map/all_to_all | solution.py:221
  11.2 0.0 copy-done
  11.2 7.2 %queries.1 = (bf16[16,8,32,128]{3,2,1,0:T(8,128)(2,1)}, bf16[16,8,32,128]{3,2,1,0:T(8,128)(2,1)}) custom-call(bf16[64,128,128]{2,1,0:T(8,128)(2,1)} %q_ref.1, f32[64,64]{1,0:T(8,128)} %copy-done.1, f32[64,64]{1,0:T(8,128)} %copy-done), custom_call_target="tpu_custom_call" | custom-call | tf_op jit(solution)/shard_map/queries/pallas_call | solution.py:75
  18.4 2.0 %all-to-all-done.1 = bf16[16,2,64,128]{3,2,1,0:T(8,128)(2,1)S(1)} async-done(((bf16[16,2,64,128]{3,2,1,0:T(8,128)(2,1)}), bf16[16,2,64,128]{3,2,1,0:T(8,128)(2,1)S(1)}, u32[]{:S(2)}, u32[]{:S(2)}) %all-to-all-start.1) | async-done | bytes 524320 | tf_op jit(solution)/shard_map/all_to_all | solution.py:221
  20.4 8.3 %all-to-all-start.3 = ((bf16[128,32,128]{2,1,0:T(8,128)(2,1)}), bf16[128,32,128]{2,1,0:T(8,128)(2,1)S(1)}, u32[]{:S(2)}, u32[]{:S(2)}) async-start(bf16[128,32,128]{2,1,0:T(8,128)(2,1)} %bitcast.24), calls=%async_computation.3 | async-start | bytes 2097152 | tf_op jit(solution)/shard_map/all_to_all | solution.py:243
  28.7 0.2 copy.4
  28.9 2.6 %collective-permute-start.3 = (bf16[2,1024,128]{2,1,0:T(8,128)(2,1)S(1)}, bf16[2,1024,128]{2,1,0:T(8,128)(2,1)S(1)}, u32[]{:S(2)}, u32[]{:S(2)}) collective-permute-start(bf16[2,1024,128]{2,1,0:T(8,128)(2,1)S(1)} %pad_maximum_fusion.c_ref), channel_id=1, source_target_pairs={{0,96},{32,0},{64,32},{96,64},{1,97},{33,1},{65,33},{97,65},{2,98}... | collective-permute-start | bytes 1572872 | tf_op jit(solution)/shard_map/ppermute | solution.py:230
  31.6 0.0 collective-permute-start.1
  31.6 16.9 %all-to-all-done.3.q_ref = bf16[128,32,128]{2,1,0:T(8,128)(2,1)S(1)} async-done(((bf16[128,32,128]{2,1,0:T(8,128)(2,1)}), bf16[128,32,128]{2,1,0:T(8,128)(2,1)S(1)}, u32[]{:S(2)}, u32[]{:S(2)}) %all-to-all-start.3) | async-done | bytes 1048608 | tf_op jit(solution)/shard_map/all_to_all | solution.py:243
  48.4 3.9 %all-to-all-start = ((bf16[128,32,128]{2,1,0:T(8,128)(2,1)}), bf16[128,32,128]{2,1,0:T(8,128)(2,1)S(1)}, u32[]{:S(2)}, u32[]{:S(2)}) async-start(bf16[128,32,128]{2,1,0:T(8,128)(2,1)} %bitcast.23), calls=%async_computation | async-start | bytes 2097152 | tf_op jit(solution)/shard_map/all_to_all | solution.py:243
  52.4 0.2 collective-permute-done.3.v_ref
  52.6 1.0 collective-permute-start.4
  53.6 0.3 collective-permute-done.1.u_ref
  53.9 0.9 collective-permute-start.2
  54.8 0.0 collective-permute-start
  54.8 1.3 collective-permute-start.7
  56.0 1.0 slice.28
  57.0 0.3 collective-permute-start.5
  57.4 0.0 collective-permute-done.4.cv_ref
  57.4 2.5 %collective-permute-start.8 = (bf16[1,1024,128]{2,1,0:T(8,128)(2,1)S(1)}, bf16[1,1024,128]{2,1,0:T(8,128)(2,1)S(1)}, u32[]{:S(2)}, u32[]{:S(2)}) collective-permute-start(bf16[1,1024,128]{2,1,0:T(8,128)(2,1)S(1)} %slice.31), channel_id=1, source_target_pairs={{0,96},{32,0},{64,32},{96,64},{1,97},{33,1},{65,33},{97,65},{2,98}... | collective-permute-start | bytes 786440 | tf_op jit(solution)/shard_map/ppermute | solution.py:236
  59.9 0.0 collective-permute-done.2.cu_ref
  59.9 0.0 copy-done.2
  59.9 0.0 copy-done.3
  59.9 0.3 collective-permute-start.6
  60.2 0.1 pad_add_fusion.where_ref
  60.2 0.0 collective-permute-done.cc_ref
  60.3 10.3 %collective-permute-done.7.g_ref = bf16[1,1024,128]{2,1,0:T(8,128)(2,1)S(1)} collective-permute-done((bf16[1,1024,128]{2,1,0:T(8,128)(2,1)S(1)}, bf16[1,1024,128]{2,1,0:T(8,128)(2,1)S(1)}, u32[]{:S(2)}, u32[]{:S(2)}) %collective-permute-start.7) | collective-permute-done | bytes 262176 | tf_op jit(solution)/shard_map/ppermute | solution.py:236
  70.6 1.3 collective-permute-done.5.h_ref
  71.9 4.3 %collective-permute-done.8.cg_ref = bf16[1,1024,128]{2,1,0:T(8,128)(2,1)S(1)} collective-permute-done((bf16[1,1024,128]{2,1,0:T(8,128)(2,1)S(1)}, bf16[1,1024,128]{2,1,0:T(8,128)(2,1)S(1)}, u32[]{:S(2)}, u32[]{:S(2)}) %collective-permute-start.8) | collective-permute-done | bytes 262176 | tf_op jit(solution)/shard_map/ppermute | solution.py:236
  76.2 1.3 collective-permute-done.6.ch_ref
  77.5 0.0 copy-done.5
  77.6 0.7 copy-done.12
  78.3 19.2 %attn.3 = bf16[128,32,128]{2,1,0:T(8,128)(2,1)} custom-call(s32[2]{0:T(128)S(1)} %pad_add_fusion.where_ref, bf16[128,32,128]{2,1,0:T(8,128)(2,1)} %copy-done.3, bf16[2,1024,128]{2,1,0:T(8,128)(2,1)} %copy-done.2, bf16[2,1024,128]{2,1,0:T(8,128)(2,1)} %copy-done.8, bf16[2,1024,128]{2,1,0:T(8,128)(2,1)} %collective-permute-done.1.u_ref, ...), custom_call_target="tpu_custom_call" | custom-call | tf_op jit(solution)/shard_map/attn/pallas_call | solution.py:194
  97.5 0.0 all-to-all-done.q_ref
  97.5 0.0 copy-start.4
  97.5 31.7 %all-to-all-start.4 = ((bf16[128,32,128]{2,1,0:T(8,128)(2,1)}), bf16[128,32,128]{2,1,0:T(8,128)(2,1)S(1)}, u32[]{:S(2)}, u32[]{:S(2)}) async-start(bf16[128,32,128]{2,1,0:T(8,128)(2,1)} %attn.3), calls=%async_computation.4 | async-start | bytes 2097152 | tf_op jit(solution)/shard_map/all_to_all | solution.py:247
  129.2 19.2 %attn.2 = bf16[128,32,128]{2,1,0:T(8,128)(2,1)} custom-call(s32[2]{0:T(128)S(1)} %pad_add_fusion.where_ref, bf16[128,32,128]{2,1,0:T(8,128)(2,1)} %copy-done.4, bf16[2,1024,128]{2,1,0:T(8,128)(2,1)} %copy-done.2, bf16[2,1024,128]{2,1,0:T(8,128)(2,1)} %copy-done.8, bf16[2,1024,128]{2,1,0:T(8,128)(2,1)} %collective-permute-done.1.u_ref, ...), custom_call_target="tpu_custom_call" | custom-call | tf_op jit(solution)/shard_map/attn/pallas_call | solution.py:194
  148.5 0.2 all-to-all-done.4
  148.7 9.5 %all-to-all-start.2 = ((bf16[128,32,128]{2,1,0:T(8,128)(2,1)}), bf16[128,32,128]{2,1,0:T(8,128)(2,1)S(1)}, u32[]{:S(2)}, u32[]{:S(2)}) async-start(bf16[128,32,128]{2,1,0:T(8,128)(2,1)} %attn.2), calls=%async_computation.2 | async-start | bytes 2097152 | tf_op jit(solution)/shard_map/all_to_all | solution.py:247
  158.2 0.7 copy.6
  158.8 18.8 %all-to-all-done.2 = bf16[128,32,128]{2,1,0:T(8,128)(2,1)S(1)} async-done(((bf16[128,32,128]{2,1,0:T(8,128)(2,1)}), bf16[128,32,128]{2,1,0:T(8,128)(2,1)S(1)}, u32[]{:S(2)}, u32[]{:S(2)}) %all-to-all-start.2) | async-done | bytes 1048608 | tf_op jit(solution)/shard_map/all_to_all | solution.py:247
  177.6 0.7 copy.5
  178.3 1.7 pad.4
  180.0 1.0 constant_dynamic-update-slice_fusion
  (25 shorter events, 0.2 us)
Async XLA Ops:
  0.2 10.9 %copy-start = (f32[64,64]{1,0:T(8,128)}, f32[64,64]{1,0:T(8,128)S(1)}, u32[]{:S(2)}) copy-start(f32[64,64]{1,0:T(8,128)S(1)} %get-tuple-element.11.sin_ref) | copy-start | bytes 49156
  0.3 10.9 %copy-start.1 = (f32[64,64]{1,0:T(8,128)}, f32[64,64]{1,0:T(8,128)S(1)}, u32[]{:S(2)}) copy-start(f32[64,64]{1,0:T(8,128)S(1)} %get-tuple-element.12.cos_ref) | copy-start | bytes 49156
  2.6 17.8 %all-to-all-start.1 = ((bf16[16,2,64,128]{3,2,1,0:T(8,128)(2,1)}), bf16[16,2,64,128]{3,2,1,0:T(8,128)(2,1)S(1)}, u32[]{:S(2)}, u32[]{:S(2)}) async-start(bf16[16,2,64,128]{3,2,1,0:T(8,128)(2,1)} %pair.1), calls=%async_computation.1 | async-start | bytes 1048576 | tf_op jit(solution)/shard_map/all_to_all | solution.py:221
  20.4 28.1 %all-to-all-start.3 = ((bf16[128,32,128]{2,1,0:T(8,128)(2,1)}), bf16[128,32,128]{2,1,0:T(8,128)(2,1)S(1)}, u32[]{:S(2)}, u32[]{:S(2)}) async-start(bf16[128,32,128]{2,1,0:T(8,128)(2,1)} %bitcast.24), calls=%async_computation.3 | async-start | bytes 2097152 | tf_op jit(solution)/shard_map/all_to_all | solution.py:243
  28.9 31.0 %copy-start.2 = (bf16[2,1024,128]{2,1,0:T(8,128)(2,1)}, bf16[2,1024,128]{2,1,0:T(8,128)(2,1)S(1)}, u32[]{:S(2)}) copy-start(bf16[2,1024,128]{2,1,0:T(8,128)(2,1)S(1)} %pad_maximum_fusion.c_ref) | copy-start | bytes 1572868
  28.9 23.7 %collective-permute-start.3 = (bf16[2,1024,128]{2,1,0:T(8,128)(2,1)S(1)}, bf16[2,1024,128]{2,1,0:T(8,128)(2,1)S(1)}, u32[]{:S(2)}, u32[]{:S(2)}) collective-permute-start(bf16[2,1024,128]{2,1,0:T(8,128)(2,1)S(1)} %pad_maximum_fusion.c_ref), channel_id=1, source_target_pairs={{0,96},{32,0},{64,32},{96,64},{1,97},{33,1},{65,33},{97,65},{2,98}... | collective-permute-start | bytes 1572872 | tf_op jit(solution)/shard_map/ppermute | solution.py:230
  31.6 22.3 %collective-permute-start.1 = (bf16[2,1024,128]{2,1,0:T(8,128)(2,1)S(1)}, bf16[2,1024,128]{2,1,0:T(8,128)(2,1)}, u32[]{:S(2)}, u32[]{:S(2)}) collective-permute-start(bf16[2,1024,128]{2,1,0:T(8,128)(2,1)S(1)} %pad_maximum_fusion.c_ref), channel_id=1, source_target_pairs={{0,32},{32,64},{64,96},{96,0},{1,33},{33,65},{65,97},{97,1},{2,34}... | collective-permute-start | bytes 1572872 | tf_op jit(solution)/shard_map/ppermute | solution.py:229
  48.4 11.5 %copy-start.3 = (bf16[128,32,128]{2,1,0:T(8,128)(2,1)}, bf16[128,32,128]{2,1,0:T(8,128)(2,1)S(1)}, u32[]{:S(2)}) copy-start(bf16[128,32,128]{2,1,0:T(8,128)(2,1)S(1)} %all-to-all-done.3.q_ref) | copy-start | bytes 3145732
  48.4 49.0 %all-to-all-start = ((bf16[128,32,128]{2,1,0:T(8,128)(2,1)}), bf16[128,32,128]{2,1,0:T(8,128)(2,1)S(1)}, u32[]{:S(2)}, u32[]{:S(2)}) async-start(bf16[128,32,128]{2,1,0:T(8,128)(2,1)} %bitcast.23), calls=%async_computation | async-start | bytes 2097152 | tf_op jit(solution)/shard_map/all_to_all | solution.py:243
  52.6 24.9 %copy-start.5 = (bf16[2,1024,128]{2,1,0:T(8,128)(2,1)}, bf16[2,1024,128]{2,1,0:T(8,128)(2,1)S(1)}, u32[]{:S(2)}) copy-start(bf16[2,1024,128]{2,1,0:T(8,128)(2,1)S(1)} %collective-permute-done.3.v_ref) | copy-start | bytes 1572868
  52.6 4.8 %collective-permute-start.4 = (bf16[2,1024,128]{2,1,0:T(8,128)(2,1)S(1)}, bf16[2,1024,128]{2,1,0:T(8,128)(2,1)S(1)}, u32[]{:S(2)}, u32[]{:S(2)}) collective-permute-start(bf16[2,1024,128]{2,1,0:T(8,128)(2,1)S(1)} %collective-permute-done.3.v_ref), channel_id=1, source_target_pairs={{0,8},{8,0},{1,9},{9,1},{2,10},{10,2},{3,11},{11,3},{4,12},{12,4},... | collective-permute-start | bytes 1572872 | tf_op jit(solution)/shard_map/ppermute | solution.py:233
  53.9 6.0 %collective-permute-start.2 = (bf16[2,1024,128]{2,1,0:T(8,128)(2,1)}, bf16[2,1024,128]{2,1,0:T(8,128)(2,1)S(1)}, u32[]{:S(2)}, u32[]{:S(2)}) collective-permute-start(bf16[2,1024,128]{2,1,0:T(8,128)(2,1)} %collective-permute-done.1.u_ref), channel_id=1, source_target_pairs={{0,8},{8,0},{1,9},{9,1},{2,10},{10,2},{3,11},{11,3},{4,12},{12,4},... | collective-permute-start | bytes 1572872 | tf_op jit(solution)/shard_map/ppermute | solution.py:233
  54.8 5.5 %collective-permute-start = (bf16[2,1024,128]{2,1,0:T(8,128)(2,1)S(1)}, bf16[2,1024,128]{2,1,0:T(8,128)(2,1)S(1)}, u32[]{:S(2)}, u32[]{:S(2)}) collective-permute-start(bf16[2,1024,128]{2,1,0:T(8,128)(2,1)S(1)} %pad_maximum_fusion.c_ref), channel_id=1, source_target_pairs={{0,8},{8,0},{1,9},{9,1},{2,10},{10,2},{3,11},{11,3},{4,12},{12,4},... | collective-permute-start | bytes 1572872 | tf_op jit(solution)/shard_map/ppermute | solution.py:233
  54.8 15.8 %collective-permute-start.7 = (bf16[1,1024,128]{2,1,0:T(8,128)(2,1)S(1)}, bf16[1,1024,128]{2,1,0:T(8,128)(2,1)S(1)}, u32[]{:S(2)}, u32[]{:S(2)}) collective-permute-start(bf16[1,1024,128]{2,1,0:T(8,128)(2,1)S(1)} %slice.30), channel_id=1, source_target_pairs={{0,96},{32,0},{64,32},{96,64},{1,97},{33,1},{65,33},{97,65},{2,98}... | collective-permute-start | bytes 786440 | tf_op jit(solution)/shard_map/ppermute | solution.py:236
  57.0 14.9 %collective-permute-start.5 = (bf16[1,1024,128]{2,1,0:T(8,128)(2,1)S(1)}, bf16[1,1024,128]{2,1,0:T(8,128)(2,1)S(1)}, u32[]{:S(2)}, u32[]{:S(2)}) collective-permute-start(bf16[1,1024,128]{2,1,0:T(8,128)(2,1)S(1)} %slice.28), channel_id=1, source_target_pairs={{0,32},{32,64},{64,96},{96,0},{1,33},{33,65},{65,97},{97,1},{2,34}... | collective-permute-start | bytes 786440 | tf_op jit(solution)/shard_map/ppermute | solution.py:236
  57.4 20.2 %copy-start.6 = (bf16[2,1024,128]{2,1,0:T(8,128)(2,1)}, bf16[2,1024,128]{2,1,0:T(8,128)(2,1)S(1)}, u32[]{:S(2)}) copy-start(bf16[2,1024,128]{2,1,0:T(8,128)(2,1)S(1)} %collective-permute-done.4.cv_ref) | copy-start | bytes 1572868
  57.4 18.8 %collective-permute-start.8 = (bf16[1,1024,128]{2,1,0:T(8,128)(2,1)S(1)}, bf16[1,1024,128]{2,1,0:T(8,128)(2,1)S(1)}, u32[]{:S(2)}, u32[]{:S(2)}) collective-permute-start(bf16[1,1024,128]{2,1,0:T(8,128)(2,1)S(1)} %slice.31), channel_id=1, source_target_pairs={{0,96},{32,0},{64,32},{96,64},{1,97},{33,1},{65,33},{97,65},{2,98}... | collective-permute-start | bytes 786440 | tf_op jit(solution)/shard_map/ppermute | solution.py:236
  59.9 17.7 %copy-start.7 = (bf16[2,1024,128]{2,1,0:T(8,128)(2,1)}, bf16[2,1024,128]{2,1,0:T(8,128)(2,1)S(1)}, u32[]{:S(2)}) copy-start(bf16[2,1024,128]{2,1,0:T(8,128)(2,1)S(1)} %collective-permute-done.2.cu_ref) | copy-start | bytes 1572868
  59.9 17.6 %collective-permute-start.6 = (bf16[1,1024,128]{2,1,0:T(8,128)(2,1)S(1)}, bf16[1,1024,128]{2,1,0:T(8,128)(2,1)S(1)}, u32[]{:S(2)}, u32[]{:S(2)}) collective-permute-start(bf16[1,1024,128]{2,1,0:T(8,128)(2,1)S(1)} %slice.29), channel_id=1, source_target_pairs={{0,32},{32,64},{64,96},{96,0},{1,33},{33,65},{65,97},{97,1},{2,34}... | collective-permute-start | bytes 786440 | tf_op jit(solution)/shard_map/ppermute | solution.py:236
  60.3 17.3 %copy-start.8 = (bf16[2,1024,128]{2,1,0:T(8,128)(2,1)}, bf16[2,1024,128]{2,1,0:T(8,128)(2,1)S(1)}, u32[]{:S(2)}) copy-start(bf16[2,1024,128]{2,1,0:T(8,128)(2,1)S(1)} %collective-permute-done.cc_ref) | copy-start | bytes 1572868
  70.6 6.9 %copy-start.9 = (bf16[1,1024,128]{2,1,0:T(8,128)(2,1)}, bf16[1,1024,128]{2,1,0:T(8,128)(2,1)S(1)}, u32[]{:S(2)}) copy-start(bf16[1,1024,128]{2,1,0:T(8,128)(2,1)S(1)} %collective-permute-done.7.g_ref) | copy-start | bytes 786436
  71.9 5.7 %copy-start.10 = (bf16[1,1024,128]{2,1,0:T(8,128)(2,1)}, bf16[1,1024,128]{2,1,0:T(8,128)(2,1)S(1)}, u32[]{:S(2)}) copy-start(bf16[1,1024,128]{2,1,0:T(8,128)(2,1)S(1)} %collective-permute-done.5.h_ref) | copy-start | bytes 786436
  76.2 1.3 copy-start.11
  77.6 0.7 copy-start.12
  97.5 31.7 %copy-start.4 = (bf16[128,32,128]{2,1,0:T(8,128)(2,1)}, bf16[128,32,128]{2,1,0:T(8,128)(2,1)S(1)}, u32[]{:S(2)}) copy-start(bf16[128,32,128]{2,1,0:T(8,128)(2,1)S(1)} %all-to-all-done.q_ref) | copy-start | bytes 3145732
  97.5 51.2 %all-to-all-start.4 = ((bf16[128,32,128]{2,1,0:T(8,128)(2,1)}), bf16[128,32,128]{2,1,0:T(8,128)(2,1)S(1)}, u32[]{:S(2)}, u32[]{:S(2)}) async-start(bf16[128,32,128]{2,1,0:T(8,128)(2,1)} %attn.3), calls=%async_computation.4 | async-start | bytes 2097152 | tf_op jit(solution)/shard_map/all_to_all | solution.py:247
  148.7 29.0 %all-to-all-start.2 = ((bf16[128,32,128]{2,1,0:T(8,128)(2,1)}), bf16[128,32,128]{2,1,0:T(8,128)(2,1)S(1)}, u32[]{:S(2)}, u32[]{:S(2)}) async-start(bf16[128,32,128]{2,1,0:T(8,128)(2,1)} %attn.2), calls=%async_computation.2 | async-start | bytes 2097152 | tf_op jit(solution)/shard_map/all_to_all | solution.py:247
